TPU v7x, 256 devices: a whole 4x4x8 slice. The times are simulated.
256 devices in a mesh: nodes: 128 (over y, z, x), feat: 2 (over core).
Axes of the slice: x: 4, y: 4, z: 8, core: 2. Of those that a mesh axis runs over, the one named last changes fastest.
Arguments:
- features: bfloat16 [65536, 128], P('nodes'), may hold values from -6 to 6
- row_counts: int32 [128], P('nodes'), may hold values from 128 to 512, as said below
- send_rows: int32 [128, 128, 64], P('nodes'), may hold values from 0 to 511, as said below
- edge_src: int32 [2, 524288], P(None, 'nodes'), may hold values from 0 to 8703, as said below
- edge_dst: int32 [2, 524288], P(None, 'nodes'), may hold values from 0 to 511, as said below
- edge_keep: int32 [2, 524288], P(None, 'nodes'), may hold values 0 or 1
- w_first: bfloat16 [128, 512], P(None, 'feat'), may hold values from -0.5 to 0.5
- b_first: float32 [512], P('feat'), may hold values from -3 to 3
- w_second: bfloat16 [512, 512], P(None, 'feat'), may hold values from -0.25 to 0.25
Outputs:
- normed: bfloat16 [2, 65536, 512], P(None, 'nodes', 'feat')
- correlation: float32 [512, 512], P('nodes', 'feat')
- barlow_loss: float32 [], replicated
Inputs may be any that keep to these rules, and one draw needn't show every extreme that they name: `row_counts`: some partition has all 512 rows live. send_rows[i, j, h] is below row_counts[i]. `edge_src`: A source below 512 is below row_counts of the edge's partition. `edge_dst`: A partition's edge slots come in aligned blocks of 1024 slots; block k targets rows k * 128 to (k + 1) * 128 - 1.
All inputs are finite; a program needn't handle non-finite values. No bound on the sum of `edge_keep` on one device may be relied on, other than what follows from the above.
Results may differ from a plain program's by a relative error of at most 0.0017.
The roundings to bfloat16 on the way count: a program that leaves them out, or rounds other values in their place, can miss the bound.
Values may be sent and summed in bfloat16 or wider, within the bound.
No kernel may reach another device: no remote copies, remote signals or barrier semaphores. Data moves between devices by JAX's collectives and lax.ppermute only.
A program may use at most 64 MiB of HBM per device.

v0:
```python
import jax
import jax.numpy as jnp
from jax import lax
from jax.sharding import Mesh
from jax.sharding import PartitionSpec as P

NODES = ("nodes_0", "nodes_1", "nodes_2")
NODES_FEAT = ("nodes_0", "nodes_1", "nodes_2", "feat")


def joined_along(tiles, dim):
    shape = list(tiles.shape[1:])
    shape[dim] *= tiles.shape[0]
    return jnp.moveaxis(tiles, 0, dim).reshape(shape)


def from_everyone(shard, axis):
    devices = lax.axis_size(axis)
    return lax.all_to_all(
        jnp.broadcast_to(shard[None], (devices, *shard.shape)), axis, 0, 0, tiled=True
    )


def gathered_copies(shard, axis, dim):
    return joined_along(from_everyone(shard, axis), dim)


def over_axes(shard, axes):
    for axis in axes:
        shard = lax.psum(shard, axis)
    return shard


def own_rows(running, axes):
    for axis in axes:
        running = lax.psum_scatter(running, axis, scatter_dimension=0, tiled=True)
    return running


def per_device(
    features, row_counts, send_rows, edge_src, edge_dst, edge_keep, w_first, b_first, w_second
):
    local_rows = features.shape[0]
    partitions = lax.axis_size(NODES)
    halo_rows = send_rows.shape[2]
    edge_total = edge_src.shape[1]
    tile_rows = min(128, local_rows)
    tiles = local_rows // tile_rows
    per_tile = edge_total // tiles
    live_rows = (jnp.arange(local_rows) < row_counts[0]).astype(jnp.float32)[:, None]
    kept_edges = edge_keep.astype(jnp.float32)
    outbound = send_rows[0]
    tile_base = (jnp.arange(tiles, dtype=jnp.int32) * tile_rows)[:, None]
    row_slots = jnp.arange(tile_rows, dtype=jnp.int32)
    tables = []
    degrees = []
    for view_index in range(2):
        inside = edge_dst[view_index].reshape(tiles, per_tile) - tile_base
        table = (inside[:, :, None] == row_slots[None, None, :]).astype(jnp.float32) * kept_edges[
            view_index
        ].reshape(tiles, per_tile)[:, :, None]
        tables.append(table)
        degrees.append(jnp.sum(table, 1).reshape(local_rows))

    def mix_view(lookup, view_index):
        width = lookup.shape[1]
        picked = lookup[edge_src[view_index]].astype(jnp.float32).reshape(tiles, per_tile, width)
        summed = jnp.einsum(
            "tes,tec->tsc",
            tables[view_index],
            picked,
            precision=lax.Precision.HIGHEST,
            preferred_element_type=jnp.float32,
        )
        summed = summed.reshape(local_rows, width)
        return (lookup[:local_rows].astype(jnp.float32) + summed) / (1.0 + degrees[view_index])[
            :, None
        ]

    arrived = lax.all_to_all(features[outbound], NODES, split_axis=0, concat_axis=0, tiled=True)
    lookup = jnp.concatenate([features, arrived.reshape(partitions * halo_rows, -1)], 0)
    weights_wide = w_first.astype(jnp.float32)
    averaged = [
        jnp.dot(mix_view(lookup, view_index), weights_wide, precision=lax.Precision.HIGHEST)
        for view_index in range(2)
    ]
    hidden = jnp.stack([jax.nn.relu(branch + b_first) for branch in averaged]).astype(jnp.bfloat16)
    summed_second = jnp.einsum(
        "gnq,qm->gnm",
        gathered_copies(hidden, "feat", 2),
        w_second,
        preferred_element_type=jnp.float32,
    )
    projected = summed_second.astype(jnp.bfloat16)
    arrived_second = lax.all_to_all(
        projected[:, outbound], NODES, split_axis=1, concat_axis=1, tiled=True
    )
    embedded = jnp.stack(
        [
            mix_view(
                jnp.concatenate(
                    [
                        projected[view_index],
                        arrived_second[view_index].reshape(partitions * halo_rows, -1),
                    ],
                    0,
                ),
                view_index,
            )
            for view_index in range(2)
        ]
    )
    column_sums, squares, node_total = (
        over_axes(jnp.sum(embedded * live_rows, 1), NODES),
        over_axes(jnp.sum(jnp.square(embedded) * live_rows, 1), NODES),
        over_axes(row_counts[0].astype(jnp.float32), NODES),
    )
    average = column_sums / node_total
    variance = squares / node_total - jnp.square(average)
    normed = (
        (embedded - average[:, None, :]) / jnp.sqrt(variance + 1e-05)[:, None, :] * live_rows
    ).astype(jnp.bfloat16)
    wide_first = gathered_copies(normed[0], "feat", 1)
    row_share = wide_first.shape[1] // partitions
    contract_rows = (((0,), (0,)), ((), ()))
    owned_rows = own_rows(
        lax.dot_general(wide_first, normed[1], contract_rows, preferred_element_type=jnp.float32),
        NODES,
    )
    correlation = owned_rows / node_total
    own_columns = correlation.shape[1]
    row_labels = lax.axis_index(NODES) * row_share + jnp.arange(row_share, dtype=jnp.int32)[:, None]
    column_labels = (
        lax.axis_index("feat") * own_columns + jnp.arange(own_columns, dtype=jnp.int32)[None, :]
    )
    partial_loss = jnp.sum(
        jnp.where(
            row_labels == column_labels,
            jnp.square(1.0 - correlation),
            0.005 * jnp.square(correlation),
        )
    )
    barlow_loss = over_axes(partial_loss, NODES_FEAT)
    return (normed, correlation, barlow_loss)


def solution(mesh):
    torus = Mesh(
        mesh.devices.reshape(4, 8, 4, mesh.shape["feat"]), ("nodes_0", "nodes_1", "nodes_2", "feat")
    )
    placed = (
        P(NODES, None),
        P(NODES),
        P(NODES, None, None),
        P(None, NODES),
        P(None, NODES),
        P(None, NODES),
        P(None, "feat"),
        P("feat"),
        P(None, "feat"),
    )
    return jax.shard_map(
        per_device,
        mesh=torus,
        in_specs=placed,
        out_specs=(P(None, NODES, "feat"), P(NODES, "feat"), P()),
        check_vma=False,
    )
```

profile of v0, /device:TPU:1, one launch (start us, length us, event | category | flops | bytes accessed | tf_op | source)
XLA Modules:
  0.0 631.2 jit_solution(14449898697765373779)
XLA Ops:
  8.2 29.2 %gather_fusion = bf16[8192,128]{1,0:T(8,128)(2,1)} fusion(bf16[512,128]{1,0:T(8,128)(2,1)S(1)} %copy-done.2, s32[8192]{0:T(1024)S(1)} %broadcast_clamp_fusion), kind=kCustom, calls=%fused_computation | custom fusion | bytes 4227072 | tf_op jit(solution)/shard_map/gather | solution.py:80
  37.5 16.5 %all-to-all-start = ((bf16[128,64,128]{2,1,0:T(8,128)(2,1)}), bf16[128,64,128]{2,1,0:T(8,128)(2,1)S(1)}, u32[]{:S(2)}, u32[]{:S(2)}) async-start(bf16[128,64,128]{2,1,0:T(8,128)(2,1)} %bitcast.1), calls=%async_computation | async-start | bytes 4194304 | tf_op jit(solution)/shard_map/all_to_all | solution.py:80
  55.0 48.3 %all-to-all-done = bf16[128,64,128]{2,1,0:T(8,128)(2,1)S(1)} async-done(((bf16[128,64,128]{2,1,0:T(8,128)(2,1)}), bf16[128,64,128]{2,1,0:T(8,128)(2,1)S(1)}, u32[]{:S(2)}, u32[]{:S(2)}) %all-to-all-start) | async-done | bytes 2097184 | tf_op jit(solution)/shard_map/all_to_all | solution.py:80
  103.3 1.3 copy-done.3
  104.6 1.8 pad_maximum_fusion.2
  106.5 14.9 %gather_fusion.1 = bf16[4096,128]{1,0:T(8,128)(2,1)} fusion(bf16[8704,128]{1,0:T(8,128)(2,1)S(1)} %pad_maximum_fusion.2, s32[4096]{0:T(1024)S(1)} %broadcast_clamp_fusion.2), kind=kCustom, calls=%fused_computation.1 | custom fusion | bytes 2113536 | tf_op jit(solution)/shard_map/gather | solution.py:67
  121.3 2.5 fusion.6
  123.8 14.9 %gather_fusion.2 = bf16[4096,128]{1,0:T(8,128)(2,1)} fusion(bf16[8704,128]{1,0:T(8,128)(2,1)S(1)} %pad_maximum_fusion.2, s32[4096]{0:T(1024)S(1)} %broadcast_clamp_fusion.1), kind=kCustom, calls=%fused_computation.2 | custom fusion | bytes 2113536 | tf_op jit(solution)/shard_map/gather | solution.py:67
  138.8 2.5 fusion.2
  142.3 8.2 %all_to_all.20 = bf16[2,2,512,256]{3,2,1,0:T(8,128)(2,1)S(1)} all-to-all(bf16[2,2,512,256]{3,2,1,0:T(8,128)(2,1)S(1)} %broadcast_in_dim.6), channel_id=1, replica_groups=mesh['nodes_0'=4,'nodes_1'=8,'nodes_2'=4,'feat'=2] {'feat'}, dimensions={0} | all-to-all | bytes 2097152 | tf_op jit(solution)/shard_map/all_to_all | solution.py:19
  151.6 63.9 %gather_fusion.3 = bf16[8192,2,256]{2,1,0:T(2,128)(2,1)} fusion(bf16[2,512,256]{2,0,1:T(2,128)(2,1)S(1)} %copy.21, s32[8192]{0:T(1024)S(1)} %broadcast_clamp_fusion), kind=kCustom, calls=%fused_computation.3 | custom fusion | bytes 16809984 | tf_op jit(solution)/shard_map/gather | solution.py:96
  215.5 8.6 %copy.30 = bf16[128,64,2,256]{3,1,2,0:T(8,128)(2,1)} copy(bf16[128,64,2,256]{3,2,1,0:T(2,128)(2,1)} %bitcast.76) | data formatting | bytes 16777216 | tf_op jit(solution)/shard_map/gather | solution.py:96
  224.0 7.7 %all-to-all-start.2 = ((bf16[2,128,64,256]{3,2,0,1:T(8,128)(2,1)}), bf16[2,128,64,256]{3,2,0,1:T(8,128)(2,1)}, u32[]{:S(2)}, u32[]{:S(2)}) async-start(bf16[2,128,64,256]{3,2,0,1:T(8,128)(2,1)} %bitcast.75), calls=%async_computation.2 | async-start | bytes 16777216 | tf_op jit(solution)/shard_map/all_to_all | solution.py:95
  232.5 180.1 %all-to-all-done.2 = bf16[2,128,64,256]{3,2,0,1:T(8,128)(2,1)} async-done(((bf16[2,128,64,256]{3,2,0,1:T(8,128)(2,1)}), bf16[2,128,64,256]{3,2,0,1:T(8,128)(2,1)}, u32[]{:S(2)}, u32[]{:S(2)}) %all-to-all-start.2) | async-done | bytes 8388640 | tf_op jit(solution)/shard_map/all_to_all | solution.py:95
  412.5 5.3 fusion.41
  417.8 2.8 pad_maximum_fusion.1
  420.7 15.8 %gather_fusion.5 = bf16[4096,256]{1,0:T(8,128)(2,1)S(1)} fusion(bf16[8704,256]{1,0:T(8,128)(2,1)} %pad_maximum_fusion.1, s32[4096]{0:T(1024)S(1)} %broadcast_clamp_fusion.1), kind=kCustom, calls=%fused_computation.5 | custom fusion | bytes 4210688 | tf_op jit(solution)/shard_map/gather | solution.py:67
  436.5 2.1 fusion
  438.6 4.0 pad_maximum_fusion
  442.6 15.8 %gather_fusion.4 = bf16[4096,256]{1,0:T(8,128)(2,1)S(1)} fusion(bf16[8704,256]{1,0:T(8,128)(2,1)} %pad_maximum_fusion, s32[4096]{0:T(1024)S(1)} %broadcast_clamp_fusion.2), kind=kCustom, calls=%fused_computation.4 | custom fusion | bytes 4210688 | tf_op jit(solution)/shard_map/gather | solution.py:67
  460.2 8.4 %all-reduce.3 = (f32[2,256]{1,0:T(2,128)S(1)}, f32[]{:T(128)}, f32[2,256]{1,0:T(2,128)S(1)}) all-reduce(f32[2,256]{1,0:T(2,128)S(1)} %get-tuple-element.4, f32[]{:T(128)S(6)} %convert_element_type.49, f32[2,256]{1,0:T(2,128)S(1)} %get-tuple-element.3), channel_id=1, replica_groups=mesh['nodes_0'=4,'nodes_1'=8,'nodes_2'=4,'feat'=2] {'nodes_0'}, use_global_device_ids=true, to_apply=%region_3.4 | all-reduce | flops 1025 | bytes 8200 | tf_op jit(solution)/shard_map/psum | solution.py:30
  468.7 16.0 %all-reduce.1 = (f32[2,256]{1,0:T(2,128)S(1)}, f32[]{:T(128)}, f32[2,256]{1,0:T(2,128)S(1)}) all-reduce(f32[2,256]{1,0:T(2,128)S(1)} %get-tuple-element.15, f32[]{:T(128)} %get-tuple-element.16, f32[2,256]{1,0:T(2,128)S(1)} %get-tuple-element.17), channel_id=1, replica_groups=mesh['nodes_0'=4,'nodes_1'=8,'nodes_2'=4,'feat'=2] {'nodes_1'}, use_global_device_ids=true, to_apply=%region_4.5 | all-reduce | flops 1025 | bytes 8200 | tf_op jit(solution)/shard_map/psum | solution.py:30
  484.7 9.2 %all-reduce.2 = (f32[2,256]{1,0:T(2,128)S(1)}, f32[]{:T(128)}, f32[2,256]{1,0:T(2,128)S(1)}) all-reduce(f32[2,256]{1,0:T(2,128)S(1)} %get-tuple-element.9, f32[]{:T(128)} %get-tuple-element.10, f32[2,256]{1,0:T(2,128)S(1)} %get-tuple-element.11), channel_id=1, replica_groups=mesh['nodes_0'=4,'nodes_1'=8,'nodes_2'=4,'feat'=2] {'nodes_2'}, use_global_device_ids=true, to_apply=%region_5.6 | all-reduce | flops 1025 | bytes 8200 | tf_op jit(solution)/shard_map/psum | solution.py:30
  494.9 12.1 %all_to_all.21 = bf16[2,512,256]{1,2,0:T(8,128)(2,1)S(1)} all-to-all(bf16[2,512,256]{1,2,0:T(8,128)(2,1)S(1)} %broadcast_in_dim.8), channel_id=1, replica_groups=mesh['nodes_0'=4,'nodes_1'=8,'nodes_2'=4,'feat'=2] {'feat'}, dimensions={0} | all-to-all | bytes 1048576 | tf_op jit(solution)/shard_map/all_to_all | solution.py:19
  508.2 16.2 %reduce-scatter.3.cloned.1.call-done = f32[128,256]{1,0:T(8,128)} async-done(((f32[512,256]{1,0:T(8,128)}), f32[128,256]{1,0:T(8,128)}) %reduce-scatter.3.cloned.1.call-update) | async-done | bytes 131088 | tf_op jit(solution)/shard_map/reduce_scatter | solution.py:36
  525.7 34.7 %reduce-scatter.5.cloned.1.call-done = f32[16,256]{1,0:T(8,128)} async-done(((f32[128,256]{1,0:T(8,128)}), f32[16,256]{1,0:T(8,128)}) %reduce-scatter.5.cloned.1.call-update) | async-done | bytes 16400 | tf_op jit(solution)/shard_map/reduce_scatter | solution.py:36
  560.5 13.7 %all-reduce = f32[16,256]{1,0:T(8,128)S(1)} all-reduce(f32[16,256]{1,0:T(8,128)} %reduce-scatter.5.cloned.1.call-done), channel_id=4, replica_groups=mesh['nodes_0'=4,'nodes_1'=8,'nodes_2'=4,'feat'=2] {'nodes_2'}, use_global_device_ids=true, to_apply=%region_15.16.clone | all-reduce | flops 4096 | bytes 32768
  574.1 1.9 select_reduce_fusion.2
  576.1 9.1 %psum.100 = f32[]{:T(128)} all-reduce(f32[]{:T(128)} %get-tuple-element.18), channel_id=1, replica_groups=mesh['nodes_0'=4,'nodes_1'=8,'nodes_2'=4,'feat'=2] {'nodes_0'}, use_global_device_ids=true, to_apply=%region_17.18 | all-reduce | flops 1 | bytes 8 | tf_op jit(solution)/shard_map/psum | solution.py:30
  585.1 12.6 %psum.101 = f32[]{:T(128)} all-reduce(f32[]{:T(128)} %psum.100), channel_id=1, replica_groups=mesh['nodes_0'=4,'nodes_1'=8,'nodes_2'=4,'feat'=2] {'nodes_1'}, use_global_device_ids=true, to_apply=%region_18.19 | all-reduce | flops 1 | bytes 8 | tf_op jit(solution)/shard_map/psum | solution.py:30
  597.7 6.6 %psum.102 = f32[]{:T(128)} all-reduce(f32[]{:T(128)} %psum.101), channel_id=1, replica_groups=mesh['nodes_0'=4,'nodes_1'=8,'nodes_2'=4,'feat'=2] {'nodes_2'}, use_global_device_ids=true, to_apply=%region_19.20 | all-reduce | flops 1 | bytes 8 | tf_op jit(solution)/shard_map/psum | solution.py:30
  604.3 20.0 %psum.103 = f32[]{:T(128)} all-reduce(f32[]{:T(128)} %psum.102), channel_id=1, replica_groups=mesh['nodes_0'=4,'nodes_1'=8,'nodes_2'=4,'feat'=2] {'feat'}, use_global_device_ids=true, to_apply=%region_20.21 | all-reduce | flops 1 | bytes 8 | tf_op jit(solution)/shard_map/psum | solution.py:30
  (67 shorter events, 8.6 us)
Async XLA Ops:
  7.2 143.4 %copy-start = (bf16[512,256]{1,0:T(8,128)(2,1)S(1)}, bf16[512,256]{1,0:T(8,128)(2,1)}, u32[]{:S(2)}) copy-start(bf16[512,256]{1,0:T(8,128)(2,1)} %param.17) | copy-start | bytes 786436
  7.2 1.0 copy-start.2
  37.5 16.5 %copy-start.6 = (s32[2,4096]{1,0:T(2,128)S(1)}, s32[2,4096]{1,0:T(2,128)}, u32[]{:S(2)}) copy-start(s32[2,4096]{1,0:T(2,128)} %param.13) | copy-start | bytes 98308
  37.5 16.6 %copy-start.7 = (s32[2,4096]{1,0:T(2,128)S(1)}, s32[2,4096]{1,0:T(2,128)}, u32[]{:S(2)}) copy-start(s32[2,4096]{1,0:T(2,128)} %param.14) | copy-start | bytes 98308
  37.5 17.4 %copy-start.8 = (s32[2,4096]{1,0:T(2,128)S(1)}, s32[2,4096]{1,0:T(2,128)}, u32[]{:S(2)}) copy-start(s32[2,4096]{1,0:T(2,128)} %param.12) | copy-start | bytes 98308
  37.5 65.8 %all-to-all-start = ((bf16[128,64,128]{2,1,0:T(8,128)(2,1)}), bf16[128,64,128]{2,1,0:T(8,128)(2,1)S(1)}, u32[]{:S(2)}, u32[]{:S(2)}) async-start(bf16[128,64,128]{2,1,0:T(8,128)(2,1)} %bitcast.1), calls=%async_computation | async-start | bytes 4194304 | tf_op jit(solution)/shard_map/all_to_all | solution.py:80
  103.3 1.4 copy-start.3
  138.7 2.5 copy-start.9
  138.7 2.5 copy-start.10
  224.0 188.5 %all-to-all-start.2 = ((bf16[2,128,64,256]{3,2,0,1:T(8,128)(2,1)}), bf16[2,128,64,256]{3,2,0,1:T(8,128)(2,1)}, u32[]{:S(2)}, u32[]{:S(2)}) async-start(bf16[2,128,64,256]{3,2,0,1:T(8,128)(2,1)} %bitcast.75), calls=%async_computation.2 | async-start | bytes 16777216 | tf_op jit(solution)/shard_map/all_to_all | solution.py:95
  231.7 292.7 %reduce-scatter.3.cloned.1.call-start = ((), (), s32[]{:S(2)}) async-start(), calls=%async_computation.6 | async-start | bytes 655360 | tf_op jit(solution)/shard_map/reduce_scatter | solution.py:36
  458.5 1.3 copy-start.5
  494.7 13.4 %copy-start.4 = (bf16[2,512,256]{2,1,0:T(8,128)(2,1)}, bf16[2,512,256]{2,1,0:T(8,128)(2,1)S(1)}, u32[]{:S(2)}) copy-start(bf16[2,512,256]{2,1,0:T(8,128)(2,1)S(1)} %multiply_convert_fusion) | copy-start | bytes 1572868
  494.7 29.8 %copy-start.11 = (u32[256]{0:T(256)S(1)}, u32[256]{0:T(256)}, u32[]{:S(2)}) copy-start(u32[256]{0:T(256)} %constant.49) | copy-start | bytes 3076
  494.7 129.6 %copy-start.1 = (bf16[512,256]{1,0:T(8,128)(2,1)S(1)}, bf16[512,256]{1,0:T(8,128)(2,1)}, u32[]{:S(2)}) copy-start(bf16[512,256]{1,0:T(8,128)(2,1)} %param.17) | copy-start | bytes 786436
  508.1 52.3 %reduce-scatter.5.cloned.1.call-start = ((), (), s32[]{:S(2)}) async-start(), calls=%async_computation.7 | async-start | bytes 147456 | tf_op jit(solution)/shard_map/reduce_scatter | solution.py:36
Sparse Core Ops, SparseCore 0:
  508.3 16.1 reduce-scatter.2
  526.9 33.4 reduce-scatter.4
where the time goes:
time: 632 us; the launch traced here: 631 us
  waiting for transfers between devices  279 us (44%)
  local copies, waits for them, and re-layouts  172 us (27%)
  blocking collectives  116 us (18%)
  starting transfers between devices  24.2 us (4%)
  between operations  15.8 us (2%)
  other arithmetic  13.5 us (2%)
  matrix products  10.7 us (2%)
    all_to_all x1, waiting for transfers between devices, per_device(): lax.all_to_all(projected[:, outbound], NODES, split_axis=1, concat_axis=1...  180 us
    psum x7, blocking collectives, over_axes(): shard = lax.psum(shard, axis)  81.9 us
    gather x2, local copies, waits for them, and re-layouts, per_device(): projected[:, outbound]  72.5 us
    gather x4, local copies, waits for them, and re-layouts, mix_view(): lookup[edge_src[view_index]].astype(jnp.float32)  61.4 us
    reduce_scatter x2, waiting for transfers between devices, own_rows(): running = lax.psum_scatter(running, axis, scatter_dimension=0, tiled=True)  51 us
    all_to_all x1, waiting for transfers between devices, per_device(): lax.all_to_all(features[outbound], NODES, split_axis=0, concat_axis=0, ti...  48.3 us
    gather x1, local copies, waits for them, and re-layouts, per_device(): features[outbound]  29.2 us
    all_to_all x2, blocking collectives, from_everyone(): lax.all_to_all(jnp.broadcast_to(shard[None], (devices, *shard.shape)), ax...  20.3 us
  transfers between devices with their start and end apart: 4, of which 4 were waited for; matrix products, arithmetic and copies ran while one was open for 0% of the time, Pallas kernels for 0%

commit v1 on v0

v1 whole, which is shorter than its diff:
```python
import functools

import jax
import jax.numpy as jnp
from jax import lax
from jax.experimental import pallas as pl
from jax.experimental.pallas import tpu as pltpu
from jax.sharding import Mesh
from jax.sharding import PartitionSpec as P

NODES = ("nodes_0", "nodes_1", "nodes_2")
NODES_FEAT = ("nodes_0", "nodes_1", "nodes_2", "feat")

LANES = 128
TILE = 128
CODE_BITS = 19
CODE_TOP = 2 ** (CODE_BITS - 1)
SCALE_BIAS = 224.0

VMEM = pl.BlockSpec(memory_space=pltpu.VMEM)
SMEM = pl.BlockSpec(memory_space=pltpu.SMEM)


def call(body, outs, scratch, *operands, scalars=(), name):
    return pl.pallas_call(
        body,
        out_shape=outs,
        in_specs=[SMEM] * len(scalars) + [VMEM] * len(operands),
        out_specs=jax.tree.map(lambda _: VMEM, outs),
        scratch_shapes=scratch,
        compiler_params=pltpu.CompilerParams(vmem_limit_bytes=56 * 2**20),
        name=name,
    )(*scalars, *operands)


def pick_rows(index, first_index, table, rows, first_row, count, unroll):
    def step(block, _):
        base = pl.multiple_of(block * unroll, unroll)
        for lane in range(unroll):
            source = index[first_index + base + lane]
            rows[pl.ds(first_row + base + lane, 1), :] = table[pl.ds(source, 1), :]
        return 0

    lax.fori_loop(0, count // unroll, step, 0)


def in_chunks(total, size, body):
    def step(block, _):
        body(pl.multiple_of(block * size, size))
        return 0

    lax.fori_loop(0, total // size, step, 0)


def several(total, unroll, body):
    def step(block, _):
        for one in range(unroll):
            body(block * unroll + one)
        return 0

    lax.fori_loop(0, total // unroll, step, 0)


def edge_table(targets, tile):
    inside = targets[tile : tile + 1, :] - tile * TILE
    row = lax.broadcasted_iota(jnp.int32, (TILE, targets.shape[1]), 0)
    table = jnp.where(inside == row, 1.0, 0.0)
    return table.astype(jnp.bfloat16), jnp.sum(table, 1, keepdims=True)


def send_features(core, outbound, features, out, table, rows):
    table[...] = features[...].astype(jnp.float32)
    half = out.shape[0] // LANES
    first = core[0] * half

    def step(block, _):
        base = pl.multiple_of(block * 4 * half, 4 * half)
        for peer in range(4):
            for slot in range(half):
                source = outbound[(block * 4 + peer) * (2 * half) + first + slot]
                rows[pl.ds(base + peer * half + slot, 1), :] = table[pl.ds(source, 1), :]
        return 0

    lax.fori_loop(0, out.shape[0] // (4 * half), step, 0)

    def narrow(base):
        out[pl.ds(base, 256), :] = rows[pl.ds(base, 256), :].astype(jnp.bfloat16)

    in_chunks(out.shape[0], 256, narrow)


def first_mix(
    live_count,
    sources,
    outbound,
    features,
    own,
    other,
    targets,
    mixed,
    words,
    table,
    picked,
    codes,
    coded,
):
    local = features.shape[0]
    halo = own.shape[0]
    table[0:local, :] = features[...].astype(jnp.float32)

    def widen(base):
        table[pl.ds(local + base, 256), :] = own[pl.ds(base, 256), :].astype(jnp.float32)
        table[pl.ds(local + halo + base, 256), :] = other[pl.ds(base, 256), :].astype(jnp.float32)

    in_chunks(halo, 256, widen)
    edges = targets.shape[1]
    pick_rows(sources, 0, table, picked, 0, edges * (local // TILE), 128)
    for tile in range(local // TILE):
        onehot, degree = edge_table(targets, tile)
        summed = jnp.dot(
            onehot,
            picked[tile * edges : (tile + 1) * edges, :].astype(jnp.bfloat16),
            preferred_element_type=jnp.float32,
        )
        rows = slice(tile * TILE, (tile + 1) * TILE)
        mix = (table[rows, :] + summed) / (1.0 + degree)
        mixed[rows, :] = mix
        top = jnp.maximum(jnp.max(jnp.abs(mix), 1, keepdims=True), 1e-30)
        step = jnp.clip(jnp.floor(8.0 * jnp.log2(top)) + (2.0 + SCALE_BIAS), 0.0, 255.0)
        code = jnp.round(mix * (jnp.exp2((SCALE_BIAS - step) * 0.125) * CODE_TOP))
        code = jnp.clip(code, -CODE_TOP, CODE_TOP - 1).astype(jnp.int32)
        codes[rows, :] = (code & (2**CODE_BITS - 1)) | (step.astype(jnp.int32) << CODE_BITS)

    pick_rows(outbound, 0, codes, coded, 0, coded.shape[0], 128)
    group = lax.broadcasted_iota(jnp.int32, (8, LANES), 1) // 16

    patch = lax.broadcasted_iota(jnp.int32, (8, LANES), 0)
    count = jnp.where(patch == 0, live_count[0] & 255, live_count[0] >> 8) << 24
    patched = (lax.broadcasted_iota(jnp.int32, (8, LANES), 1) == 1) & (patch < 2)

    def pack(peer):
        base = pl.multiple_of(peer * 64, 64)
        to = pl.multiple_of(peer * 40, 8)
        octet = [coded[pl.ds(base + 8 * k, 8), :] for k in range(8)]
        for k in range(4):
            low = (octet[k] >> 3) & 0xFFFF
            words[pl.ds(to + 8 * k, 8), :] = low | ((octet[k + 4] >> 3) << 16)
        rest = jnp.zeros((8, LANES), jnp.int32)
        steps = jnp.zeros((8, LANES), jnp.int32)
        for k in range(8):
            rest = rest | ((octet[k] & 7) << (3 * k))
            steps = jnp.where(group == k, octet[k], steps)
        rest = rest | jnp.where(patched, count, (steps >> CODE_BITS) << 24)
        words[pl.ds(to + 32, 8), :] = rest

    several(coded.shape[0] // 64, 8, pack)


def split_three(value):
    first = value.astype(jnp.bfloat16)
    rest = value - first.astype(jnp.float32)
    second = rest.astype(jnp.bfloat16)
    third = (rest - second.astype(jnp.float32)).astype(jnp.bfloat16)
    return first, second, third


def second_mix(
    core,
    live_count,
    sources,
    words,
    mixed,
    targets,
    w1_own,
    w1_other,
    b_own,
    b_other,
    w2_own,
    w2_other,
    embedded,
    sums,
    node_total,
    table,
    picked,
    w1,
    w2,
):
    local = mixed.shape[0]
    half = w1_own.shape[1]
    me = core[0]
    mine = pl.multiple_of(me * half, half)
    theirs = pl.multiple_of((1 - me) * half, half)
    for piece in range(3):
        w1[piece * LANES : (piece + 1) * LANES, 0:half] = w1_own[...]
        w1[piece * LANES : (piece + 1) * LANES, half : 2 * half] = w1_other[...]
    w2[0:half, 0:half] = w2_own[pl.ds(mine, half), :]
    w2[half : 2 * half, 0:half] = w2_own[pl.ds(theirs, half), :]
    w2[0:half, half : 2 * half] = w2_other[pl.ds(mine, half), :]
    w2[half : 2 * half, half : 2 * half] = w2_other[pl.ds(theirs, half), :]
    bias = jnp.concatenate([b_own[...], b_other[...]], 1)

    table[0:local, :] = mixed[...]

    def unpack(peer):
        base = pl.multiple_of(peer * 40, 8)
        to = pl.multiple_of(local + peer * 64, 64)
        pairs = [words[pl.ds(base + 8 * k, 8), :] for k in range(4)]
        rest = words[pl.ds(base + 32, 8), :]
        step = (rest >> 24) & 255
        scale = jnp.exp2((step.astype(jnp.float32) - SCALE_BIAS) * 0.125) * (1.0 / CODE_TOP)
        for k in range(8):
            high = (pairs[k] << 16) >> 16 if k < 4 else pairs[k - 4] >> 16
            code = (high << 3) | ((rest >> (3 * k)) & 7)
            table[pl.ds(to + 8 * k, 8), :] = (
                code.astype(jnp.float32) * scale[:, 16 * k : 16 * k + 1]
            )
        return step

    def unpack_several(block, counts):
        for one in range(8):
            counts = counts + unpack(block * 8 + one)
        return counts

    counts = lax.fori_loop(
        0, words.shape[0] // 320, unpack_several, jnp.zeros((8, LANES), jnp.int32)
    )
    sublane = lax.broadcasted_iota(jnp.int32, (8, LANES), 0)
    weight = jnp.where(sublane == 0, 1.0, jnp.where(sublane == 1, 256.0, 0.0))
    lane = lax.broadcasted_iota(jnp.int32, (8, LANES), 1)
    counts = jnp.where(lane == 1, counts.astype(jnp.float32) * weight, 0.0)
    counts = jnp.sum(jnp.sum(counts, 1, keepdims=True), 0, keepdims=True)
    node_total[...] = jnp.broadcast_to(counts, node_total.shape)
    edges = targets.shape[1]
    total = jnp.zeros((1, 2 * half), jnp.float32)
    squares = jnp.zeros((1, 2 * half), jnp.float32)
    for tile in range(local // TILE):
        rows = slice(tile * TILE, (tile + 1) * TILE)
        picked[0:TILE, :] = mixed[rows, :]
        pick_rows(sources, tile * edges, table, picked, TILE, edges, 128)
        value = jnp.concatenate(split_three(picked[...]), 1)
        hidden = jnp.dot(value, w1[...], preferred_element_type=jnp.float32) + bias
        hidden = jnp.maximum(hidden, 0.0).astype(jnp.bfloat16)
        projected = jnp.dot(hidden, w2[...], preferred_element_type=jnp.float32)
        projected = projected.astype(jnp.bfloat16)
        onehot, degree = edge_table(targets, tile)
        summed = jnp.dot(onehot, projected[TILE:, :], preferred_element_type=jnp.float32)
        value = (projected[0:TILE, :].astype(jnp.float32) + summed) / (1.0 + degree)
        embedded[rows, :] = value
        slot = tile * TILE + lax.broadcasted_iota(jnp.int32, (TILE, 1), 0)
        value = jnp.where(slot < live_count[0], value, 0.0)
        total = total + jnp.sum(value, 0, keepdims=True)
        squares = squares + jnp.sum(value * value, 0, keepdims=True)
    for part in range(4):
        columns = slice(part * LANES, (part + 1) * LANES)
        sums[:, part : part + 1, :] = jnp.broadcast_to(
            total[:, columns][None], (sums.shape[0], 1, LANES)
        )
        sums[:, part + 4 : part + 5, :] = jnp.broadcast_to(
            squares[:, columns][None], (sums.shape[0], 1, LANES)
        )


def normalize(live_count, sums, node_total, embedded, out):
    total = node_total[...]
    scaled = jnp.sum(sums[...], 0) / total
    mean, square = scaled[0:4, :], scaled[4:8, :]
    dev = jnp.sqrt(square - mean * mean + 1e-05)
    slot = lax.broadcasted_iota(jnp.int32, (embedded.shape[0], 1), 0)
    live = slot < live_count[0]
    for part in range(4):
        columns = slice(part * LANES, (part + 1) * LANES)
        value = (embedded[:, columns] - mean[part : part + 1, :]) / dev[part : part + 1, :]
        out[:, columns] = jnp.where(live, value, 0.0).astype(jnp.bfloat16)


def correlate(core, own, other, normed, out):
    half = normed.shape[2]
    width = 2 * half
    contract = (((0,), (0,)), ((), ()))

    def give(left, right):
        product = lax.dot_general(left, right, contract, preferred_element_type=jnp.float32)
        for pair in range(width // 8):
            near = product[pair * 8 : pair * 8 + 8, 0:LANES]
            far = product[pair * 8 : pair * 8 + 8, LANES:half]
            out[2 * pair] = jnp.concatenate([near[0:4], far[0:4]], 0)
            out[2 * pair + 1] = jnp.concatenate([near[4:8], far[4:8]], 0)

    @pl.when(core[0] == 0)
    def _():
        normed[0] = own[:, 0:half]
        normed[1] = other[:, half:width]
        give(own[...], other[:, half:width])

    @pl.when(core[0] == 1)
    def _():
        normed[0] = other[:, half:width]
        normed[1] = own[:, 0:half]
        give(other[...], own[:, 0:half])


def finish(core, node, arrived, node_total, correlation, loss):
    half = correlation.shape[1]
    summed = jnp.sum(arrived[...], 0) / node_total[...]
    value = jnp.concatenate([summed[0:4, :], summed[4:8, :]], 1)
    correlation[...] = value
    share = correlation.shape[0]
    row = lax.broadcasted_iota(jnp.int32, (share, half), 0) + node[0] * share
    column = lax.broadcasted_iota(jnp.int32, (share, half), 1) + core[0] * half
    terms = jnp.where(row == column, jnp.square(1.0 - value), 0.005 * jnp.square(value))
    terms = jnp.sum(jnp.sum(terms, 1, keepdims=True), 0, keepdims=True)
    loss[...] = jnp.broadcast_to(terms[None], loss.shape)


def per_device(
    features, row_counts, send_rows, edge_src, edge_dst, edge_keep, w_first, b_first, w_second
):
    local, f_in = features.shape
    peers, halo = send_rows.shape[1], send_rows.shape[2]
    edges = edge_src.shape[1]
    tiles = local // TILE
    half = w_first.shape[1]
    width = 2 * half
    f32, bf16, i32 = jnp.float32, jnp.bfloat16, jnp.int32
    shape = jax.ShapeDtypeStruct
    core_index = lax.axis_index("feat")
    node_index = lax.axis_index(NODES)
    core = core_index.reshape(1).astype(i32)
    node = node_index.reshape(1).astype(i32)
    swap = [(0, 1), (1, 0)]

    def partner(value):
        return lax.ppermute(value, "feat", swap)

    w1_other, w2_other = partner(w_first), partner(w_second)
    bias = b_first.reshape(1, half)
    bias_other = partner(bias)
    outbound = send_rows.reshape(peers * halo)
    sources = lax.dynamic_index_in_dim(edge_src, core_index, 0, False)
    targets = lax.dynamic_index_in_dim(edge_dst, core_index, 0, False)
    kept = lax.dynamic_index_in_dim(edge_keep, core_index, 0, False)
    targets = jnp.where(kept == 1, targets, -1).reshape(tiles, edges // tiles)

    rows_half = peers * halo // 2
    sent = call(
        send_features,
        shape((rows_half, f_in), bf16),
        [pltpu.VMEM((local, f_in), f32), pltpu.VMEM((rows_half, f_in), f32)],
        features,
        scalars=(core, outbound),
        name="send_features",
    )
    got = lax.all_to_all(
        sent.reshape(peers, halo // 2, f_in), NODES, split_axis=0, concat_axis=0, tiled=True
    )
    got_other = partner(got)
    remote = sources - local
    slot_half = (remote % halo) // (halo // 2)
    from_other = (slot_half != core_index).astype(i32)
    remote = (remote // halo) * (halo // 2) + remote % (halo // 2) + from_other * rows_half
    first_sources = jnp.where(sources < local, sources, remote + local)
    mixed, words = call(
        first_mix,
        (shape((local, f_in), f32), shape((peers * 40, f_in), i32)),
        [
            pltpu.VMEM((local + 2 * rows_half, f_in), f32),
            pltpu.VMEM((edges, f_in), f32),
            pltpu.VMEM((local, f_in), i32),
            pltpu.VMEM((peers * halo, f_in), i32),
        ],
        features,
        got.reshape(rows_half, f_in),
        got_other.reshape(rows_half, f_in),
        targets,
        scalars=(row_counts, first_sources, outbound),
        name="first_mix",
    )
    arrived = lax.all_to_all(
        words.reshape(peers, 40, f_in), NODES, split_axis=0, concat_axis=0, tiled=True
    )
    embedded, sums, node_total = call(
        second_mix,
        (
            shape((local, width), f32),
            shape((peers, 8, LANES), f32),
            shape((8, LANES), f32),
        ),
        [
            pltpu.VMEM((local + peers * halo, f_in), f32),
            pltpu.VMEM((TILE + edges // tiles, f_in), f32),
            pltpu.VMEM((3 * f_in, width), bf16),
            pltpu.VMEM((width, width), bf16),
        ],
        arrived.reshape(peers * 40, f_in),
        mixed,
        targets,
        w_first,
        w1_other,
        bias,
        bias_other,
        w_second,
        w2_other,
        scalars=(core, row_counts, sources),
        name="second_mix",
    )
    sums = lax.all_to_all(sums, NODES, split_axis=0, concat_axis=0, tiled=True)
    own = call(
        normalize,
        shape((local, width), bf16),
        [],
        sums,
        node_total,
        embedded,
        scalars=(row_counts,),
        name="normalize",
    )
    normed, partial = call(
        correlate,
        (shape((2, local, half), bf16), shape((peers, 8, LANES), f32)),
        [],
        own,
        partner(own),
        scalars=(core,),
        name="correlate",
    )
    partial = lax.all_to_all(partial, NODES, split_axis=0, concat_axis=0, tiled=True)
    devices = lax.axis_size(NODES_FEAT)
    correlation, loss = call(
        finish,
        (shape((width // peers, half), f32), shape((devices, 1, LANES), f32)),
        [],
        partial,
        node_total,
        scalars=(core, node),
        name="finish",
    )
    losses = lax.all_to_all(loss, NODES_FEAT, 0, 0, tiled=True)
    return (normed, correlation, jnp.sum(losses[:, 0, 0]))


def solution(mesh):
    torus = Mesh(
        mesh.devices.reshape(4, 8, 4, mesh.shape["feat"]), ("nodes_0", "nodes_1", "nodes_2", "feat")
    )
    placed = (
        P(NODES, None),
        P(NODES),
        P(NODES, None, None),
        P(None, NODES),
        P(None, NODES),
        P(None, NODES),
        P(None, "feat"),
        P("feat"),
        P(None, "feat"),
    )
    return jax.shard_map(
        per_device,
        mesh=torus,
        in_specs=placed,
        out_specs=(P(None, NODES, "feat"), P(NODES, "feat"), P()),
        check_vma=False,
    )
```

time: 632 us -> 247 us (0.39)
  waiting for transfers between devices: 279 us -> 78.3 us
  local copies, waits for them, and re-layouts: 172 us -> 6.27 us
  Pallas kernels: 0 us -> 44.3 us
  blocking collectives: 116 us -> 92.6 us
  between operations: 15.8 us -> 1.42 us
  other arithmetic: 13.5 us -> 1.58 us
  matrix products: 10.7 us -> 0 us
    gather x7 -> x0, local copies, waits for them, and re-layouts: 163 us -> none  [the longest x2 72.5 us: per_device(): projected[:, outbound]]
    all_to_all x2, waiting for transfers between devices: 228 us -> 75.3 us  [the longest x1 58.2 us: per_device(): lax.all_to_all(words.reshape(peers, 40, f_in), NODES, split_axis=0, conca...]
    psum x7 -> x0, blocking collectives: 81.9 us -> none  [over_axes(): shard = lax.psum(shard, axis)]
    all_to_all x2 -> x3, blocking collectives: 20.3 us -> 92.6 us  [the longest x1 43.6 us: per_device(): lax.all_to_all(sent.reshape(peers, halo // 2, f_in), NODES, split_axis=0,...]
    reduce_scatter x2 -> x0, waiting for transfers between devices: 51 us -> none  [own_rows(): running = lax.psum_scatter(running, axis, scatter_dimension=0, tiled=True)]
    pallas_call x0 -> x6, Pallas kernels: none -> 44.3 us  [call(): pl.pallas_call(body, out_shape=outs, in_specs=[SMEM] * len(scalars) + [VM...]
    unnamed x1 -> x0, blocking collectives: 13.7 us -> none
    dot_general x8 -> x0, matrix products: 10.7 us -> none  [the longest x4 8.36 us: mix_view(): jnp.einsum('tes,tec->tsc', tables[view_index], picked, precision=lax.Prec...]
  transfers between devices with their start and end apart: 4 -> 7, of which waited for: 4 -> 5; matrix products, arithmetic and copies ran while one was open for 0% -> 1% of each run, Pallas kernels for 0% -> 0%
where the time goes in v1:
time: 247 us; the launch traced here: 246 us
  blocking collectives  92.6 us (37%)
  waiting for transfers between devices  78.3 us (32%)
  Pallas kernels  44.3 us (18%)
  starting transfers between devices  21.9 us (9%)
  local copies, waits for them, and re-layouts  6.27 us (3%)
    all_to_all x1, waiting for transfers between devices, per_device(): lax.all_to_all(words.reshape(peers, 40, f_in), NODES, split_axis=0, conca...  58.2 us
    pallas_call x6, Pallas kernels, call(): pl.pallas_call(body, out_shape=outs, in_specs=[SMEM] * len(scalars) + [VM...  44.3 us
    all_to_all x1, blocking collectives, per_device(): lax.all_to_all(sent.reshape(peers, halo // 2, f_in), NODES, split_axis=0,...  43.6 us
    all_to_all x1, blocking collectives, per_device(): sums = lax.all_to_all(sums, NODES, split_axis=0, concat_axis=0, tiled=True)  27.5 us
    all_to_all x1, blocking collectives, per_device(): losses = lax.all_to_all(loss, NODES_FEAT, 0, 0, tiled=True)  21.5 us
    all_to_all x1, waiting for transfers between devices, per_device(): lax.all_to_all(partial, NODES, split_axis=0, concat_axis=0, tiled=True)  17.1 us
    ppermute x5, starting transfers between devices, partner(): return lax.ppermute(value, 'feat', swap)  8.18 us
    all_to_all x1, starting transfers between devices, per_device(): lax.all_to_all(words.reshape(peers, 40, f_in), NODES, split_axis=0, conca...  7.14 us
  transfers between devices with their start and end apart: 7, of which 5 were waited for; matrix products, arithmetic and copies ran while one was open for 1% of the time, Pallas kernels for 0%

profile of v1, /device:TPU:1, one launch (start us, length us, event | category | flops | bytes accessed | tf_op | source)
XLA Modules:
  0.0 246.4 jit_solution(16013011315552542533)
XLA Ops:
  0.7 0.9 copy.12
  1.5 0.7 reshape.41.outbound
  2.2 5.8 %send_features.1 = bf16[4096,128]{1,0:T(8,128)(2,1)} custom-call(s32[1]{0:T(128)} %bitcast.core, s32[8192]{0:T(1024)} %reshape.41.outbound, bf16[512,128]{1,0:T(8,128)(2,1)} %features.3), custom_call_target="tpu_custom_call" | custom-call | tf_op jit(solution)/shard_map/send_features/pallas_call | solution.py:25
  8.0 43.6 %all_to_all.25 = bf16[128,32,128]{2,1,0:T(8,128)(2,1)S(1)} all-to-all(bf16[128,32,128]{2,1,0:T(8,128)(2,1)} %bitcast.11), channel_id=1, replica_groups=mesh['nodes_0'=4,'nodes_1'=8,'nodes_2'=4,'feat'=2] {'nodes_0','nodes_1',..., dimensions={0} | all-to-all | bytes 2097152 | tf_op jit(solution)/shard_map/all_to_all | solution.py:353
  51.6 3.6 %collective-permute-start = (bf16[128,32,128]{2,1,0:T(8,128)(2,1)S(1)}, bf16[128,32,128]{2,1,0:T(8,128)(2,1)S(1)}, u32[]{:S(2)}, u32[]{:S(2)}) collective-permute-start(bf16[128,32,128]{2,1,0:T(8,128)(2,1)S(1)} %all_to_all.25), channel_id=1, source_target_pairs={{0,1},{1,0},{2,3},{3,2},{4,5},{5,4},{6,7},{7,6},{8,9},{9,8},{10,11... | collective-permute-start | bytes 3145736 | tf_op jit(solution)/shard_map/ppermute | solution.py:333
  55.2 0.1 fusion.6
  55.3 0.6 select_n.43.targets
  56.6 0.6 compare_select_fusion.1.sources
  57.2 0.3 collective-permute-done
  57.5 1.0 copy-done.3
  58.5 15.4 %first_mix.1 = (f32[512,128]{1,0:T(8,128)}, s32[5120,128]{1,0:T(8,128)}) custom-call(s32[1]{0:T(128)S(6)} %copy.13.live_count, s32[4096]{0:T(1024)} %compare_select_fusion.1.sources, s32[8192]{0:T(1024)} %reshape.41.outbound, bf16[512,128]{1,0:T(8,128)(2,1)} %features.3, bf16[4096,128]{1,0:T(8,128)(2,1)} %bitcast.10, bf16[4096,128]{1,0:T(8,128)(2,1)} %bitcast.13, ...), custom_call_target="tpu_custom_call" | custom-call | tf_op jit(solution)/shard_map/first_mix/pallas_call | solution.py:25
  73.9 7.1 %all-to-all-start.1 = ((s32[128,40,128]{2,1,0:T(8,128)}), s32[128,40,128]{2,1,0:T(8,128)S(1)}, u32[]{:S(2)}, u32[]{:S(2)}) async-start(s32[128,40,128]{2,1,0:T(8,128)} %bitcast.12), calls=%async_computation.1 | async-start | bytes 5242880 | tf_op jit(solution)/shard_map/all_to_all | solution.py:378
  81.1 0.7 collective-permute-start.3
  81.8 0.1 collective-permute-start.1
  82.0 0.4 collective-permute-start.2
  82.4 0.9 collective-permute-done.2.b_other
  83.3 0.0 collective-permute-done.3.w2_other
  83.3 58.2 %all-to-all-done.1 = s32[128,40,128]{2,1,0:T(8,128)S(1)} async-done(((s32[128,40,128]{2,1,0:T(8,128)}), s32[128,40,128]{2,1,0:T(8,128)S(1)}, u32[]{:S(2)}, u32[]{:S(2)}) %all-to-all-start.1) | async-done | bytes 2621472 | tf_op jit(solution)/shard_map/all_to_all | solution.py:378
  141.5 1.5 copy-done
  143.0 16.0 %second_mix.1 = (f32[512,512]{1,0:T(8,128)}, f32[128,8,128]{2,1,0:T(8,128)}, f32[8,128]{1,0:T(8,128)}) custom-call(s32[1]{0:T(128)} %bitcast.core, s32[1]{0:T(128)S(6)} %copy.13.live_count, s32[4096]{0:T(1024)} %bitcast.15, s32[5120,128]{1,0:T(8,128)} %bitcast.9, f32[512,128]{1,0:T(8,128)} %get-tuple-element.13.mixed, s32[4,1024]{1,0:T(4,128)} %select_n.43.targets, ...), custom_call_target="tpu_custom_call" | custom-call | tf_op jit(solution)/shard_map/second_mix/pallas_call | solution.py:25
  159.0 27.5 %all_to_all.26.sums = f32[128,8,128]{2,1,0:T(8,128)} all-to-all(f32[128,8,128]{2,1,0:T(8,128)} %get-tuple-element.14), channel_id=1, replica_groups=mesh['nodes_0'=4,'nodes_1'=8,'nodes_2'=4,'feat'=2] {'nodes_0','nodes_1',..., dimensions={0} | all-to-all | bytes 1048576 | tf_op jit(solution)/shard_map/all_to_all | solution.py:406
  186.5 2.5 %normalize.1.own = bf16[512,512]{1,0:T(8,128)(2,1)} custom-call(s32[1]{0:T(128)S(6)} %copy.13.live_count, f32[128,8,128]{2,1,0:T(8,128)} %all_to_all.26.sums, f32[8,128]{1,0:T(8,128)} %get-tuple-element.15.node_total, f32[512,512]{1,0:T(8,128)} %get-tuple-element.16.embedded), custom_call_target="tpu_custom_call" | custom-call | tf_op jit(solution)/shard_map/normalize/pallas_call | solution.py:25
  189.0 3.4 %collective-permute-start.4 = (bf16[512,512]{1,0:T(8,128)(2,1)}, bf16[512,512]{1,0:T(8,128)(2,1)S(1)}, u32[]{:S(2)}, u32[]{:S(2)}) collective-permute-start(bf16[512,512]{1,0:T(8,128)(2,1)} %normalize.1.own), channel_id=1, source_target_pairs={{0,1},{1,0},{2,3},{3,2},{4,5},{5,4},{6,7},{7,6},{8,9},{9,8},{10,11... | collective-permute-start | bytes 1572872 | tf_op jit(solution)/shard_map/ppermute | solution.py:333
  192.4 1.7 collective-permute-done.4.other
  194.2 0.8 copy-done.4
  195.0 2.5 %correlate.1 = (bf16[2,512,256]{2,1,0:T(8,128)(2,1)}, f32[128,8,128]{2,1,0:T(8,128)}) custom-call(s32[1]{0:T(128)} %bitcast.core, bf16[512,512]{1,0:T(8,128)(2,1)} %normalize.1.own, bf16[512,512]{1,0:T(8,128)(2,1)} %copy-done.4), custom_call_target="tpu_custom_call" | custom-call | tf_op jit(solution)/shard_map/correlate/pallas_call | solution.py:25
  197.5 6.6 %all-to-all-start.3 = ((f32[128,8,128]{2,1,0:T(8,128)}), f32[128,8,128]{2,1,0:T(8,128)S(1)}, u32[]{:S(2)}, u32[]{:S(2)}) async-start(f32[128,8,128]{2,1,0:T(8,128)} %get-tuple-element.18), calls=%async_computation.3 | async-start | bytes 1048576 | tf_op jit(solution)/shard_map/all_to_all | solution.py:426
  204.1 17.1 %all-to-all-done.3.arrived = f32[128,8,128]{2,1,0:T(8,128)S(1)} async-done(((f32[128,8,128]{2,1,0:T(8,128)}), f32[128,8,128]{2,1,0:T(8,128)S(1)}, u32[]{:S(2)}, u32[]{:S(2)}) %all-to-all-start.3) | async-done | bytes 524320 | tf_op jit(solution)/shard_map/all_to_all | solution.py:426
  221.3 0.8 copy-done.2
  222.1 2.0 finish.1
  224.0 21.5 %all_to_all.27 = f32[256,1,128]{2,1,0:T(1,128)S(1)} all-to-all(f32[256,1,128]{2,1,0:T(1,128)} %get-tuple-element.20), channel_id=1, replica_groups=mesh['nodes_0'=4,'nodes_1'=8,'nodes_2'=4,'feat'=2] {'nodes_0','nodes_1',..., dimensions={0} | all-to-all | bytes 262144 | tf_op jit(solution)/shard_map/all_to_all | solution.py:437
  245.5 0.9 slice_reduce_fusion
  (27 shorter events, 0.1 us)
Async XLA Ops:
  0.6 54.6 %copy-start.12 = (s32[2,4096]{1,0:T(2,128)S(1)}, s32[2,4096]{1,0:T(2,128)}, u32[]{:S(2)}) copy-start(s32[2,4096]{1,0:T(2,128)} %param.12) | copy-start | bytes 98308
  0.6 54.6 %copy-start.10 = (s32[2,4096]{1,0:T(2,128)S(1)}, s32[2,4096]{1,0:T(2,128)}, u32[]{:S(2)}) copy-start(s32[2,4096]{1,0:T(2,128)} %param.13) | copy-start | bytes 98308
  0.7 54.6 %copy-start.11 = (s32[2,4096]{1,0:T(2,128)S(1)}, s32[2,4096]{1,0:T(2,128)}, u32[]{:S(2)}) copy-start(s32[2,4096]{1,0:T(2,128)} %param.14) | copy-start | bytes 98308
  51.6 5.9 %copy-start.1 = (bf16[128,32,128]{2,1,0:T(8,128)(2,1)}, bf16[128,32,128]{2,1,0:T(8,128)(2,1)S(1)}, u32[]{:S(2)}) copy-start(bf16[128,32,128]{2,1,0:T(8,128)(2,1)S(1)} %all_to_all.25) | copy-start | bytes 3145732
  51.6 5.9 %collective-permute-start = (bf16[128,32,128]{2,1,0:T(8,128)(2,1)S(1)}, bf16[128,32,128]{2,1,0:T(8,128)(2,1)S(1)}, u32[]{:S(2)}, u32[]{:S(2)}) collective-permute-start(bf16[128,32,128]{2,1,0:T(8,128)(2,1)S(1)} %all_to_all.25), channel_id=1, source_target_pairs={{0,1},{1,0},{2,3},{3,2},{4,5},{5,4},{6,7},{7,6},{8,9},{9,8},{10,11... | collective-permute-start | bytes 3145736 | tf_op jit(solution)/shard_map/ppermute | solution.py:333
  55.3 18.6 %copy-start.7 = (s32[1,4096]{1,0:T(1,128)}, s32[1,4096]{1,0:T(1,128)S(1)}, u32[]{:S(2)}) copy-start(s32[1,4096]{1,0:T(1,128)S(1)} %get-tuple-element.22) | copy-start | bytes 49156
  57.5 1.0 copy-start.3
  73.9 7.2 %copy-start.5 = (bf16[512,256]{1,0:T(8,128)(2,1)S(1)}, bf16[512,256]{1,0:T(8,128)(2,1)}, u32[]{:S(2)}) copy-start(bf16[512,256]{1,0:T(8,128)(2,1)} %w2_own.1) | copy-start | bytes 786436
  73.9 7.9 %copy-start.8 = (bf16[128,256]{1,0:T(8,128)(2,1)S(1)}, bf16[128,256]{1,0:T(8,128)(2,1)}, u32[]{:S(2)}) copy-start(bf16[128,256]{1,0:T(8,128)(2,1)} %w1_own.1) | copy-start | bytes 196612
  73.9 8.0 %copy-start.13 = (f32[256]{0:T(256)S(1)}, f32[256]{0:T(256)}, u32[]{:S(2)}) copy-start(f32[256]{0:T(256)} %param.16) | copy-start | bytes 3076
  73.9 67.5 %all-to-all-start.1 = ((s32[128,40,128]{2,1,0:T(8,128)}), s32[128,40,128]{2,1,0:T(8,128)S(1)}, u32[]{:S(2)}, u32[]{:S(2)}) async-start(s32[128,40,128]{2,1,0:T(8,128)} %bitcast.12), calls=%async_computation.1 | async-start | bytes 5242880 | tf_op jit(solution)/shard_map/all_to_all | solution.py:378
  81.1 2.2 collective-permute-start.3
  81.8 1.4 collective-permute-start.1
  82.0 1.3 collective-permute-start.2
  83.3 58.2 %copy-start.14 = (f32[1,256]{1,0:T(1,128)}, f32[1,256]{1,0:T(1,128)S(1)}, u32[]{:S(2)}) copy-start(f32[1,256]{1,0:T(1,128)S(1)} %collective-permute-done.2.b_other) | copy-start | bytes 3076
  83.3 58.2 %copy-start.9 = (bf16[128,256]{1,0:T(8,128)(2,1)}, bf16[128,256]{1,0:T(8,128)(2,1)S(1)}, u32[]{:S(2)}) copy-start(bf16[128,256]{1,0:T(8,128)(2,1)S(1)} %collective-permute-done.1.w1_other) | copy-start | bytes 196612
  83.3 58.2 %copy-start.6 = (bf16[512,256]{1,0:T(8,128)(2,1)}, bf16[512,256]{1,0:T(8,128)(2,1)S(1)}, u32[]{:S(2)}) copy-start(bf16[512,256]{1,0:T(8,128)(2,1)S(1)} %collective-permute-done.3.w2_other) | copy-start | bytes 786436
  141.5 1.5 copy-start
  189.0 5.1 %collective-permute-start.4 = (bf16[512,512]{1,0:T(8,128)(2,1)}, bf16[512,512]{1,0:T(8,128)(2,1)S(1)}, u32[]{:S(2)}, u32[]{:S(2)}) collective-permute-start(bf16[512,512]{1,0:T(8,128)(2,1)} %normalize.1.own), channel_id=1, source_target_pairs={{0,1},{1,0},{2,3},{3,2},{4,5},{5,4},{6,7},{7,6},{8,9},{9,8},{10,11... | collective-permute-start | bytes 1572872 | tf_op jit(solution)/shard_map/ppermute | solution.py:333
  194.2 0.8 copy-start.4
  197.5 23.8 %all-to-all-start.3 = ((f32[128,8,128]{2,1,0:T(8,128)}), f32[128,8,128]{2,1,0:T(8,128)S(1)}, u32[]{:S(2)}, u32[]{:S(2)}) async-start(f32[128,8,128]{2,1,0:T(8,128)} %get-tuple-element.18), calls=%async_computation.3 | async-start | bytes 1048576 | tf_op jit(solution)/shard_map/all_to_all | solution.py:426
  221.2 0.8 copy-start.2

commit v2 on v1

--- a/solution.py
+++ b/solution.py
@@ -9,7 +9,8 @@
 from jax.sharding import PartitionSpec as P
 
 NODES = ("nodes_0", "nodes_1", "nodes_2")
-NODES_FEAT = ("nodes_0", "nodes_1", "nodes_2", "feat")
+PLANE = ("nodes_0", "nodes_2")
+PLANE_FEAT = ("nodes_0", "nodes_2", "feat")
 
 LANES = 128
 TILE = 128
@@ -28,7 +29,7 @@
         in_specs=[SMEM] * len(scalars) + [VMEM] * len(operands),
         out_specs=jax.tree.map(lambda _: VMEM, outs),
         scratch_shapes=scratch,
-        compiler_params=pltpu.CompilerParams(vmem_limit_bytes=56 * 2**20),
+        compiler_params=pltpu.CompilerParams(vmem_limit_bytes=26 * 2**20),
         name=name,
     )(*scalars, *operands)
 
@@ -37,7 +38,7 @@
     def step(block, _):
         base = pl.multiple_of(block * unroll, unroll)
         for lane in range(unroll):
-            source = index[first_index + base + lane]
+            source = index.at[pl.ds(lane, index.shape[0] - unroll)][first_index + base]
             rows[pl.ds(first_row + base + lane, 1), :] = table[pl.ds(source, 1), :]
         return 0
 
@@ -77,7 +78,8 @@
         base = pl.multiple_of(block * 4 * half, 4 * half)
         for peer in range(4):
             for slot in range(half):
-                source = outbound[(block * 4 + peer) * (2 * half) + first + slot]
+                near = outbound.at[pl.ds(peer * 2 * half + slot, outbound.shape[0] - 8 * half)]
+                source = near[block * (8 * half) + first]
                 rows[pl.ds(base + peer * half + slot, 1), :] = table[pl.ds(source, 1), :]
         return 0
 
@@ -252,12 +254,17 @@
         squares = squares + jnp.sum(value * value, 0, keepdims=True)
     for part in range(4):
         columns = slice(part * LANES, (part + 1) * LANES)
-        sums[:, part : part + 1, :] = jnp.broadcast_to(
-            total[:, columns][None], (sums.shape[0], 1, LANES)
-        )
-        sums[:, part + 4 : part + 5, :] = jnp.broadcast_to(
-            squares[:, columns][None], (sums.shape[0], 1, LANES)
-        )
+        for peer in range(sums.shape[0]):
+            sums[peer, part : part + 1, :] = total[:, columns]
+            sums[peer, part + 4 : part + 5, :] = squares[:, columns]
+
+
+def add_and_copy(arrived, out):
+    total = arrived[0]
+    for peer in range(1, arrived.shape[0]):
+        total = total + arrived[peer]
+    for peer in range(out.shape[0]):
+        out[peer] = total
 
 
 def normalize(live_count, sums, node_total, embedded, out):
@@ -276,15 +283,18 @@
 def correlate(core, own, other, normed, out):
     half = normed.shape[2]
     width = 2 * half
+    groups, depth, wide = out.shape[0], out.shape[1] // 4, 4
     contract = (((0,), (0,)), ((), ()))
 
     def give(left, right):
         product = lax.dot_general(left, right, contract, preferred_element_type=jnp.float32)
-        for pair in range(width // 8):
-            near = product[pair * 8 : pair * 8 + 8, 0:LANES]
-            far = product[pair * 8 : pair * 8 + 8, LANES:half]
-            out[2 * pair] = jnp.concatenate([near[0:4], far[0:4]], 0)
-            out[2 * pair + 1] = jnp.concatenate([near[4:8], far[4:8]], 0)
+        for group in range(groups):
+            for near in range(0, depth, 2):
+                rows = []
+                for n1 in (near, near + 1):
+                    first = ((group // wide) * depth * wide + n1 * wide + group % wide) * 4
+                    rows.append(product[first : first + 4, :])
+                out[group, near * 4 : near * 4 + 8, :] = jnp.concatenate(rows, 0)
 
     @pl.when(core[0] == 0)
     def _():
@@ -301,12 +311,19 @@
 
 def finish(core, node, arrived, node_total, correlation, loss):
     half = correlation.shape[1]
-    summed = jnp.sum(arrived[...], 0) / node_total[...]
-    value = jnp.concatenate([summed[0:4, :], summed[4:8, :]], 1)
-    correlation[...] = value
-    share = correlation.shape[0]
-    row = lax.broadcasted_iota(jnp.int32, (share, half), 0) + node[0] * share
-    column = lax.broadcasted_iota(jnp.int32, (share, half), 1) + core[0] * half
+    share, depth, wide = 4, 8, 4
+    n0, n1, n2 = node[0] // (depth * wide), (node[0] // wide) % depth, node[0] % wide
+    value = arrived[0]
+    for peer in range(1, arrived.shape[0]):
+        value = value + arrived[peer]
+    value = value / node_total[0:1, 0:1]
+    place = lax.broadcasted_iota(jnp.int32, value.shape, 0)
+    row = ((n0 * depth + place // share) * wide + n2) * share + place % share
+    column = lax.broadcasted_iota(jnp.int32, value.shape, 1) + core[0] * half
+    mine = value[0:share, :]
+    for other in range(1, depth):
+        mine = jnp.where(n1 == other, value[other * share : (other + 1) * share, :], mine)
+    correlation[...] = mine
     terms = jnp.where(row == column, jnp.square(1.0 - value), 0.005 * jnp.square(value))
     terms = jnp.sum(jnp.sum(terms, 1, keepdims=True), 0, keepdims=True)
     loss[...] = jnp.broadcast_to(terms[None], loss.shape)
@@ -328,9 +345,17 @@
     core = core_index.reshape(1).astype(i32)
     node = node_index.reshape(1).astype(i32)
     swap = [(0, 1), (1, 0)]
+    planes, depth = lax.axis_size(PLANE), lax.axis_size("nodes_1")
 
     def partner(value):
         return lax.ppermute(value, "feat", swap)
+
+    def sum_over_nodes(blocks, name):
+        blocks = lax.all_to_all(blocks, PLANE, split_axis=0, concat_axis=0, tiled=True)
+        copies = call(
+            add_and_copy, shape((depth, *blocks.shape[1:]), f32), [], blocks, name=name
+        )
+        return lax.all_to_all(copies, "nodes_1", split_axis=0, concat_axis=0, tiled=True)
 
     w1_other, w2_other = partner(w_first), partner(w_second)
     bias = b_first.reshape(1, half)
@@ -382,7 +407,7 @@
         second_mix,
         (
             shape((local, width), f32),
-            shape((peers, 8, LANES), f32),
+            shape((planes, 8, LANES), f32),
             shape((8, LANES), f32),
         ),
         [
@@ -403,7 +428,7 @@
         scalars=(core, row_counts, sources),
         name="second_mix",
     )
-    sums = lax.all_to_all(sums, NODES, split_axis=0, concat_axis=0, tiled=True)
+    sums = sum_over_nodes(sums, "add_sums")
     own = call(
         normalize,
         shape((local, width), bf16),
@@ -416,15 +441,15 @@
     )
     normed, partial = call(
         correlate,
-        (shape((2, local, half), bf16), shape((peers, 8, LANES), f32)),
+        (shape((2, local, half), bf16), shape((planes, width // planes, half), f32)),
         [],
         own,
         partner(own),
         scalars=(core,),
         name="correlate",
     )
-    partial = lax.all_to_all(partial, NODES, split_axis=0, concat_axis=0, tiled=True)
-    devices = lax.axis_size(NODES_FEAT)
+    partial = sum_over_nodes(partial, "add_products")
+    devices = lax.axis_size(PLANE_FEAT)
     correlation, loss = call(
         finish,
         (shape((width // peers, half), f32), shape((devices, 1, LANES), f32)),
@@ -434,7 +459,7 @@
         scalars=(core, node),
         name="finish",
     )
-    losses = lax.all_to_all(loss, NODES_FEAT, 0, 0, tiled=True)
+    losses = lax.all_to_all(loss, PLANE_FEAT, 0, 0, tiled=True)
     return (normed, correlation, jnp.sum(losses[:, 0, 0]))
 
 

time: 247 us -> 221 us (0.89)
  Pallas kernels: 44.3 us -> 29.4 us
  waiting for transfers between devices: 78.3 us -> 71.1 us
  starting transfers between devices: 21.9 us -> 19 us
    pallas_call x6 -> x8, Pallas kernels: 44.3 us -> 29.4 us  [call(): pl.pallas_call(body, out_shape=outs, in_specs=[SMEM] * len(scalars) + [VM...]
    all_to_all x1, waiting for transfers between devices: 17.1 us -> 9.61 us  [sum_over_nodes(): lax.all_to_all(copies, 'nodes_1', split_axis=0, concat_axis=0, tiled=True)]
    all_to_all x1, starting transfers between devices: 6.61 us -> 3.41 us  [sum_over_nodes(): lax.all_to_all(copies, 'nodes_1', split_axis=0, concat_axis=0, tiled=True)]
    all_to_all x2 -> x4, blocking collectives: 49 us -> 50.1 us  [the longest x2 25.1 us: sum_over_nodes(): lax.all_to_all(blocks, PLANE, split_axis=0, concat_axis=0, tiled=True)]
    unnamed x31 -> x23, local copies, waits for them, and re-layouts: 4.97 us -> 4.78 us
  transfers between devices with their start and end apart: 7 -> 7, of which waited for: 5 -> 5; matrix products, arithmetic and copies ran while one was open for 1% -> 0% of each run, Pallas kernels for 0% -> 0%
where the time goes in v2:
time: 221 us; the launch traced here: 220 us
  blocking collectives  93.5 us (42%)
  waiting for transfers between devices  71.1 us (32%)
  Pallas kernels  29.4 us (13%)
  starting transfers between devices  19 us (9%)
  local copies, waits for them, and re-layouts  4.87 us (2%)
    all_to_all x1, waiting for transfers between devices, per_device(): lax.all_to_all(words.reshape(peers, 40, f_in), NODES, split_axis=0, conca...  57.6 us
    all_to_all x1, blocking collectives, per_device(): lax.all_to_all(sent.reshape(peers, halo // 2, f_in), NODES, split_axis=0,...  43.4 us
    pallas_call x8, Pallas kernels, call(): pl.pallas_call(body, out_shape=outs, in_specs=[SMEM] * len(scalars) + [VM...  29.4 us
    all_to_all x2, blocking collectives, sum_over_nodes(): lax.all_to_all(blocks, PLANE, split_axis=0, concat_axis=0, tiled=True)  25.1 us
    all_to_all x1, blocking collectives, per_device(): losses = lax.all_to_all(loss, PLANE_FEAT, 0, 0, tiled=True)  13.7 us
    all_to_all x1, blocking collectives, sum_over_nodes(): lax.all_to_all(copies, 'nodes_1', split_axis=0, concat_axis=0, tiled=True)  11.3 us
    all_to_all x1, waiting for transfers between devices, sum_over_nodes(): lax.all_to_all(copies, 'nodes_1', split_axis=0, concat_axis=0, tiled=True)  9.61 us
    ppermute x5, starting transfers between devices, partner(): return lax.ppermute(value, 'feat', swap)  8.48 us
  transfers between devices with their start and end apart: 7, of which 5 were waited for; matrix products, arithmetic and copies ran while one was open for 0% of the time, Pallas kernels for 0%

profile of v2, /device:TPU:1, one launch (start us, length us, event | category | flops | bytes accessed | tf_op | source)
XLA Modules:
  0.0 220.1 jit_solution(13905378866737802845)
XLA Ops:
  0.7 0.9 copy.12
  1.6 0.1 reshape.41.outbound
  1.6 0.9 copy-done.1
  2.5 3.6 %send_features.1 = bf16[4096,128]{1,0:T(8,128)(2,1)S(1)} custom-call(s32[1]{0:T(128)} %bitcast.core, s32[8192]{0:T(1024)S(1)} %reshape.41.outbound, bf16[512,128]{1,0:T(8,128)(2,1)S(1)} %copy-done.1), custom_call_target="tpu_custom_call" | custom-call | tf_op jit(solution)/shard_map/send_features/pallas_call | solution.py:26
  6.1 43.4 %all_to_all.35 = bf16[128,32,128]{2,1,0:T(8,128)(2,1)S(1)} all-to-all(bf16[128,32,128]{2,1,0:T(8,128)(2,1)S(1)} %bitcast.11), channel_id=1, replica_groups=mesh['nodes_0'=4,'nodes_1'=8,'nodes_2'=4,'feat'=2] {'nodes_0','nodes_1',..., dimensions={0} | all-to-all | bytes 2097152 | tf_op jit(solution)/shard_map/all_to_all | solution.py:378
  49.5 3.6 %collective-permute-start = (bf16[128,32,128]{2,1,0:T(8,128)(2,1)S(1)}, bf16[128,32,128]{2,1,0:T(8,128)(2,1)S(1)}, u32[]{:S(2)}, u32[]{:S(2)}) collective-permute-start(bf16[128,32,128]{2,1,0:T(8,128)(2,1)S(1)} %all_to_all.35), channel_id=1, source_target_pairs={{0,1},{1,0},{2,3},{3,2},{4,5},{5,4},{6,7},{7,6},{8,9},{9,8},{10,11... | collective-permute-start | bytes 3145736 | tf_op jit(solution)/shard_map/ppermute | solution.py:351
  53.1 0.1 fusion.6
  53.9 1.5 collective-permute-done
  55.4 10.4 %first_mix.1 = (f32[512,128]{1,0:T(8,128)S(1)}, s32[5120,128]{1,0:T(8,128)S(1)}) custom-call(s32[1]{0:T(128)S(6)} %copy.13.live_count, s32[4096]{0:T(1024)S(1)} %compare_select_fusion.1.sources, s32[8192]{0:T(1024)S(1)} %reshape.41.outbound, bf16[512,128]{1,0:T(8,128)(2,1)S(1)} %copy-done.2, bf16[4096,128]{1,0:T(8,128)(2,1)S(1)} %bitcast.10, ...), custom_call_target="tpu_custom_call" | custom-call | tf_op jit(solution)/shard_map/first_mix/pallas_call | solution.py:26
  65.8 1.5 copy-done
  67.3 7.1 %all-to-all-start.1 = ((s32[128,40,128]{2,1,0:T(8,128)}), s32[128,40,128]{2,1,0:T(8,128)S(1)}, u32[]{:S(2)}, u32[]{:S(2)}) async-start(s32[128,40,128]{2,1,0:T(8,128)} %bitcast.12), calls=%async_computation.1 | async-start | bytes 5242880 | tf_op jit(solution)/shard_map/all_to_all | solution.py:403
  74.5 0.7 collective-permute-start.3
  75.2 0.1 collective-permute-start.1
  75.3 0.4 collective-permute-start.2
  75.7 0.9 collective-permute-done.2.b_other
  76.7 0.6 copy-done.5
  77.3 57.6 %all-to-all-done.1 = s32[128,40,128]{2,1,0:T(8,128)S(1)} async-done(((s32[128,40,128]{2,1,0:T(8,128)}), s32[128,40,128]{2,1,0:T(8,128)S(1)}, u32[]{:S(2)}, u32[]{:S(2)}) %all-to-all-start.1) | async-done | bytes 2621472 | tf_op jit(solution)/shard_map/all_to_all | solution.py:403
  134.8 0.8 copy-done.6
  135.7 12.7 %second_mix.1 = (f32[512,512]{1,0:T(8,128)S(1)}, f32[16,8,128]{2,1,0:T(8,128)S(1)}, f32[8,128]{1,0:T(8,128)S(1)}) custom-call(s32[1]{0:T(128)} %bitcast.core, s32[1]{0:T(128)S(6)} %copy.13.live_count, s32[4096]{0:T(1024)S(1)} %bitcast.15, s32[5120,128]{1,0:T(8,128)S(1)} %bitcast.9, f32[512,128]{1,0:T(8,128)S(1)} %get-tuple-element.13.mixed, ...), custom_call_target="tpu_custom_call" | custom-call | tf_op jit(solution)/shard_map/second_mix/pallas_call | solution.py:26
  148.4 11.6 %all_to_all.36.arrived = f32[16,8,128]{2,1,0:T(8,128)S(1)} all-to-all(f32[16,8,128]{2,1,0:T(8,128)S(1)} %get-tuple-element.14), channel_id=1, replica_groups=mesh['nodes_0'=4,'nodes_1'=8,'nodes_2'=4,'feat'=2] {'nodes_0','nodes_2'}, dimensions={0} | all-to-all | bytes 131072 | tf_op jit(solution)/shard_map/all_to_all | solution.py:354
  159.9 11.3 %all_to_all.37.sums = f32[8,8,128]{2,1,0:T(8,128)S(1)} all-to-all(f32[8,8,128]{2,1,0:T(8,128)S(1)} %add_sums.1), channel_id=1, replica_groups=mesh['nodes_0'=4,'nodes_1'=8,'nodes_2'=4,'feat'=2] {'nodes_1'}, dimensions={0} | all-to-all | bytes 65536 | tf_op jit(solution)/shard_map/all_to_all | solution.py:358
  171.2 0.2 normalize.1.own
  171.5 3.7 %collective-permute-start.4 = (bf16[512,512]{1,0:T(8,128)(2,1)S(1)}, bf16[512,512]{1,0:T(8,128)(2,1)S(1)}, u32[]{:S(2)}, u32[]{:S(2)}) collective-permute-start(bf16[512,512]{1,0:T(8,128)(2,1)S(1)} %normalize.1.own), channel_id=1, source_target_pairs={{0,1},{1,0},{2,3},{3,2},{4,5},{5,4},{6,7},{7,6},{8,9},{9,8},{10,11... | collective-permute-start | bytes 1572872 | tf_op jit(solution)/shard_map/ppermute | solution.py:351
  175.1 1.5 collective-permute-done.4.other
  176.6 1.1 correlate.1
  177.8 13.5 %all_to_all.38.arrived = f32[16,32,256]{2,1,0:T(8,128)S(1)} all-to-all(f32[16,32,256]{2,1,0:T(8,128)S(1)} %get-tuple-element.18), channel_id=1, replica_groups=mesh['nodes_0'=4,'nodes_1'=8,'nodes_2'=4,'feat'=2] {'nodes_0','nodes_2'}, dimensions={0} | all-to-all | bytes 1048576 | tf_op jit(solution)/shard_map/all_to_all | solution.py:354
  191.3 0.7 add_products.1
  192.1 3.4 %all-to-all-start.5 = ((f32[8,32,256]{2,1,0:T(8,128)}), f32[8,32,256]{2,1,0:T(8,128)S(1)}, u32[]{:S(2)}, u32[]{:S(2)}) async-start(f32[8,32,256]{2,1,0:T(8,128)} %add_products.1), calls=%async_computation.5 | async-start | bytes 524288 | tf_op jit(solution)/shard_map/all_to_all | solution.py:358
  195.5 9.6 %all-to-all-done.5.arrived = f32[8,32,256]{2,1,0:T(8,128)S(1)} async-done(((f32[8,32,256]{2,1,0:T(8,128)}), f32[8,32,256]{2,1,0:T(8,128)S(1)}, u32[]{:S(2)}, u32[]{:S(2)}) %all-to-all-start.5) | async-done | bytes 262176 | tf_op jit(solution)/shard_map/all_to_all | solution.py:358
  205.1 0.6 finish.1
  205.8 13.7 %all_to_all.39 = f32[32,1,128]{2,1,0:T(1,128)S(1)} all-to-all(f32[32,1,128]{2,1,0:T(1,128)S(1)} %get-tuple-element.20), channel_id=1, replica_groups=mesh['nodes_0'=4,'nodes_1'=8,'nodes_2'=4,'feat'=2] {'nodes_0','nodes_2',..., dimensions={0} | all-to-all | bytes 32768 | tf_op jit(solution)/shard_map/all_to_all | solution.py:462
  219.4 0.6 slice_reduce_fusion
  (23 shorter events, 0.1 us)
Async XLA Ops:
  0.6 54.8 %copy-start.2 = (bf16[512,128]{1,0:T(8,128)(2,1)S(1)}, bf16[512,128]{1,0:T(8,128)(2,1)}, u32[]{:S(2)}) copy-start(bf16[512,128]{1,0:T(8,128)(2,1)} %features.3) | copy-start | bytes 393220
  0.6 52.5 %copy-start.8 = (s32[2,4096]{1,0:T(2,128)S(1)}, s32[2,4096]{1,0:T(2,128)}, u32[]{:S(2)}) copy-start(s32[2,4096]{1,0:T(2,128)} %param.13) | copy-start | bytes 98308
  0.7 52.5 %copy-start.9 = (s32[2,4096]{1,0:T(2,128)S(1)}, s32[2,4096]{1,0:T(2,128)}, u32[]{:S(2)}) copy-start(s32[2,4096]{1,0:T(2,128)} %param.14) | copy-start | bytes 98308
  1.6 0.9 copy-start.1
  2.5 50.6 %copy-start.10 = (s32[2,4096]{1,0:T(2,128)S(1)}, s32[2,4096]{1,0:T(2,128)}, u32[]{:S(2)}) copy-start(s32[2,4096]{1,0:T(2,128)} %param.12) | copy-start | bytes 98308
  49.5 5.9 %collective-permute-start = (bf16[128,32,128]{2,1,0:T(8,128)(2,1)S(1)}, bf16[128,32,128]{2,1,0:T(8,128)(2,1)S(1)}, u32[]{:S(2)}, u32[]{:S(2)}) collective-permute-start(bf16[128,32,128]{2,1,0:T(8,128)(2,1)S(1)} %all_to_all.35), channel_id=1, source_target_pairs={{0,1},{1,0},{2,3},{3,2},{4,5},{5,4},{6,7},{7,6},{8,9},{9,8},{10,11... | collective-permute-start | bytes 3145736 | tf_op jit(solution)/shard_map/ppermute | solution.py:351
  65.8 1.5 copy-start
  67.3 7.1 %copy-start.3 = (bf16[512,256]{1,0:T(8,128)(2,1)S(1)}, bf16[512,256]{1,0:T(8,128)(2,1)}, u32[]{:S(2)}) copy-start(bf16[512,256]{1,0:T(8,128)(2,1)} %w2_own.1) | copy-start | bytes 786436
  67.3 7.9 %copy-start.4 = (bf16[128,256]{1,0:T(8,128)(2,1)S(1)}, bf16[128,256]{1,0:T(8,128)(2,1)}, u32[]{:S(2)}) copy-start(bf16[128,256]{1,0:T(8,128)(2,1)} %w1_own.1) | copy-start | bytes 196612
  67.3 8.0 %copy-start.7 = (f32[256]{0:T(256)S(1)}, f32[256]{0:T(256)}, u32[]{:S(2)}) copy-start(f32[256]{0:T(256)} %param.16) | copy-start | bytes 3076
  67.3 67.5 %all-to-all-start.1 = ((s32[128,40,128]{2,1,0:T(8,128)}), s32[128,40,128]{2,1,0:T(8,128)S(1)}, u32[]{:S(2)}, u32[]{:S(2)}) async-start(s32[128,40,128]{2,1,0:T(8,128)} %bitcast.12), calls=%async_computation.1 | async-start | bytes 5242880 | tf_op jit(solution)/shard_map/all_to_all | solution.py:403
  74.5 2.8 %collective-permute-start.3 = (bf16[512,256]{1,0:T(8,128)(2,1)S(1)}, bf16[512,256]{1,0:T(8,128)(2,1)S(1)}, u32[]{:S(2)}, u32[]{:S(2)}) collective-permute-start(bf16[512,256]{1,0:T(8,128)(2,1)S(1)} %copy-done.3), channel_id=1, source_target_pairs={{0,1},{1,0},{2,3},{3,2},{4,5},{5,4},{6,7},{7,6},{8,9},{9,8},{10,11... | collective-permute-start | bytes 786440 | tf_op jit(solution)/shard_map/ppermute | solution.py:351
  75.2 1.4 collective-permute-start.1
  75.3 1.3 collective-permute-start.2
  76.7 0.6 copy-start.5
  134.8 0.8 copy-start.6
  171.5 5.2 %collective-permute-start.4 = (bf16[512,512]{1,0:T(8,128)(2,1)S(1)}, bf16[512,512]{1,0:T(8,128)(2,1)S(1)}, u32[]{:S(2)}, u32[]{:S(2)}) collective-permute-start(bf16[512,512]{1,0:T(8,128)(2,1)S(1)} %normalize.1.own), channel_id=1, source_target_pairs={{0,1},{1,0},{2,3},{3,2},{4,5},{5,4},{6,7},{7,6},{8,9},{9,8},{10,11... | collective-permute-start | bytes 1572872 | tf_op jit(solution)/shard_map/ppermute | solution.py:351
  192.1 13.0 %all-to-all-start.5 = ((f32[8,32,256]{2,1,0:T(8,128)}), f32[8,32,256]{2,1,0:T(8,128)S(1)}, u32[]{:S(2)}, u32[]{:S(2)}) async-start(f32[8,32,256]{2,1,0:T(8,128)} %add_products.1), calls=%async_computation.5 | async-start | bytes 524288 | tf_op jit(solution)/shard_map/all_to_all | solution.py:358

commit v3 on v2

--- a/solution.py
+++ b/solution.py
@@ -51,15 +51,6 @@
         return 0
 
     lax.fori_loop(0, total // size, step, 0)
-
-
-def several(total, unroll, body):
-    def step(block, _):
-        for one in range(unroll):
-            body(block * unroll + one)
-        return 0
-
-    lax.fori_loop(0, total // unroll, step, 0)
 
 
 def edge_table(targets, tile):
@@ -104,7 +95,8 @@
     table,
     picked,
     codes,
-    coded,
+    coded_even,
+    coded_odd,
 ):
     local = features.shape[0]
     halo = own.shape[0]
@@ -133,17 +125,20 @@
         code = jnp.clip(code, -CODE_TOP, CODE_TOP - 1).astype(jnp.int32)
         codes[rows, :] = (code & (2**CODE_BITS - 1)) | (step.astype(jnp.int32) << CODE_BITS)
 
-    pick_rows(outbound, 0, codes, coded, 0, coded.shape[0], 128)
     group = lax.broadcasted_iota(jnp.int32, (8, LANES), 1) // 16
 
     patch = lax.broadcasted_iota(jnp.int32, (8, LANES), 0)
     count = jnp.where(patch == 0, live_count[0] & 255, live_count[0] >> 8) << 24
     patched = (lax.broadcasted_iota(jnp.int32, (8, LANES), 1) == 1) & (patch < 2)
 
-    def pack(peer):
-        base = pl.multiple_of(peer * 64, 64)
+    def pick(block, side, coded):
+        for slot in range(128):
+            near = outbound.at[pl.ds(side * 128 + slot, outbound.shape[0] - 255)]
+            coded[slot : slot + 1, :] = codes[pl.ds(near[block * 256], 1), :]
+
+    def pack(peer, first, coded):
         to = pl.multiple_of(peer * 40, 8)
-        octet = [coded[pl.ds(base + 8 * k, 8), :] for k in range(8)]
+        octet = [coded[first + 8 * k : first + 8 * k + 8, :] for k in range(8)]
         for k in range(4):
             low = (octet[k] >> 3) & 0xFFFF
             words[pl.ds(to + 8 * k, 8), :] = low | ((octet[k + 4] >> 3) << 16)
@@ -155,7 +150,19 @@
         rest = rest | jnp.where(patched, count, (steps >> CODE_BITS) << 24)
         words[pl.ds(to + 32, 8), :] = rest
 
-    several(coded.shape[0] // 64, 8, pack)
+    blocks = words.shape[0] // 160
+    pick(0, 0, coded_even)
+
+    def both(block, _):
+        pick(block, 1, coded_odd)
+        pack(block * 4, 0, coded_even)
+        pack(block * 4 + 1, 64, coded_even)
+        pick(jnp.minimum(block + 1, blocks - 1), 0, coded_even)
+        pack(block * 4 + 2, 0, coded_odd)
+        pack(block * 4 + 3, 64, coded_odd)
+        return 0
+
+    lax.fori_loop(0, blocks, both, 0)
 
 
 def split_three(value):
@@ -183,7 +190,8 @@
     sums,
     node_total,
     table,
-    picked,
+    picked_even,
+    picked_odd,
     w1,
     w2,
 ):
@@ -235,10 +243,19 @@
     edges = targets.shape[1]
     total = jnp.zeros((1, 2 * half), jnp.float32)
     squares = jnp.zeros((1, 2 * half), jnp.float32)
+
+    def pick(tile, picked):
+        picked[0:TILE, :] = mixed[tile * TILE : (tile + 1) * TILE, :]
+        for edge in range(edges):
+            source = sources[tile * edges + edge]
+            picked[TILE + edge : TILE + edge + 1, :] = table[pl.ds(source, 1), :]
+
+    pick(0, picked_even)
     for tile in range(local // TILE):
         rows = slice(tile * TILE, (tile + 1) * TILE)
-        picked[0:TILE, :] = mixed[rows, :]
-        pick_rows(sources, tile * edges, table, picked, TILE, edges, 128)
+        picked, later = (picked_even, picked_odd) if tile % 2 == 0 else (picked_odd, picked_even)
+        if tile + 1 < local // TILE:
+            pick(tile + 1, later)
         value = jnp.concatenate(split_three(picked[...]), 1)
         hidden = jnp.dot(value, w1[...], preferred_element_type=jnp.float32) + bias
         hidden = jnp.maximum(hidden, 0.0).astype(jnp.bfloat16)
@@ -375,6 +392,9 @@
         scalars=(core, outbound),
         name="send_features",
     )
+    sent, w1_other, w2_other, bias_other = lax.optimization_barrier(
+        (sent, w1_other, w2_other, bias_other)
+    )
     got = lax.all_to_all(
         sent.reshape(peers, halo // 2, f_in), NODES, split_axis=0, concat_axis=0, tiled=True
     )
@@ -391,7 +411,8 @@
             pltpu.VMEM((local + 2 * rows_half, f_in), f32),
             pltpu.VMEM((edges, f_in), f32),
             pltpu.VMEM((local, f_in), i32),
-            pltpu.VMEM((peers * halo, f_in), i32),
+            pltpu.VMEM((2 * halo, f_in), i32),
+            pltpu.VMEM((2 * halo, f_in), i32),
         ],
         features,
         got.reshape(rows_half, f_in),
@@ -412,6 +433,7 @@
         ),
         [
             pltpu.VMEM((local + peers * halo, f_in), f32),
+            pltpu.VMEM((TILE + edges // tiles, f_in), f32),
             pltpu.VMEM((TILE + edges // tiles, f_in), f32),
             pltpu.VMEM((3 * f_in, width), bf16),
             pltpu.VMEM((width, width), bf16),

time: 221 us -> 218 us (0.986)
  blocking collectives: 93.5 us -> 159 us
  waiting for transfers between devices: 71.1 us -> 12.6 us
  starting transfers between devices: 19 us -> 13.6 us
  local copies, waits for them, and re-layouts: 4.87 us -> 1.88 us
    all_to_all x0 -> x1, blocking collectives: none -> 67.3 us  [per_device(): lax.all_to_all(words.reshape(peers, 40, f_in), NODES, split_axis=0, conca...]
    all_to_all x1 -> x0, waiting for transfers between devices: 57.6 us -> none  [per_device(): lax.all_to_all(words.reshape(peers, 40, f_in), NODES, split_axis=0, conca...]
    all_to_all x1 -> x0, starting transfers between devices: 7.12 us -> none  [per_device(): lax.all_to_all(words.reshape(peers, 40, f_in), NODES, split_axis=0, conca...]
    unnamed x23 -> x17, local copies, waits for them, and re-layouts: 4.78 us -> 1.79 us
  transfers between devices with their start and end apart: 7 -> 6, of which waited for: 5 -> 3; matrix products, arithmetic and copies ran while one was open for 0% -> 0% of each run, Pallas kernels for 0% -> 2%
where the time goes in v3:
time: 218 us; the launch traced here: 217 us
  blocking collectives  159 us (73%)
  Pallas kernels  27.8 us (13%)
  starting transfers between devices  13.6 us (6%)
  waiting for transfers between devices  12.6 us (6%)
    all_to_all x1, blocking collectives, per_device(): lax.all_to_all(words.reshape(peers, 40, f_in), NODES, split_axis=0, conca...  67.3 us
    all_to_all x1, blocking collectives, per_device(): lax.all_to_all(sent.reshape(peers, halo // 2, f_in), NODES, split_axis=0,...  41.7 us
    pallas_call x8, Pallas kernels, call(): pl.pallas_call(body, out_shape=outs, in_specs=[SMEM] * len(scalars) + [VM...  27.8 us
    all_to_all x2, blocking collectives, sum_over_nodes(): lax.all_to_all(blocks, PLANE, split_axis=0, concat_axis=0, tiled=True)  25.1 us
    all_to_all x1, blocking collectives, per_device(): losses = lax.all_to_all(loss, PLANE_FEAT, 0, 0, tiled=True)  13.7 us
    all_to_all x1, blocking collectives, sum_over_nodes(): lax.all_to_all(copies, 'nodes_1', split_axis=0, concat_axis=0, tiled=True)  11.3 us
    ppermute x5, starting transfers between devices, partner(): return lax.ppermute(value, 'feat', swap)  10.2 us
    all_to_all x1, waiting for transfers between devices, sum_over_nodes(): lax.all_to_all(copies, 'nodes_1', split_axis=0, concat_axis=0, tiled=True)  9.6 us
  transfers between devices with their start and end apart: 6, of which 3 were waited for; matrix products, arithmetic and copies ran while one was open for 0% of the time, Pallas kernels for 2%

profile of v3, /device:TPU:1, one launch (start us, length us, event | category | flops | bytes accessed | tf_op | source)
XLA Modules:
  0.0 217.3 jit_solution(18092059039757533255)
XLA Ops:
  0.6 0.0 copy-start.1
  0.7 3.3 %collective-permute-start.1 = (bf16[512,256]{1,0:T(8,128)(2,1)}, bf16[512,256]{1,0:T(8,128)(2,1)S(1)}, u32[]{:S(2)}, u32[]{:S(2)}) collective-permute-start(bf16[512,256]{1,0:T(8,128)(2,1)} %w2_own.1), channel_id=1, source_target_pairs={{0,1},{1,0},{2,3},{3,2},{4,5},{5,4},{6,7},{7,6},{8,9},{9,8},{10,11... | collective-permute-start | bytes 786440 | tf_op jit(solution)/shard_map/ppermute | solution.py:368
  4.0 0.1 collective-permute-start
  4.1 0.4 collective-permute-start.2
  4.5 0.8 copy.12
  5.3 0.1 reshape.41.outbound
  5.4 0.9 copy-done
  6.3 3.6 %send_features.1 = bf16[4096,128]{1,0:T(8,128)(2,1)S(1)} custom-call(s32[1]{0:T(128)} %bitcast.core, s32[8192]{0:T(1024)S(1)} %reshape.41.outbound, bf16[512,128]{1,0:T(8,128)(2,1)S(1)} %copy-done), custom_call_target="tpu_custom_call" | custom-call | tf_op jit(solution)/shard_map/send_features/pallas_call | solution.py:26
  9.9 0.0 collective-permute-done.2.b_other
  9.9 41.7 %all_to_all.35 = bf16[128,32,128]{2,1,0:T(8,128)(2,1)S(1)} all-to-all(bf16[128,32,128]{2,1,0:T(8,128)(2,1)S(1)} %bitcast.11), channel_id=1, replica_groups=mesh['nodes_0'=4,'nodes_1'=8,'nodes_2'=4,'feat'=2] {'nodes_0','nodes_1',..., dimensions={0} | all-to-all | bytes 2097152 | tf_op jit(solution)/shard_map/all_to_all | solution.py:398
  51.6 2.8 %collective-permute-start.3 = (bf16[128,32,128]{2,1,0:T(8,128)(2,1)S(1)}, bf16[128,32,128]{2,1,0:T(8,128)(2,1)S(1)}, u32[]{:S(2)}, u32[]{:S(2)}) collective-permute-start(bf16[128,32,128]{2,1,0:T(8,128)(2,1)S(1)} %all_to_all.35), channel_id=1, source_target_pairs={{0,1},{1,0},{2,3},{3,2},{4,5},{5,4},{6,7},{7,6},{8,9},{9,8},{10,11... | collective-permute-start | bytes 3145736 | tf_op jit(solution)/shard_map/ppermute | solution.py:368
  55.1 0.1 fusion.6
  55.2 1.5 collective-permute-done.3
  56.7 9.9 %first_mix.1 = (f32[512,128]{1,0:T(8,128)S(1)}, s32[5120,128]{1,0:T(8,128)S(1)}) custom-call(s32[1]{0:T(128)S(6)} %copy.13.live_count, s32[4096]{0:T(1024)S(1)} %compare_select_fusion.1.sources, s32[8192]{0:T(1024)S(1)} %reshape.41.outbound, bf16[512,128]{1,0:T(8,128)(2,1)S(1)} %copy-done.1, bf16[4096,128]{1,0:T(8,128)(2,1)S(1)} %bitcast.10, ...), custom_call_target="tpu_custom_call" | custom-call | tf_op jit(solution)/shard_map/first_mix/pallas_call | solution.py:26
  66.6 0.0 copy-start.2
  66.6 0.0 copy-start.3
  66.7 0.0 copy-start.4
  66.7 67.3 %all_to_all.36 = s32[128,40,128]{2,1,0:T(8,128)S(1)} all-to-all(s32[128,40,128]{2,1,0:T(8,128)S(1)} %bitcast.12), channel_id=1, replica_groups=mesh['nodes_0'=4,'nodes_1'=8,'nodes_2'=4,'feat'=2] {'nodes_0','nodes_1',..., dimensions={0} | all-to-all | bytes 5242880 | tf_op jit(solution)/shard_map/all_to_all | solution.py:424
  134.0 11.5 %second_mix.1 = (f32[512,512]{1,0:T(8,128)S(1)}, f32[16,8,128]{2,1,0:T(8,128)S(1)}, f32[8,128]{1,0:T(8,128)S(1)}) custom-call(s32[1]{0:T(128)} %bitcast.core, s32[1]{0:T(128)S(6)} %copy.13.live_count, s32[4096]{0:T(1024)S(1)} %bitcast.15, s32[5120,128]{1,0:T(8,128)S(1)} %bitcast.9, f32[512,128]{1,0:T(8,128)S(1)} %get-tuple-element.18.mixed, ...), custom_call_target="tpu_custom_call" | custom-call | tf_op jit(solution)/shard_map/second_mix/pallas_call | solution.py:26
  145.5 11.6 %all_to_all.37.arrived = f32[16,8,128]{2,1,0:T(8,128)S(1)} all-to-all(f32[16,8,128]{2,1,0:T(8,128)S(1)} %get-tuple-element.22), channel_id=1, replica_groups=mesh['nodes_0'=4,'nodes_1'=8,'nodes_2'=4,'feat'=2] {'nodes_0','nodes_2'}, dimensions={0} | all-to-all | bytes 131072 | tf_op jit(solution)/shard_map/all_to_all | solution.py:371
  157.2 11.3 %all_to_all.38.sums = f32[8,8,128]{2,1,0:T(8,128)S(1)} all-to-all(f32[8,8,128]{2,1,0:T(8,128)S(1)} %add_sums.1), channel_id=1, replica_groups=mesh['nodes_0'=4,'nodes_1'=8,'nodes_2'=4,'feat'=2] {'nodes_1'}, dimensions={0} | all-to-all | bytes 65536 | tf_op jit(solution)/shard_map/all_to_all | solution.py:375
  168.4 0.2 normalize.1.own
  168.7 3.6 %collective-permute-start.4 = (bf16[512,512]{1,0:T(8,128)(2,1)S(1)}, bf16[512,512]{1,0:T(8,128)(2,1)S(1)}, u32[]{:S(2)}, u32[]{:S(2)}) collective-permute-start(bf16[512,512]{1,0:T(8,128)(2,1)S(1)} %normalize.1.own), channel_id=1, source_target_pairs={{0,1},{1,0},{2,3},{3,2},{4,5},{5,4},{6,7},{7,6},{8,9},{9,8},{10,11... | collective-permute-start | bytes 1572872 | tf_op jit(solution)/shard_map/ppermute | solution.py:368
  172.3 1.5 collective-permute-done.4.other
  173.8 1.1 correlate.1
  175.0 13.5 %all_to_all.39.arrived = f32[16,32,256]{2,1,0:T(8,128)S(1)} all-to-all(f32[16,32,256]{2,1,0:T(8,128)S(1)} %get-tuple-element.26), channel_id=1, replica_groups=mesh['nodes_0'=4,'nodes_1'=8,'nodes_2'=4,'feat'=2] {'nodes_0','nodes_2'}, dimensions={0} | all-to-all | bytes 1048576 | tf_op jit(solution)/shard_map/all_to_all | solution.py:371
  188.5 0.7 add_products.1
  189.3 3.4 %all-to-all-start.5 = ((f32[8,32,256]{2,1,0:T(8,128)}), f32[8,32,256]{2,1,0:T(8,128)S(1)}, u32[]{:S(2)}, u32[]{:S(2)}) async-start(f32[8,32,256]{2,1,0:T(8,128)} %add_products.1), calls=%async_computation.5 | async-start | bytes 524288 | tf_op jit(solution)/shard_map/all_to_all | solution.py:375
  192.7 9.6 %all-to-all-done.5.arrived = f32[8,32,256]{2,1,0:T(8,128)S(1)} async-done(((f32[8,32,256]{2,1,0:T(8,128)}), f32[8,32,256]{2,1,0:T(8,128)S(1)}, u32[]{:S(2)}, u32[]{:S(2)}) %all-to-all-start.5) | async-done | bytes 262176 | tf_op jit(solution)/shard_map/all_to_all | solution.py:375
  202.3 0.6 finish.1
  202.9 13.7 %all_to_all.40 = f32[32,1,128]{2,1,0:T(1,128)S(1)} all-to-all(f32[32,1,128]{2,1,0:T(1,128)S(1)} %get-tuple-element.28), channel_id=1, replica_groups=mesh['nodes_0'=4,'nodes_1'=8,'nodes_2'=4,'feat'=2] {'nodes_0','nodes_2',..., dimensions={0} | all-to-all | bytes 32768 | tf_op jit(solution)/shard_map/all_to_all | solution.py:484
  216.6 0.6 slice_reduce_fusion
  (16 shorter events, 0.1 us)
Async XLA Ops:
  0.6 56.0 %copy-start.1 = (bf16[512,128]{1,0:T(8,128)(2,1)S(1)}, bf16[512,128]{1,0:T(8,128)(2,1)}, u32[]{:S(2)}) copy-start(bf16[512,128]{1,0:T(8,128)(2,1)} %features.3) | copy-start | bytes 393220
  0.6 54.4 %copy-start.6 = (s32[2,4096]{1,0:T(2,128)S(1)}, s32[2,4096]{1,0:T(2,128)}, u32[]{:S(2)}) copy-start(s32[2,4096]{1,0:T(2,128)} %param.14) | copy-start | bytes 98308
  0.7 54.4 %copy-start.5 = (s32[2,4096]{1,0:T(2,128)S(1)}, s32[2,4096]{1,0:T(2,128)}, u32[]{:S(2)}) copy-start(s32[2,4096]{1,0:T(2,128)} %param.13) | copy-start | bytes 98308
  0.7 9.2 %collective-permute-start.1 = (bf16[512,256]{1,0:T(8,128)(2,1)}, bf16[512,256]{1,0:T(8,128)(2,1)S(1)}, u32[]{:S(2)}, u32[]{:S(2)}) collective-permute-start(bf16[512,256]{1,0:T(8,128)(2,1)} %w2_own.1), channel_id=1, source_target_pairs={{0,1},{1,0},{2,3},{3,2},{4,5},{5,4},{6,7},{7,6},{8,9},{9,8},{10,11... | collective-permute-start | bytes 786440 | tf_op jit(solution)/shard_map/ppermute | solution.py:368
  4.0 5.9 %collective-permute-start = (bf16[128,256]{1,0:T(8,128)(2,1)}, bf16[128,256]{1,0:T(8,128)(2,1)S(1)}, u32[]{:S(2)}, u32[]{:S(2)}) collective-permute-start(bf16[128,256]{1,0:T(8,128)(2,1)} %w1_own.1), channel_id=1, source_target_pairs={{0,1},{1,0},{2,3},{3,2},{4,5},{5,4},{6,7},{7,6},{8,9},{9,8},{10,11... | collective-permute-start | bytes 196616 | tf_op jit(solution)/shard_map/ppermute | solution.py:368
  4.1 5.8 %collective-permute-start.2 = (f32[1,256]{1,0:T(1,128)}, f32[1,256]{1,0:T(1,128)S(1)}, u32[]{:S(2)}, u32[]{:S(2)}) collective-permute-start(f32[1,256]{1,0:T(1,128)} %bitcast.16), channel_id=1, source_target_pairs={{0,1},{1,0},{2,3},{3,2},{4,5},{5,4},{6,7},{7,6},{8,9},{9,8},{10,11... | collective-permute-start | bytes 3080 | tf_op jit(solution)/shard_map/ppermute | solution.py:368
  5.4 0.9 copy-start
  6.3 48.8 %copy-start.7 = (s32[2,4096]{1,0:T(2,128)S(1)}, s32[2,4096]{1,0:T(2,128)}, u32[]{:S(2)}) copy-start(s32[2,4096]{1,0:T(2,128)} %param.12) | copy-start | bytes 98308
  51.6 5.1 %collective-permute-start.3 = (bf16[128,32,128]{2,1,0:T(8,128)(2,1)S(1)}, bf16[128,32,128]{2,1,0:T(8,128)(2,1)S(1)}, u32[]{:S(2)}, u32[]{:S(2)}) collective-permute-start(bf16[128,32,128]{2,1,0:T(8,128)(2,1)S(1)} %all_to_all.35), channel_id=1, source_target_pairs={{0,1},{1,0},{2,3},{3,2},{4,5},{5,4},{6,7},{7,6},{8,9},{9,8},{10,11... | collective-permute-start | bytes 3145736 | tf_op jit(solution)/shard_map/ppermute | solution.py:368
  66.6 67.4 %copy-start.2 = (bf16[512,256]{1,0:T(8,128)(2,1)S(1)}, bf16[512,256]{1,0:T(8,128)(2,1)}, u32[]{:S(2)}) copy-start(bf16[512,256]{1,0:T(8,128)(2,1)} %w2_own.1) | copy-start | bytes 786436
  66.6 67.3 %copy-start.3 = (bf16[128,256]{1,0:T(8,128)(2,1)S(1)}, bf16[128,256]{1,0:T(8,128)(2,1)}, u32[]{:S(2)}) copy-start(bf16[128,256]{1,0:T(8,128)(2,1)} %w1_own.1) | copy-start | bytes 196612
  66.7 67.3 %copy-start.4 = (f32[256]{0:T(256)S(1)}, f32[256]{0:T(256)}, u32[]{:S(2)}) copy-start(f32[256]{0:T(256)} %param.16) | copy-start | bytes 3076
  168.7 5.2 %collective-permute-start.4 = (bf16[512,512]{1,0:T(8,128)(2,1)S(1)}, bf16[512,512]{1,0:T(8,128)(2,1)S(1)}, u32[]{:S(2)}, u32[]{:S(2)}) collective-permute-start(bf16[512,512]{1,0:T(8,128)(2,1)S(1)} %normalize.1.own), channel_id=1, source_target_pairs={{0,1},{1,0},{2,3},{3,2},{4,5},{5,4},{6,7},{7,6},{8,9},{9,8},{10,11... | collective-permute-start | bytes 1572872 | tf_op jit(solution)/shard_map/ppermute | solution.py:368
  189.3 13.0 %all-to-all-start.5 = ((f32[8,32,256]{2,1,0:T(8,128)}), f32[8,32,256]{2,1,0:T(8,128)S(1)}, u32[]{:S(2)}, u32[]{:S(2)}) async-start(f32[8,32,256]{2,1,0:T(8,128)} %add_products.1), calls=%async_computation.5 | async-start | bytes 524288 | tf_op jit(solution)/shard_map/all_to_all | solution.py:375

commit v4 on v3

--- a/solution.py
+++ b/solution.py
@@ -14,9 +14,11 @@
 
 LANES = 128
 TILE = 128
-CODE_BITS = 19
+CODE_BITS = 18
 CODE_TOP = 2 ** (CODE_BITS - 1)
 SCALE_BIAS = 224.0
+COARSE = 5
+PACKED = 36
 
 VMEM = pl.BlockSpec(memory_space=pltpu.VMEM)
 SMEM = pl.BlockSpec(memory_space=pltpu.SMEM)
@@ -100,7 +102,7 @@
 ):
     local = features.shape[0]
     halo = own.shape[0]
-    table[0:local, :] = features[...].astype(jnp.float32)
+    table[0:local, :] = features[...]
 
     def widen(base):
         table[pl.ds(local + base, 256), :] = own[pl.ds(base, 256), :].astype(jnp.float32)
@@ -125,11 +127,9 @@
         code = jnp.clip(code, -CODE_TOP, CODE_TOP - 1).astype(jnp.int32)
         codes[rows, :] = (code & (2**CODE_BITS - 1)) | (step.astype(jnp.int32) << CODE_BITS)
 
-    group = lax.broadcasted_iota(jnp.int32, (8, LANES), 1) // 16
-
-    patch = lax.broadcasted_iota(jnp.int32, (8, LANES), 0)
-    count = jnp.where(patch == 0, live_count[0] & 255, live_count[0] >> 8) << 24
-    patched = (lax.broadcasted_iota(jnp.int32, (8, LANES), 1) == 1) & (patch < 2)
+    lane = lax.broadcasted_iota(jnp.int32, (8, LANES), 1)
+    row = lax.broadcasted_iota(jnp.int32, (8, LANES), 0)
+    counted = jnp.where((lane == COARSE - 1) & (row == 0), live_count[0], 0)
 
     def pick(block, side, coded):
         for slot in range(128):
@@ -137,20 +137,21 @@
             coded[slot : slot + 1, :] = codes[pl.ds(near[block * 256], 1), :]
 
     def pack(peer, first, coded):
-        to = pl.multiple_of(peer * 40, 8)
+        to = peer * PACKED
         octet = [coded[first + 8 * k : first + 8 * k + 8, :] for k in range(8)]
         for k in range(4):
-            low = (octet[k] >> 3) & 0xFFFF
-            words[pl.ds(to + 8 * k, 8), :] = low | ((octet[k + 4] >> 3) << 16)
-        rest = jnp.zeros((8, LANES), jnp.int32)
-        steps = jnp.zeros((8, LANES), jnp.int32)
+            low = (octet[k] >> 2) & 0xFFFF
+            words[pl.ds(to + 8 * k, 8), :] = low | ((octet[k + 4] >> 2) << 16)
+        fine = jnp.zeros((8, LANES), jnp.int32)
+        coarse = counted
         for k in range(8):
-            rest = rest | ((octet[k] & 7) << (3 * k))
-            steps = jnp.where(group == k, octet[k], steps)
-        rest = rest | jnp.where(patched, count, (steps >> CODE_BITS) << 24)
-        words[pl.ds(to + 32, 8), :] = rest
-
-    blocks = words.shape[0] // 160
+            fine = fine | ((octet[k] & 3) << (4 * k + 2 * (row // 4)))
+            scale = (octet[k] >> CODE_BITS) << (16 * (k % 2) + 8 * (row // 4))
+            coarse = coarse | jnp.where(lane == k // 2, scale, 0)
+        fine = jnp.where(lane < COARSE, coarse, fine)
+        words[pl.ds(to + 32, 4), :] = fine[0:4, :] | fine[4:8, :]
+
+    blocks = words.shape[0] // (4 * PACKED)
     pick(0, 0, coded_even)
 
     def both(block, _):
@@ -211,20 +212,27 @@
 
     table[0:local, :] = mixed[...]
 
+    lane = lax.broadcasted_iota(jnp.int32, (8, LANES), 1)
+    row = lax.broadcasted_iota(jnp.int32, (8, LANES), 0)
+
     def unpack(peer):
-        base = pl.multiple_of(peer * 40, 8)
+        base = peer * PACKED
         to = pl.multiple_of(local + peer * 64, 64)
         pairs = [words[pl.ds(base + 8 * k, 8), :] for k in range(4)]
-        rest = words[pl.ds(base + 32, 8), :]
-        step = (rest >> 24) & 255
-        scale = jnp.exp2((step.astype(jnp.float32) - SCALE_BIAS) * 0.125) * (1.0 / CODE_TOP)
+        rest = words[pl.ds(base + 28, 8), :]
+        rest = jnp.where(row < 4, pltpu.roll(rest, 4, 0), rest)
+        scales = []
+        for side in range(2):
+            step = (rest >> (16 * side + 8 * (row // 4))) & 255
+            scale = jnp.exp2((step.astype(jnp.float32) - SCALE_BIAS) * 0.125)
+            scales.append(scale * (1.0 / CODE_TOP))
+        fine = jnp.where(lane < COARSE, -0x55555556, rest)
         for k in range(8):
             high = (pairs[k] << 16) >> 16 if k < 4 else pairs[k - 4] >> 16
-            code = (high << 3) | ((rest >> (3 * k)) & 7)
-            table[pl.ds(to + 8 * k, 8), :] = (
-                code.astype(jnp.float32) * scale[:, 16 * k : 16 * k + 1]
-            )
-        return step
+            code = (high << 2) | ((fine >> (4 * k + 2 * (row // 4))) & 3)
+            scale = scales[k % 2][:, k // 2 : k // 2 + 1]
+            table[pl.ds(to + 8 * k, 8), :] = code.astype(jnp.float32) * scale
+        return rest
 
     def unpack_several(block, counts):
         for one in range(8):
@@ -232,12 +240,9 @@
         return counts
 
     counts = lax.fori_loop(
-        0, words.shape[0] // 320, unpack_several, jnp.zeros((8, LANES), jnp.int32)
-    )
-    sublane = lax.broadcasted_iota(jnp.int32, (8, LANES), 0)
-    weight = jnp.where(sublane == 0, 1.0, jnp.where(sublane == 1, 256.0, 0.0))
-    lane = lax.broadcasted_iota(jnp.int32, (8, LANES), 1)
-    counts = jnp.where(lane == 1, counts.astype(jnp.float32) * weight, 0.0)
+        0, words.shape[0] // (8 * PACKED), unpack_several, jnp.zeros((8, LANES), jnp.int32)
+    )
+    counts = jnp.where((lane == COARSE - 1) & (row == 0), counts, 0).astype(jnp.float32)
     counts = jnp.sum(jnp.sum(counts, 1, keepdims=True), 0, keepdims=True)
     node_total[...] = jnp.broadcast_to(counts, node_total.shape)
     edges = targets.shape[1]
@@ -384,10 +389,10 @@
     targets = jnp.where(kept == 1, targets, -1).reshape(tiles, edges // tiles)
 
     rows_half = peers * halo // 2
-    sent = call(
+    sent, wide = call(
         send_features,
-        shape((rows_half, f_in), bf16),
-        [pltpu.VMEM((local, f_in), f32), pltpu.VMEM((rows_half, f_in), f32)],
+        (shape((rows_half, f_in), bf16), shape((local, f_in), f32)),
+        [pltpu.VMEM((rows_half, f_in), f32)],
         features,
         scalars=(core, outbound),
         name="send_features",
@@ -406,7 +411,7 @@
     first_sources = jnp.where(sources < local, sources, remote + local)
     mixed, words = call(
         first_mix,
-        (shape((local, f_in), f32), shape((peers * 40, f_in), i32)),
+        (shape((local, f_in), f32), shape((peers * PACKED, f_in), i32)),
         [
             pltpu.VMEM((local + 2 * rows_half, f_in), f32),
             pltpu.VMEM((edges, f_in), f32),
@@ -414,7 +419,7 @@
             pltpu.VMEM((2 * halo, f_in), i32),
             pltpu.VMEM((2 * halo, f_in), i32),
         ],
-        features,
+        wide,
         got.reshape(rows_half, f_in),
         got_other.reshape(rows_half, f_in),
         targets,
@@ -422,7 +427,7 @@
         name="first_mix",
     )
     arrived = lax.all_to_all(
-        words.reshape(peers, 40, f_in), NODES, split_axis=0, concat_axis=0, tiled=True
+        words.reshape(peers * PACKED // 4, 4, f_in), NODES, split_axis=0, concat_axis=0, tiled=True
     )
     embedded, sums, node_total = call(
         second_mix,
@@ -438,7 +443,7 @@
             pltpu.VMEM((3 * f_in, width), bf16),
             pltpu.VMEM((width, width), bf16),
         ],
-        arrived.reshape(peers * 40, f_in),
+        arrived.reshape(peers * PACKED, f_in),
         mixed,
         targets,
         w_first,

time: 218 us -> 212 us (0.972)
  blocking collectives: 159 us -> 154 us
    all_to_all x1, blocking collectives: 67.3 us -> 61.8 us  [per_device(): lax.all_to_all(words.reshape(peers * PACKED // 4, 4, f_in), NODES, split_...]
where the time goes in v4:
time: 212 us
  blocking collectives  154 us (73%)
  Pallas kernels  28 us (13%)
  starting transfers between devices  13.6 us (6%)
  waiting for transfers between devices  12.6 us (6%)
    all_to_all x1, blocking collectives, per_device(): lax.all_to_all(words.reshape(peers * PACKED // 4, 4, f_in), NODES, split_...  61.8 us
    all_to_all x1, blocking collectives, per_device(): lax.all_to_all(sent.reshape(peers, halo // 2, f_in), NODES, split_axis=0,...  41.7 us
    pallas_call x8, Pallas kernels, call(): pl.pallas_call(body, out_shape=outs, in_specs=[SMEM] * len(scalars) + [VM...  28 us
    all_to_all x2, blocking collectives, sum_over_nodes(): lax.all_to_all(blocks, PLANE, split_axis=0, concat_axis=0, tiled=True)  25.2 us
    all_to_all x1, blocking collectives, per_device(): losses = lax.all_to_all(loss, PLANE_FEAT, 0, 0, tiled=True)  13.7 us
    all_to_all x1, blocking collectives, sum_over_nodes(): lax.all_to_all(copies, 'nodes_1', split_axis=0, concat_axis=0, tiled=True)  11.1 us
    ppermute x5, starting transfers between devices, partner(): return lax.ppermute(value, 'feat', swap)  10.2 us
    all_to_all x1, waiting for transfers between devices, sum_over_nodes(): lax.all_to_all(copies, 'nodes_1', split_axis=0, concat_axis=0, tiled=True)  9.61 us
  transfers between devices with their start and end apart: 6, of which 3 were waited for; matrix products, arithmetic and copies ran while one was open for 0% of the time, Pallas kernels for 2%

profile of v4, /device:TPU:1, one launch (start us, length us, event | category | flops | bytes accessed | tf_op | source)
XLA Modules:
  0.0 211.8 jit_solution(13704293049443189985)
XLA Ops:
  0.7 3.3 %collective-permute-start.1 = (bf16[512,256]{1,0:T(8,128)(2,1)}, bf16[512,256]{1,0:T(8,128)(2,1)S(1)}, u32[]{:S(2)}, u32[]{:S(2)}) collective-permute-start(bf16[512,256]{1,0:T(8,128)(2,1)} %w2_own.1), channel_id=1, source_target_pairs={{0,1},{1,0},{2,3},{3,2},{4,5},{5,4},{6,7},{7,6},{8,9},{9,8},{10,11... | collective-permute-start | bytes 786440 | tf_op jit(solution)/shard_map/ppermute | solution.py:373
  3.9 0.1 collective-permute-start
  4.1 0.4 collective-permute-start.2
  4.5 0.8 copy.12
  5.3 0.1 reshape.41.outbound
  5.4 0.9 copy-done.1
  6.3 3.6 %send_features.1 = (bf16[4096,128]{1,0:T(8,128)(2,1)S(1)}, f32[512,128]{1,0:T(8,128)S(1)}) custom-call(s32[1]{0:T(128)} %bitcast.core, s32[8192]{0:T(1024)S(1)} %reshape.41.outbound, bf16[512,128]{1,0:T(8,128)(2,1)S(1)} %copy-done.1), custom_call_target="tpu_custom_call" | custom-call | tf_op jit(solution)/shard_map/send_features/pallas_call | solution.py:28
  9.9 0.0 collective-permute-done.2.b_other
  9.9 0.0 collective-permute-done.w1_other
  9.9 41.7 %all_to_all.35 = bf16[128,32,128]{2,1,0:T(8,128)(2,1)S(1)} all-to-all(bf16[128,32,128]{2,1,0:T(8,128)(2,1)S(1)} %bitcast.12), channel_id=1, replica_groups=mesh['nodes_0'=4,'nodes_1'=8,'nodes_2'=4,'feat'=2] {'nodes_0','nodes_1',..., dimensions={0} | all-to-all | bytes 2097152 | tf_op jit(solution)/shard_map/all_to_all | solution.py:403
  51.6 2.8 %collective-permute-start.3 = (bf16[128,32,128]{2,1,0:T(8,128)(2,1)S(1)}, bf16[128,32,128]{2,1,0:T(8,128)(2,1)S(1)}, u32[]{:S(2)}, u32[]{:S(2)}) collective-permute-start(bf16[128,32,128]{2,1,0:T(8,128)(2,1)S(1)} %all_to_all.35), channel_id=1, source_target_pairs={{0,1},{1,0},{2,3},{3,2},{4,5},{5,4},{6,7},{7,6},{8,9},{9,8},{10,11... | collective-permute-start | bytes 3145736 | tf_op jit(solution)/shard_map/ppermute | solution.py:373
  55.1 0.1 fusion.6
  55.2 1.5 collective-permute-done.3
  56.7 10.1 %first_mix.1 = (f32[512,128]{1,0:T(8,128)S(1)}, s32[4608,128]{1,0:T(8,128)S(1)}) custom-call(s32[1]{0:T(128)S(6)} %copy.13.live_count, s32[4096]{0:T(1024)S(1)} %compare_select_fusion.1.sources, s32[8192]{0:T(1024)S(1)} %reshape.41.outbound, f32[512,128]{1,0:T(8,128)S(1)} %get-tuple-element.18.features, bf16[4096,128]{1,0:T(8,128)(2,1)S(1)} %bitcast.10, ...), custom_call_target="tpu_custom_call" | custom-call | tf_op jit(solution)/shard_map/first_mix/pallas_call | solution.py:28
  66.8 0.0 copy-start
  66.8 0.0 copy-start.2
  66.8 0.0 copy-start.3
  66.8 61.8 %all_to_all.36 = s32[1152,4,128]{2,1,0:T(4,128)S(1)} all-to-all(s32[1152,4,128]{2,1,0:T(4,128)S(1)} %bitcast.11), channel_id=1, replica_groups=mesh['nodes_0'=4,'nodes_1'=8,'nodes_2'=4,'feat'=2] {'nodes_0','nodes_1',..., dimensions={0} | all-to-all | bytes 4718592 | tf_op jit(solution)/shard_map/all_to_all | solution.py:429
  128.6 11.5 %second_mix.1 = (f32[512,512]{1,0:T(8,128)S(1)}, f32[16,8,128]{2,1,0:T(8,128)S(1)}, f32[8,128]{1,0:T(8,128)S(1)}) custom-call(s32[1]{0:T(128)} %bitcast.core, s32[1]{0:T(128)S(6)} %copy.13.live_count, s32[4096]{0:T(1024)S(1)} %bitcast.15, s32[4608,128]{1,0:T(8,128)S(1)} %bitcast.9, f32[512,128]{1,0:T(8,128)S(1)} %get-tuple-element.22.mixed, ...), custom_call_target="tpu_custom_call" | custom-call | tf_op jit(solution)/shard_map/second_mix/pallas_call | solution.py:28
  140.2 11.6 %all_to_all.37.arrived = f32[16,8,128]{2,1,0:T(8,128)S(1)} all-to-all(f32[16,8,128]{2,1,0:T(8,128)S(1)} %get-tuple-element.26), channel_id=1, replica_groups=mesh['nodes_0'=4,'nodes_1'=8,'nodes_2'=4,'feat'=2] {'nodes_0','nodes_2'}, dimensions={0} | all-to-all | bytes 131072 | tf_op jit(solution)/shard_map/all_to_all | solution.py:376
  151.8 11.1 %all_to_all.38.sums = f32[8,8,128]{2,1,0:T(8,128)S(1)} all-to-all(f32[8,8,128]{2,1,0:T(8,128)S(1)} %add_sums.1), channel_id=1, replica_groups=mesh['nodes_0'=4,'nodes_1'=8,'nodes_2'=4,'feat'=2] {'nodes_1'}, dimensions={0} | all-to-all | bytes 65536 | tf_op jit(solution)/shard_map/all_to_all | solution.py:380
  162.9 0.2 normalize.1.own
  163.2 3.6 %collective-permute-start.4 = (bf16[512,512]{1,0:T(8,128)(2,1)S(1)}, bf16[512,512]{1,0:T(8,128)(2,1)S(1)}, u32[]{:S(2)}, u32[]{:S(2)}) collective-permute-start(bf16[512,512]{1,0:T(8,128)(2,1)S(1)} %normalize.1.own), channel_id=1, source_target_pairs={{0,1},{1,0},{2,3},{3,2},{4,5},{5,4},{6,7},{7,6},{8,9},{9,8},{10,11... | collective-permute-start | bytes 1572872 | tf_op jit(solution)/shard_map/ppermute | solution.py:373
  166.8 1.5 collective-permute-done.4.other
  168.3 1.1 correlate.1
  169.5 13.5 %all_to_all.39.arrived = f32[16,32,256]{2,1,0:T(8,128)S(1)} all-to-all(f32[16,32,256]{2,1,0:T(8,128)S(1)} %get-tuple-element.30), channel_id=1, replica_groups=mesh['nodes_0'=4,'nodes_1'=8,'nodes_2'=4,'feat'=2] {'nodes_0','nodes_2'}, dimensions={0} | all-to-all | bytes 1048576 | tf_op jit(solution)/shard_map/all_to_all | solution.py:376
  183.0 0.7 add_products.1
  183.8 3.4 %all-to-all-start.5 = ((f32[8,32,256]{2,1,0:T(8,128)}), f32[8,32,256]{2,1,0:T(8,128)S(1)}, u32[]{:S(2)}, u32[]{:S(2)}) async-start(f32[8,32,256]{2,1,0:T(8,128)} %add_products.1), calls=%async_computation.5 | async-start | bytes 524288 | tf_op jit(solution)/shard_map/all_to_all | solution.py:380
  187.2 9.6 %all-to-all-done.5.arrived = f32[8,32,256]{2,1,0:T(8,128)S(1)} async-done(((f32[8,32,256]{2,1,0:T(8,128)}), f32[8,32,256]{2,1,0:T(8,128)S(1)}, u32[]{:S(2)}, u32[]{:S(2)}) %all-to-all-start.5) | async-done | bytes 262176 | tf_op jit(solution)/shard_map/all_to_all | solution.py:380
  196.8 0.6 finish.1
  197.5 13.7 %all_to_all.40 = f32[32,1,128]{2,1,0:T(1,128)S(1)} all-to-all(f32[32,1,128]{2,1,0:T(1,128)S(1)} %get-tuple-element.32), channel_id=1, replica_groups=mesh['nodes_0'=4,'nodes_1'=8,'nodes_2'=4,'feat'=2] {'nodes_0','nodes_2',..., dimensions={0} | all-to-all | bytes 32768 | tf_op jit(solution)/shard_map/all_to_all | solution.py:489
  211.1 0.6 slice_reduce_fusion
  (14 shorter events, 0.1 us)
Async XLA Ops:
  0.6 54.4 %copy-start.5 = (s32[2,4096]{1,0:T(2,128)S(1)}, s32[2,4096]{1,0:T(2,128)}, u32[]{:S(2)}) copy-start(s32[2,4096]{1,0:T(2,128)} %param.14) | copy-start | bytes 98308
  0.6 54.4 %copy-start.4 = (s32[2,4096]{1,0:T(2,128)S(1)}, s32[2,4096]{1,0:T(2,128)}, u32[]{:S(2)}) copy-start(s32[2,4096]{1,0:T(2,128)} %param.13) | copy-start | bytes 98308
  0.7 54.4 %copy-start.6 = (s32[2,4096]{1,0:T(2,128)S(1)}, s32[2,4096]{1,0:T(2,128)}, u32[]{:S(2)}) copy-start(s32[2,4096]{1,0:T(2,128)} %param.12) | copy-start | bytes 98308
  0.7 9.3 %collective-permute-start.1 = (bf16[512,256]{1,0:T(8,128)(2,1)}, bf16[512,256]{1,0:T(8,128)(2,1)S(1)}, u32[]{:S(2)}, u32[]{:S(2)}) collective-permute-start(bf16[512,256]{1,0:T(8,128)(2,1)} %w2_own.1), channel_id=1, source_target_pairs={{0,1},{1,0},{2,3},{3,2},{4,5},{5,4},{6,7},{7,6},{8,9},{9,8},{10,11... | collective-permute-start | bytes 786440 | tf_op jit(solution)/shard_map/ppermute | solution.py:373
  3.9 6.0 %collective-permute-start = (bf16[128,256]{1,0:T(8,128)(2,1)}, bf16[128,256]{1,0:T(8,128)(2,1)S(1)}, u32[]{:S(2)}, u32[]{:S(2)}) collective-permute-start(bf16[128,256]{1,0:T(8,128)(2,1)} %w1_own.1), channel_id=1, source_target_pairs={{0,1},{1,0},{2,3},{3,2},{4,5},{5,4},{6,7},{7,6},{8,9},{9,8},{10,11... | collective-permute-start | bytes 196616 | tf_op jit(solution)/shard_map/ppermute | solution.py:373
  4.1 5.8 %collective-permute-start.2 = (f32[1,256]{1,0:T(1,128)}, f32[1,256]{1,0:T(1,128)S(1)}, u32[]{:S(2)}, u32[]{:S(2)}) collective-permute-start(f32[1,256]{1,0:T(1,128)} %bitcast.16), channel_id=1, source_target_pairs={{0,1},{1,0},{2,3},{3,2},{4,5},{5,4},{6,7},{7,6},{8,9},{9,8},{10,11... | collective-permute-start | bytes 3080 | tf_op jit(solution)/shard_map/ppermute | solution.py:373
  5.4 0.9 copy-start.1
  51.6 5.1 %collective-permute-start.3 = (bf16[128,32,128]{2,1,0:T(8,128)(2,1)S(1)}, bf16[128,32,128]{2,1,0:T(8,128)(2,1)S(1)}, u32[]{:S(2)}, u32[]{:S(2)}) collective-permute-start(bf16[128,32,128]{2,1,0:T(8,128)(2,1)S(1)} %all_to_all.35), channel_id=1, source_target_pairs={{0,1},{1,0},{2,3},{3,2},{4,5},{5,4},{6,7},{7,6},{8,9},{9,8},{10,11... | collective-permute-start | bytes 3145736 | tf_op jit(solution)/shard_map/ppermute | solution.py:373
  66.8 61.9 %copy-start = (bf16[512,256]{1,0:T(8,128)(2,1)S(1)}, bf16[512,256]{1,0:T(8,128)(2,1)}, u32[]{:S(2)}) copy-start(bf16[512,256]{1,0:T(8,128)(2,1)} %w2_own.1) | copy-start | bytes 786436
  66.8 61.9 %copy-start.2 = (bf16[128,256]{1,0:T(8,128)(2,1)S(1)}, bf16[128,256]{1,0:T(8,128)(2,1)}, u32[]{:S(2)}) copy-start(bf16[128,256]{1,0:T(8,128)(2,1)} %w1_own.1) | copy-start | bytes 196612
  66.8 61.8 %copy-start.3 = (f32[256]{0:T(256)S(1)}, f32[256]{0:T(256)}, u32[]{:S(2)}) copy-start(f32[256]{0:T(256)} %param.16) | copy-start | bytes 3076
  163.2 5.2 %collective-permute-start.4 = (bf16[512,512]{1,0:T(8,128)(2,1)S(1)}, bf16[512,512]{1,0:T(8,128)(2,1)S(1)}, u32[]{:S(2)}, u32[]{:S(2)}) collective-permute-start(bf16[512,512]{1,0:T(8,128)(2,1)S(1)} %normalize.1.own), channel_id=1, source_target_pairs={{0,1},{1,0},{2,3},{3,2},{4,5},{5,4},{6,7},{7,6},{8,9},{9,8},{10,11... | collective-permute-start | bytes 1572872 | tf_op jit(solution)/shard_map/ppermute | solution.py:373
  183.8 13.0 %all-to-all-start.5 = ((f32[8,32,256]{2,1,0:T(8,128)}), f32[8,32,256]{2,1,0:T(8,128)S(1)}, u32[]{:S(2)}, u32[]{:S(2)}) async-start(f32[8,32,256]{2,1,0:T(8,128)} %add_products.1), calls=%async_computation.5 | async-start | bytes 524288 | tf_op jit(solution)/shard_map/all_to_all | solution.py:380

commit v5 on v4

--- a/solution.py
+++ b/solution.py
@@ -11,6 +11,7 @@
 NODES = ("nodes_0", "nodes_1", "nodes_2")
 PLANE = ("nodes_0", "nodes_2")
 PLANE_FEAT = ("nodes_0", "nodes_2", "feat")
+NODES_FEAT = ("nodes_0", "nodes_1", "nodes_2", "feat")
 
 LANES = 128
 TILE = 128
@@ -36,17 +37,6 @@
     )(*scalars, *operands)
 
 
-def pick_rows(index, first_index, table, rows, first_row, count, unroll):
-    def step(block, _):
-        base = pl.multiple_of(block * unroll, unroll)
-        for lane in range(unroll):
-            source = index.at[pl.ds(lane, index.shape[0] - unroll)][first_index + base]
-            rows[pl.ds(first_row + base + lane, 1), :] = table[pl.ds(source, 1), :]
-        return 0
-
-    lax.fori_loop(0, count // unroll, step, 0)
-
-
 def in_chunks(total, size, body):
     def step(block, _):
         body(pl.multiple_of(block * size, size))
@@ -62,18 +52,24 @@
     return table.astype(jnp.bfloat16), jnp.sum(table, 1, keepdims=True)
 
 
+def place_of(core, peer, peers):
+    return jnp.where(core[0] == 0, peer, peers - 1 - peer)
+
+
 def send_features(core, outbound, features, out, table, rows):
     table[...] = features[...].astype(jnp.float32)
     half = out.shape[0] // LANES
     first = core[0] * half
 
     def step(block, _):
-        base = pl.multiple_of(block * 4 * half, 4 * half)
+        place = place_of(core, block, out.shape[0] // (4 * half))
+        base = pl.multiple_of(place * 4 * half, 4 * half)
         for peer in range(4):
+            to = base + jnp.where(core[0] == 0, peer, 3 - peer) * half
             for slot in range(half):
                 near = outbound.at[pl.ds(peer * 2 * half + slot, outbound.shape[0] - 8 * half)]
                 source = near[block * (8 * half) + first]
-                rows[pl.ds(base + peer * half + slot, 1), :] = table[pl.ds(source, 1), :]
+                rows[pl.ds(to + slot, 1), :] = table[pl.ds(source, 1), :]
         return 0
 
     lax.fori_loop(0, out.shape[0] // (4 * half), step, 0)
@@ -85,6 +81,7 @@
 
 
 def first_mix(
+    core,
     live_count,
     sources,
     outbound,
@@ -95,7 +92,8 @@
     mixed,
     words,
     table,
-    picked,
+    picked_even,
+    picked_odd,
     codes,
     coded_even,
     coded_odd,
@@ -110,13 +108,20 @@
 
     in_chunks(halo, 256, widen)
     edges = targets.shape[1]
-    pick_rows(sources, 0, table, picked, 0, edges * (local // TILE), 128)
+
+    def pick(tile, picked):
+        for edge in range(edges):
+            source = sources[tile * edges + edge]
+            picked[edge : edge + 1, :] = table[pl.ds(source, 1), :]
+
+    pick(0, picked_even)
     for tile in range(local // TILE):
+        picked, later = (picked_even, picked_odd) if tile % 2 == 0 else (picked_odd, picked_even)
+        if tile + 1 < local // TILE:
+            pick(tile + 1, later)
         onehot, degree = edge_table(targets, tile)
         summed = jnp.dot(
-            onehot,
-            picked[tile * edges : (tile + 1) * edges, :].astype(jnp.bfloat16),
-            preferred_element_type=jnp.float32,
+            onehot, picked[...].astype(jnp.bfloat16), preferred_element_type=jnp.float32
         )
         rows = slice(tile * TILE, (tile + 1) * TILE)
         mix = (table[rows, :] + summed) / (1.0 + degree)
@@ -131,13 +136,13 @@
     row = lax.broadcasted_iota(jnp.int32, (8, LANES), 0)
     counted = jnp.where((lane == COARSE - 1) & (row == 0), live_count[0], 0)
 
-    def pick(block, side, coded):
+    def pick_slots(block, side, coded):
         for slot in range(128):
             near = outbound.at[pl.ds(side * 128 + slot, outbound.shape[0] - 255)]
             coded[slot : slot + 1, :] = codes[pl.ds(near[block * 256], 1), :]
 
     def pack(peer, first, coded):
-        to = peer * PACKED
+        to = place_of(core, peer, words.shape[0] // PACKED) * PACKED
         octet = [coded[first + 8 * k : first + 8 * k + 8, :] for k in range(8)]
         for k in range(4):
             low = (octet[k] >> 2) & 0xFFFF
@@ -152,13 +157,13 @@
         words[pl.ds(to + 32, 4), :] = fine[0:4, :] | fine[4:8, :]
 
     blocks = words.shape[0] // (4 * PACKED)
-    pick(0, 0, coded_even)
+    pick_slots(0, 0, coded_even)
 
     def both(block, _):
-        pick(block, 1, coded_odd)
+        pick_slots(block, 1, coded_odd)
         pack(block * 4, 0, coded_even)
         pack(block * 4 + 1, 64, coded_even)
-        pick(jnp.minimum(block + 1, blocks - 1), 0, coded_even)
+        pick_slots(jnp.minimum(block + 1, blocks - 1), 0, coded_even)
         pack(block * 4 + 2, 0, coded_odd)
         pack(block * 4 + 3, 64, coded_odd)
         return 0
@@ -217,7 +222,8 @@
 
     def unpack(peer):
         base = peer * PACKED
-        to = pl.multiple_of(local + peer * 64, 64)
+        to = place_of(core, peer, words.shape[0] // PACKED) * 64
+        to = pl.multiple_of(local + to, 64)
         pairs = [words[pl.ds(base + 8 * k, 8), :] for k in range(4)]
         rest = words[pl.ds(base + 28, 8), :]
         rest = jnp.where(row < 4, pltpu.roll(rest, 4, 0), rest)
@@ -289,6 +295,42 @@
         out[peer] = total
 
 
+def put_products(out, place, values):
+    sides = [[values[8 * m : 8 * m + 8, side : side + LANES] for side in (0, LANES)] for m in range(4)]
+    top = jnp.zeros((8, LANES), jnp.float32)
+    for pair in sides:
+        for side in pair:
+            top = jnp.maximum(top, jnp.abs(side))
+    top = jnp.maximum(jnp.max(top, 0, keepdims=True), 1e-30)
+    step = jnp.floor(8.0 * jnp.log2(top)) + 2.0
+    scale = jnp.exp2(step * -0.125) * 32767.0
+    first = place * PACKED
+    for m, pair in enumerate(sides):
+        low, high = (jnp.round(side * scale).astype(jnp.int32) for side in pair)
+        out[first + 8 * m : first + 8 * m + 8, :] = (low & 0xFFFF) | (high << 16)
+    out[first + 32 : first + 36, :] = jnp.broadcast_to(step.astype(jnp.int32), (4, LANES))
+
+
+def sum_products(arrived):
+    total = [[0.0, 0.0] for _ in range(4)]
+    for place in range(arrived.shape[0] // PACKED):
+        first = place * PACKED
+        step = arrived[first + 32 : first + 33, :].astype(jnp.float32)
+        scale = jnp.exp2(step * 0.125) * (1.0 / 32767.0)
+        for m in range(4):
+            word = arrived[first + 8 * m : first + 8 * m + 8, :]
+            total[m][0] = total[m][0] + ((word << 16) >> 16).astype(jnp.float32) * scale
+            total[m][1] = total[m][1] + (word >> 16).astype(jnp.float32) * scale
+    return jnp.concatenate([jnp.concatenate(pair, 1) for pair in total], 0)
+
+
+def add_products(arrived, out):
+    total = sum_products(arrived)
+    put_products(out, 0, total)
+    for place in range(1, out.shape[0] // PACKED):
+        out[place * PACKED : (place + 1) * PACKED, :] = out[0:PACKED, :]
+
+
 def normalize(live_count, sums, node_total, embedded, out):
     total = node_total[...]
     scaled = jnp.sum(sums[...], 0) / total
@@ -305,18 +347,17 @@
 def correlate(core, own, other, normed, out):
     half = normed.shape[2]
     width = 2 * half
-    groups, depth, wide = out.shape[0], out.shape[1] // 4, 4
+    groups, depth, wide = out.shape[0] // PACKED, 8, 4
     contract = (((0,), (0,)), ((), ()))
 
     def give(left, right):
         product = lax.dot_general(left, right, contract, preferred_element_type=jnp.float32)
         for group in range(groups):
-            for near in range(0, depth, 2):
-                rows = []
-                for n1 in (near, near + 1):
-                    first = ((group // wide) * depth * wide + n1 * wide + group % wide) * 4
-                    rows.append(product[first : first + 4, :])
-                out[group, near * 4 : near * 4 + 8, :] = jnp.concatenate(rows, 0)
+            rows = []
+            for n1 in range(depth):
+                first = ((group // wide) * depth * wide + n1 * wide + group % wide) * 4
+                rows.append(product[first : first + 4, :])
+            put_products(out, group, jnp.concatenate(rows, 0))
 
     @pl.when(core[0] == 0)
     def _():
@@ -335,10 +376,7 @@
     half = correlation.shape[1]
     share, depth, wide = 4, 8, 4
     n0, n1, n2 = node[0] // (depth * wide), (node[0] // wide) % depth, node[0] % wide
-    value = arrived[0]
-    for peer in range(1, arrived.shape[0]):
-        value = value + arrived[peer]
-    value = value / node_total[0:1, 0:1]
+    value = sum_products(arrived) / node_total[0:1, 0:1]
     place = lax.broadcasted_iota(jnp.int32, value.shape, 0)
     row = ((n0 * depth + place // share) * wide + n2) * share + place % share
     column = lax.broadcasted_iota(jnp.int32, value.shape, 1) + core[0] * half
@@ -372,10 +410,23 @@
     def partner(value):
         return lax.ppermute(value, "feat", swap)
 
-    def sum_over_nodes(blocks, name):
+    first_cores = [2 * peer for peer in range(peers)]
+    second_cores = [2 * peer + 1 for peer in reversed(range(peers))]
+
+    def over_nodes(blocks):
+        return lax.all_to_all(
+            blocks,
+            NODES_FEAT,
+            split_axis=0,
+            concat_axis=0,
+            axis_index_groups=[first_cores, second_cores],
+            tiled=True,
+        )
+
+    def sum_over_nodes(blocks):
         blocks = lax.all_to_all(blocks, PLANE, split_axis=0, concat_axis=0, tiled=True)
         copies = call(
-            add_and_copy, shape((depth, *blocks.shape[1:]), f32), [], blocks, name=name
+            add_and_copy, shape((depth, *blocks.shape[1:]), f32), [], blocks, name="add_sums"
         )
         return lax.all_to_all(copies, "nodes_1", split_axis=0, concat_axis=0, tiled=True)
 
@@ -400,21 +451,21 @@
     sent, w1_other, w2_other, bias_other = lax.optimization_barrier(
         (sent, w1_other, w2_other, bias_other)
     )
-    got = lax.all_to_all(
-        sent.reshape(peers, halo // 2, f_in), NODES, split_axis=0, concat_axis=0, tiled=True
-    )
+    got = over_nodes(sent.reshape(peers, halo // 2, f_in))
     got_other = partner(got)
     remote = sources - local
     slot_half = (remote % halo) // (halo // 2)
     from_other = (slot_half != core_index).astype(i32)
-    remote = (remote // halo) * (halo // 2) + remote % (halo // 2) + from_other * rows_half
+    sender = jnp.where(slot_half == 1, peers - 1 - remote // halo, remote // halo)
+    remote = sender * (halo // 2) + remote % (halo // 2) + from_other * rows_half
     first_sources = jnp.where(sources < local, sources, remote + local)
     mixed, words = call(
         first_mix,
         (shape((local, f_in), f32), shape((peers * PACKED, f_in), i32)),
         [
             pltpu.VMEM((local + 2 * rows_half, f_in), f32),
-            pltpu.VMEM((edges, f_in), f32),
+            pltpu.VMEM((edges // tiles, f_in), f32),
+            pltpu.VMEM((edges // tiles, f_in), f32),
             pltpu.VMEM((local, f_in), i32),
             pltpu.VMEM((2 * halo, f_in), i32),
             pltpu.VMEM((2 * halo, f_in), i32),
@@ -423,12 +474,10 @@
         got.reshape(rows_half, f_in),
         got_other.reshape(rows_half, f_in),
         targets,
-        scalars=(row_counts, first_sources, outbound),
+        scalars=(core, row_counts, first_sources, outbound),
         name="first_mix",
     )
-    arrived = lax.all_to_all(
-        words.reshape(peers * PACKED // 4, 4, f_in), NODES, split_axis=0, concat_axis=0, tiled=True
-    )
+    arrived = over_nodes(words.reshape(peers * PACKED // 4, 4, f_in))
     embedded, sums, node_total = call(
         second_mix,
         (
@@ -455,7 +504,7 @@
         scalars=(core, row_counts, sources),
         name="second_mix",
     )
-    sums = sum_over_nodes(sums, "add_sums")
+    sums = sum_over_nodes(sums)
     own = call(
         normalize,
         shape((local, width), bf16),
@@ -468,14 +517,27 @@
     )
     normed, partial = call(
         correlate,
-        (shape((2, local, half), bf16), shape((planes, width // planes, half), f32)),
+        (shape((2, local, half), bf16), shape((planes * PACKED, LANES), i32)),
         [],
         own,
         partner(own),
         scalars=(core,),
         name="correlate",
     )
-    partial = sum_over_nodes(partial, "add_products")
+    partial = lax.all_to_all(
+        partial.reshape(planes * PACKED // 4, 4, LANES), PLANE, split_axis=0, concat_axis=0, tiled=True
+    )
+    partial = call(
+        add_products,
+        shape((depth * PACKED, LANES), i32),
+        [],
+        partial.reshape(planes * PACKED, LANES),
+        name="add_products",
+    )
+    partial = lax.all_to_all(
+        partial.reshape(depth * PACKED // 4, 4, LANES), "nodes_1", split_axis=0, concat_axis=0, tiled=True
+    )
+    partial = partial.reshape(depth * PACKED, LANES)
     devices = lax.axis_size(PLANE_FEAT)
     correlation, loss = call(
         finish,

time: 212 us -> 207 us (0.976)
  blocking collectives: 154 us -> 149 us
    all_to_all x2 -> x1, blocking collectives: 25.2 us -> 12.9 us  [sum_over_nodes(): lax.all_to_all(blocks, PLANE, split_axis=0, concat_axis=0, tiled=True)]
    all_to_all x2 -> x3, blocking collectives: 104 us -> 113 us  [the longest x2 101 us: over_nodes(): lax.all_to_all(blocks, NODES_FEAT, split_axis=0, concat_axis=0, axis_inde...]
  transfers between devices with their start and end apart: 6 -> 6, of which waited for: 3 -> 3; matrix products, arithmetic and copies ran while one was open for 0% -> 1% of each run, Pallas kernels for 2% -> 2%
where the time goes in v5:
time: 207 us
  blocking collectives  149 us (72%)
  Pallas kernels  28.7 us (14%)
  starting transfers between devices  13.8 us (7%)
  waiting for transfers between devices  11.1 us (5%)
    all_to_all x2, blocking collectives, over_nodes(): lax.all_to_all(blocks, NODES_FEAT, split_axis=0, concat_axis=0, axis_inde...  101 us
    pallas_call x8, Pallas kernels, call(): pl.pallas_call(body, out_shape=outs, in_specs=[SMEM] * len(scalars) + [VM...  28.7 us
    all_to_all x1, blocking collectives, sum_over_nodes(): lax.all_to_all(blocks, PLANE, split_axis=0, concat_axis=0, tiled=True)  12.9 us
    all_to_all x1, blocking collectives, per_device(): losses = lax.all_to_all(loss, PLANE_FEAT, 0, 0, tiled=True)  12.5 us
    all_to_all x1, blocking collectives, per_device(): lax.all_to_all(partial.reshape(planes * PACKED // 4, 4, LANES), PLANE, sp...  11.3 us
    all_to_all x1, blocking collectives, sum_over_nodes(): lax.all_to_all(copies, 'nodes_1', split_axis=0, concat_axis=0, tiled=True)  11 us
    ppermute x5, starting transfers between devices, partner(): return lax.ppermute(value, 'feat', swap)  10.4 us
    all_to_all x1, waiting for transfers between devices, per_device(): lax.all_to_all(partial.reshape(depth * PACKED // 4, 4, LANES), 'nodes_1',...  8.1 us
  transfers between devices with their start and end apart: 6, of which 3 were waited for; matrix products, arithmetic and copies ran while one was open for 1% of the time, Pallas kernels for 2%

profile of v5, /device:TPU:1, one launch (start us, length us, event | category | flops | bytes accessed | tf_op | source)
XLA Modules:
  0.0 206.9 jit_solution(15489171757174475713)
XLA Ops:
  0.7 3.3 %collective-permute-start.1 = (bf16[512,256]{1,0:T(8,128)(2,1)}, bf16[512,256]{1,0:T(8,128)(2,1)S(1)}, u32[]{:S(2)}, u32[]{:S(2)}) collective-permute-start(bf16[512,256]{1,0:T(8,128)(2,1)} %w2_own.1), channel_id=1, source_target_pairs={{0,1},{1,0},{2,3},{3,2},{4,5},{5,4},{6,7},{7,6},{8,9},{9,8},{10,11... | collective-permute-start | bytes 786440 | tf_op jit(solution)/shard_map/ppermute | solution.py:411
  3.9 0.1 collective-permute-start
  4.1 0.4 collective-permute-start.2
  4.5 0.8 copy.12
  5.3 0.1 reshape.53.outbound
  5.4 0.9 copy-done.1
  6.3 3.9 %send_features.1 = (bf16[4096,128]{1,0:T(8,128)(2,1)S(1)}, f32[512,128]{1,0:T(8,128)S(1)}) custom-call(s32[1]{0:T(128)} %bitcast.core, s32[8192]{0:T(1024)S(1)} %reshape.53.outbound, bf16[512,128]{1,0:T(8,128)(2,1)S(1)} %copy-done.1), custom_call_target="tpu_custom_call" | custom-call | tf_op jit(solution)/shard_map/send_features/pallas_call | solution.py:29
  10.2 0.0 collective-permute-done.w1_other
  10.2 0.0 collective-permute-done.1.w2_other
  10.2 37.7 %all_to_all.35 = bf16[128,32,128]{2,1,0:T(8,128)(2,1)S(1)} all-to-all(bf16[128,32,128]{2,1,0:T(8,128)(2,1)S(1)} %bitcast.18), channel_id=1, replica_groups={{0,2,4,6,8,10,12,14,16,18,20,22,24,26,28,30,32,34,36,38,40,42,44,46,48,..., dimensions={0} | all-to-all | bytes 2097152 | tf_op jit(solution)/shard_map/all_to_all | solution.py:417
  47.9 2.8 %collective-permute-start.3 = (bf16[128,32,128]{2,1,0:T(8,128)(2,1)S(1)}, bf16[128,32,128]{2,1,0:T(8,128)(2,1)S(1)}, u32[]{:S(2)}, u32[]{:S(2)}) collective-permute-start(bf16[128,32,128]{2,1,0:T(8,128)(2,1)S(1)} %all_to_all.35), channel_id=1, source_target_pairs={{0,1},{1,0},{2,3},{3,2},{4,5},{5,4},{6,7},{7,6},{8,9},{9,8},{10,11... | collective-permute-start | bytes 3145736 | tf_op jit(solution)/shard_map/ppermute | solution.py:411
  51.4 0.1 fusion.5
  51.5 1.5 collective-permute-done.3
  53.0 10.4 %first_mix.1 = (f32[512,128]{1,0:T(8,128)S(1)}, s32[4608,128]{1,0:T(8,128)S(1)}) custom-call(s32[1]{0:T(128)} %bitcast.core, s32[1]{0:T(128)S(6)} %copy.13.live_count, s32[4096]{0:T(1024)S(1)} %compare_select_fusion.1.sources, s32[8192]{0:T(1024)S(1)} %reshape.53.outbound, f32[512,128]{1,0:T(8,128)S(1)} %get-tuple-element.18.features, ...), custom_call_target="tpu_custom_call" | custom-call | tf_op jit(solution)/shard_map/first_mix/pallas_call | solution.py:29
  63.3 0.0 copy-start
  63.4 0.0 copy-start.2
  63.4 0.0 copy-start.3
  63.4 63.8 %all_to_all.36 = s32[1152,4,128]{2,1,0:T(4,128)S(1)} all-to-all(s32[1152,4,128]{2,1,0:T(4,128)S(1)} %bitcast.15), channel_id=1, replica_groups={{0,2,4,6,8,10,12,14,16,18,20,22,24,26,28,30,32,34,36,38,40,42,44,46,48,..., dimensions={0} | all-to-all | bytes 4718592 | tf_op jit(solution)/shard_map/all_to_all | solution.py:417
  127.2 11.6 %second_mix.1 = (f32[512,512]{1,0:T(8,128)S(1)}, f32[16,8,128]{2,1,0:T(8,128)S(1)}, f32[8,128]{1,0:T(8,128)S(1)}) custom-call(s32[1]{0:T(128)} %bitcast.core, s32[1]{0:T(128)S(6)} %copy.13.live_count, s32[4096]{0:T(1024)S(1)} %bitcast.22, s32[4608,128]{1,0:T(8,128)S(1)} %bitcast.13, f32[512,128]{1,0:T(8,128)S(1)} %get-tuple-element.22.mixed, ...), custom_call_target="tpu_custom_call" | custom-call | tf_op jit(solution)/shard_map/second_mix/pallas_call | solution.py:29
  138.7 12.9 %all_to_all.37.arrived = f32[16,8,128]{2,1,0:T(8,128)S(1)} all-to-all(f32[16,8,128]{2,1,0:T(8,128)S(1)} %get-tuple-element.26), channel_id=1, replica_groups=mesh['nodes_0'=4,'nodes_1'=8,'nodes_2'=4,'feat'=2] {'nodes_0','nodes_2'}, dimensions={0} | all-to-all | bytes 131072 | tf_op jit(solution)/shard_map/all_to_all | solution.py:427
  151.6 11.0 %all_to_all.38.sums = f32[8,8,128]{2,1,0:T(8,128)S(1)} all-to-all(f32[8,8,128]{2,1,0:T(8,128)S(1)} %add_sums.1), channel_id=1, replica_groups=mesh['nodes_0'=4,'nodes_1'=8,'nodes_2'=4,'feat'=2] {'nodes_1'}, dimensions={0} | all-to-all | bytes 65536 | tf_op jit(solution)/shard_map/all_to_all | solution.py:431
  162.7 0.2 normalize.1.own
  162.9 3.9 %collective-permute-start.4 = (bf16[512,512]{1,0:T(8,128)(2,1)S(1)}, bf16[512,512]{1,0:T(8,128)(2,1)S(1)}, u32[]{:S(2)}, u32[]{:S(2)}) collective-permute-start(bf16[512,512]{1,0:T(8,128)(2,1)S(1)} %normalize.1.own), channel_id=1, source_target_pairs={{0,1},{1,0},{2,3},{3,2},{4,5},{5,4},{6,7},{7,6},{8,9},{9,8},{10,11... | collective-permute-start | bytes 1572872 | tf_op jit(solution)/shard_map/ppermute | solution.py:411
  166.8 1.5 collective-permute-done.4.other
  168.3 1.2 correlate.1
  169.5 11.3 %all_to_all.39 = s32[144,4,128]{2,1,0:T(4,128)S(1)} all-to-all(s32[144,4,128]{2,1,0:T(4,128)S(1)} %bitcast.20), channel_id=1, replica_groups=mesh['nodes_0'=4,'nodes_1'=8,'nodes_2'=4,'feat'=2] {'nodes_0','nodes_2'}, dimensions={0} | all-to-all | bytes 589824 | tf_op jit(solution)/shard_map/all_to_all | solution.py:527
  180.8 0.8 add_products.1
  181.6 3.4 %all-to-all-start.5 = ((s32[72,4,128]{2,1,0:T(4,128)}), s32[72,4,128]{2,1,0:T(4,128)S(1)}, u32[]{:S(2)}, u32[]{:S(2)}) async-start(s32[72,4,128]{2,1,0:T(4,128)} %bitcast.11), calls=%async_computation.5 | async-start | bytes 294912 | tf_op jit(solution)/shard_map/all_to_all | solution.py:537
  185.0 8.1 %all-to-all-done.5 = s32[72,4,128]{2,1,0:T(4,128)S(1)} async-done(((s32[72,4,128]{2,1,0:T(4,128)}), s32[72,4,128]{2,1,0:T(4,128)S(1)}, u32[]{:S(2)}, u32[]{:S(2)}) %all-to-all-start.5) | async-done | bytes 147488 | tf_op jit(solution)/shard_map/all_to_all | solution.py:537
  193.1 0.7 finish.1
  193.8 12.5 %all_to_all.40 = f32[32,1,128]{2,1,0:T(1,128)S(1)} all-to-all(f32[32,1,128]{2,1,0:T(1,128)S(1)} %get-tuple-element.32), channel_id=1, replica_groups=mesh['nodes_0'=4,'nodes_1'=8,'nodes_2'=4,'feat'=2] {'nodes_0','nodes_2',..., dimensions={0} | all-to-all | bytes 32768 | tf_op jit(solution)/shard_map/all_to_all | solution.py:551
  206.2 0.6 slice_reduce_fusion
  (14 shorter events, 0.1 us)
Async XLA Ops:
  0.6 50.7 %copy-start.5 = (s32[2,4096]{1,0:T(2,128)S(1)}, s32[2,4096]{1,0:T(2,128)}, u32[]{:S(2)}) copy-start(s32[2,4096]{1,0:T(2,128)} %param.14) | copy-start | bytes 98308
  0.6 50.7 %copy-start.4 = (s32[2,4096]{1,0:T(2,128)S(1)}, s32[2,4096]{1,0:T(2,128)}, u32[]{:S(2)}) copy-start(s32[2,4096]{1,0:T(2,128)} %param.13) | copy-start | bytes 98308
  0.7 50.7 %copy-start.6 = (s32[2,4096]{1,0:T(2,128)S(1)}, s32[2,4096]{1,0:T(2,128)}, u32[]{:S(2)}) copy-start(s32[2,4096]{1,0:T(2,128)} %param.12) | copy-start | bytes 98308
  0.7 9.5 %collective-permute-start.1 = (bf16[512,256]{1,0:T(8,128)(2,1)}, bf16[512,256]{1,0:T(8,128)(2,1)S(1)}, u32[]{:S(2)}, u32[]{:S(2)}) collective-permute-start(bf16[512,256]{1,0:T(8,128)(2,1)} %w2_own.1), channel_id=1, source_target_pairs={{0,1},{1,0},{2,3},{3,2},{4,5},{5,4},{6,7},{7,6},{8,9},{9,8},{10,11... | collective-permute-start | bytes 786440 | tf_op jit(solution)/shard_map/ppermute | solution.py:411
  3.9 6.2 %collective-permute-start = (bf16[128,256]{1,0:T(8,128)(2,1)}, bf16[128,256]{1,0:T(8,128)(2,1)S(1)}, u32[]{:S(2)}, u32[]{:S(2)}) collective-permute-start(bf16[128,256]{1,0:T(8,128)(2,1)} %w1_own.1), channel_id=1, source_target_pairs={{0,1},{1,0},{2,3},{3,2},{4,5},{5,4},{6,7},{7,6},{8,9},{9,8},{10,11... | collective-permute-start | bytes 196616 | tf_op jit(solution)/shard_map/ppermute | solution.py:411
  4.1 6.1 %collective-permute-start.2 = (f32[1,256]{1,0:T(1,128)}, f32[1,256]{1,0:T(1,128)S(1)}, u32[]{:S(2)}, u32[]{:S(2)}) collective-permute-start(f32[1,256]{1,0:T(1,128)} %bitcast.23), channel_id=1, source_target_pairs={{0,1},{1,0},{2,3},{3,2},{4,5},{5,4},{6,7},{7,6},{8,9},{9,8},{10,11... | collective-permute-start | bytes 3080 | tf_op jit(solution)/shard_map/ppermute | solution.py:411
  5.4 0.9 copy-start.1
  47.9 5.0 %collective-permute-start.3 = (bf16[128,32,128]{2,1,0:T(8,128)(2,1)S(1)}, bf16[128,32,128]{2,1,0:T(8,128)(2,1)S(1)}, u32[]{:S(2)}, u32[]{:S(2)}) collective-permute-start(bf16[128,32,128]{2,1,0:T(8,128)(2,1)S(1)} %all_to_all.35), channel_id=1, source_target_pairs={{0,1},{1,0},{2,3},{3,2},{4,5},{5,4},{6,7},{7,6},{8,9},{9,8},{10,11... | collective-permute-start | bytes 3145736 | tf_op jit(solution)/shard_map/ppermute | solution.py:411
  63.3 63.8 %copy-start = (bf16[512,256]{1,0:T(8,128)(2,1)S(1)}, bf16[512,256]{1,0:T(8,128)(2,1)}, u32[]{:S(2)}) copy-start(bf16[512,256]{1,0:T(8,128)(2,1)} %w2_own.1) | copy-start | bytes 786436
  63.4 63.8 %copy-start.2 = (bf16[128,256]{1,0:T(8,128)(2,1)S(1)}, bf16[128,256]{1,0:T(8,128)(2,1)}, u32[]{:S(2)}) copy-start(bf16[128,256]{1,0:T(8,128)(2,1)} %w1_own.1) | copy-start | bytes 196612
  63.4 63.8 %copy-start.3 = (f32[256]{0:T(256)S(1)}, f32[256]{0:T(256)}, u32[]{:S(2)}) copy-start(f32[256]{0:T(256)} %param.16) | copy-start | bytes 3076
  162.9 5.4 %collective-permute-start.4 = (bf16[512,512]{1,0:T(8,128)(2,1)S(1)}, bf16[512,512]{1,0:T(8,128)(2,1)S(1)}, u32[]{:S(2)}, u32[]{:S(2)}) collective-permute-start(bf16[512,512]{1,0:T(8,128)(2,1)S(1)} %normalize.1.own), channel_id=1, source_target_pairs={{0,1},{1,0},{2,3},{3,2},{4,5},{5,4},{6,7},{7,6},{8,9},{9,8},{10,11... | collective-permute-start | bytes 1572872 | tf_op jit(solution)/shard_map/ppermute | solution.py:411
  181.6 11.5 %all-to-all-start.5 = ((s32[72,4,128]{2,1,0:T(4,128)}), s32[72,4,128]{2,1,0:T(4,128)S(1)}, u32[]{:S(2)}, u32[]{:S(2)}) async-start(s32[72,4,128]{2,1,0:T(4,128)} %bitcast.11), calls=%async_computation.5 | async-start | bytes 294912 | tf_op jit(solution)/shard_map/all_to_all | solution.py:537

commit v6 on v5

--- a/solution.py
+++ b/solution.py
@@ -15,11 +15,12 @@
 
 LANES = 128
 TILE = 128
-CODE_BITS = 18
+CODE_BITS = 17
 CODE_TOP = 2 ** (CODE_BITS - 1)
 SCALE_BIAS = 224.0
-COARSE = 5
-PACKED = 36
+COARSE = 9
+PACKED = 34
+PRODUCTS = 36
 
 VMEM = pl.BlockSpec(memory_space=pltpu.VMEM)
 SMEM = pl.BlockSpec(memory_space=pltpu.SMEM)
@@ -92,8 +93,7 @@
     mixed,
     words,
     table,
-    picked_even,
-    picked_odd,
+    picked,
     codes,
     coded_even,
     coded_odd,
@@ -109,19 +109,20 @@
     in_chunks(halo, 256, widen)
     edges = targets.shape[1]
 
-    def pick(tile, picked):
-        for edge in range(edges):
-            source = sources[tile * edges + edge]
-            picked[edge : edge + 1, :] = table[pl.ds(source, 1), :]
-
-    pick(0, picked_even)
+    def pick(block, _):
+        base = pl.multiple_of(block * 128, 128)
+        for edge in range(128):
+            near = sources.at[pl.ds(edge, sources.shape[0] - 128)]
+            picked[pl.ds(base + edge, 1), :] = table[pl.ds(near[base], 1), :]
+        return 0
+
+    lax.fori_loop(0, sources.shape[0] // 128, pick, 0)
     for tile in range(local // TILE):
-        picked, later = (picked_even, picked_odd) if tile % 2 == 0 else (picked_odd, picked_even)
-        if tile + 1 < local // TILE:
-            pick(tile + 1, later)
         onehot, degree = edge_table(targets, tile)
         summed = jnp.dot(
-            onehot, picked[...].astype(jnp.bfloat16), preferred_element_type=jnp.float32
+            onehot,
+            picked[tile * edges : (tile + 1) * edges, :].astype(jnp.bfloat16),
+            preferred_element_type=jnp.float32,
         )
         rows = slice(tile * TILE, (tile + 1) * TILE)
         mix = (table[rows, :] + summed) / (1.0 + degree)
@@ -145,16 +146,18 @@
         to = place_of(core, peer, words.shape[0] // PACKED) * PACKED
         octet = [coded[first + 8 * k : first + 8 * k + 8, :] for k in range(8)]
         for k in range(4):
-            low = (octet[k] >> 2) & 0xFFFF
-            words[pl.ds(to + 8 * k, 8), :] = low | ((octet[k + 4] >> 2) << 16)
+            low = (octet[k] >> 1) & 0xFFFF
+            words[pl.ds(to + 8 * k, 8), :] = low | ((octet[k + 4] >> 1) << 16)
         fine = jnp.zeros((8, LANES), jnp.int32)
         coarse = counted
         for k in range(8):
-            fine = fine | ((octet[k] & 3) << (4 * k + 2 * (row // 4)))
-            scale = (octet[k] >> CODE_BITS) << (16 * (k % 2) + 8 * (row // 4))
-            coarse = coarse | jnp.where(lane == k // 2, scale, 0)
+            fine = fine | ((octet[k] & 1) << (4 * k + row // 2))
+            scale = (octet[k] >> CODE_BITS) << (8 * (row // 2))
+            coarse = coarse | jnp.where(lane == k, scale, 0)
         fine = jnp.where(lane < COARSE, coarse, fine)
-        words[pl.ds(to + 32, 4), :] = fine[0:4, :] | fine[4:8, :]
+        fine = fine | pltpu.roll(fine, 4, 0)
+        fine = fine | pltpu.roll(fine, 2, 0)
+        words[pl.ds(to + 32, 2), :] = fine[0:2, :]
 
     blocks = words.shape[0] // (4 * PACKED)
     pick_slots(0, 0, coded_even)
@@ -225,19 +228,16 @@
         to = place_of(core, peer, words.shape[0] // PACKED) * 64
         to = pl.multiple_of(local + to, 64)
         pairs = [words[pl.ds(base + 8 * k, 8), :] for k in range(4)]
-        rest = words[pl.ds(base + 28, 8), :]
+        rest = words[pl.ds(base + 26, 8), :]
+        rest = jnp.where(row < 6, pltpu.roll(rest, 6, 0), rest)
         rest = jnp.where(row < 4, pltpu.roll(rest, 4, 0), rest)
-        scales = []
-        for side in range(2):
-            step = (rest >> (16 * side + 8 * (row // 4))) & 255
-            scale = jnp.exp2((step.astype(jnp.float32) - SCALE_BIAS) * 0.125)
-            scales.append(scale * (1.0 / CODE_TOP))
-        fine = jnp.where(lane < COARSE, -0x55555556, rest)
+        step = (rest >> (8 * (row // 2))) & 255
+        scale = jnp.exp2((step.astype(jnp.float32) - SCALE_BIAS) * 0.125) * (1.0 / CODE_TOP)
+        fine = jnp.where(lane < COARSE, 0, rest)
         for k in range(8):
             high = (pairs[k] << 16) >> 16 if k < 4 else pairs[k - 4] >> 16
-            code = (high << 2) | ((fine >> (4 * k + 2 * (row // 4))) & 3)
-            scale = scales[k % 2][:, k // 2 : k // 2 + 1]
-            table[pl.ds(to + 8 * k, 8), :] = code.astype(jnp.float32) * scale
+            code = (high << 1) | ((fine >> (4 * k + row // 2)) & 1)
+            table[pl.ds(to + 8 * k, 8), :] = code.astype(jnp.float32) * scale[:, k : k + 1]
         return rest
 
     def unpack_several(block, counts):
@@ -304,7 +304,7 @@
     top = jnp.maximum(jnp.max(top, 0, keepdims=True), 1e-30)
     step = jnp.floor(8.0 * jnp.log2(top)) + 2.0
     scale = jnp.exp2(step * -0.125) * 32767.0
-    first = place * PACKED
+    first = place * PRODUCTS
     for m, pair in enumerate(sides):
         low, high = (jnp.round(side * scale).astype(jnp.int32) for side in pair)
         out[first + 8 * m : first + 8 * m + 8, :] = (low & 0xFFFF) | (high << 16)
@@ -313,8 +313,8 @@
 
 def sum_products(arrived):
     total = [[0.0, 0.0] for _ in range(4)]
-    for place in range(arrived.shape[0] // PACKED):
-        first = place * PACKED
+    for place in range(arrived.shape[0] // PRODUCTS):
+        first = place * PRODUCTS
         step = arrived[first + 32 : first + 33, :].astype(jnp.float32)
         scale = jnp.exp2(step * 0.125) * (1.0 / 32767.0)
         for m in range(4):
@@ -327,8 +327,8 @@
 def add_products(arrived, out):
     total = sum_products(arrived)
     put_products(out, 0, total)
-    for place in range(1, out.shape[0] // PACKED):
-        out[place * PACKED : (place + 1) * PACKED, :] = out[0:PACKED, :]
+    for place in range(1, out.shape[0] // PRODUCTS):
+        out[place * PRODUCTS : (place + 1) * PRODUCTS, :] = out[0:PRODUCTS, :]
 
 
 def normalize(live_count, sums, node_total, embedded, out):
@@ -347,7 +347,7 @@
 def correlate(core, own, other, normed, out):
     half = normed.shape[2]
     width = 2 * half
-    groups, depth, wide = out.shape[0] // PACKED, 8, 4
+    groups, depth, wide = out.shape[0] // PRODUCTS, 8, 4
     contract = (((0,), (0,)), ((), ()))
 
     def give(left, right):
@@ -464,8 +464,7 @@
         (shape((local, f_in), f32), shape((peers * PACKED, f_in), i32)),
         [
             pltpu.VMEM((local + 2 * rows_half, f_in), f32),
-            pltpu.VMEM((edges // tiles, f_in), f32),
-            pltpu.VMEM((edges // tiles, f_in), f32),
+            pltpu.VMEM((edges, f_in), f32),
             pltpu.VMEM((local, f_in), i32),
             pltpu.VMEM((2 * halo, f_in), i32),
             pltpu.VMEM((2 * halo, f_in), i32),
@@ -477,7 +476,7 @@
         scalars=(core, row_counts, first_sources, outbound),
         name="first_mix",
     )
-    arrived = over_nodes(words.reshape(peers * PACKED // 4, 4, f_in))
+    arrived = over_nodes(words.reshape(peers * PACKED // 2, 2, f_in))
     embedded, sums, node_total = call(
         second_mix,
         (
@@ -517,7 +516,7 @@
     )
     normed, partial = call(
         correlate,
-        (shape((2, local, half), bf16), shape((planes * PACKED, LANES), i32)),
+        (shape((2, local, half), bf16), shape((planes * PRODUCTS, LANES), i32)),
         [],
         own,
         partner(own),
@@ -525,19 +524,19 @@
         name="correlate",
     )
     partial = lax.all_to_all(
-        partial.reshape(planes * PACKED // 4, 4, LANES), PLANE, split_axis=0, concat_axis=0, tiled=True
+        partial.reshape(planes * PRODUCTS // 4, 4, LANES), PLANE, split_axis=0, concat_axis=0, tiled=True
     )
     partial = call(
         add_products,
-        shape((depth * PACKED, LANES), i32),
+        shape((depth * PRODUCTS, LANES), i32),
         [],
-        partial.reshape(planes * PACKED, LANES),
+        partial.reshape(planes * PRODUCTS, LANES),
         name="add_products",
     )
     partial = lax.all_to_all(
-        partial.reshape(depth * PACKED // 4, 4, LANES), "nodes_1", split_axis=0, concat_axis=0, tiled=True
-    )
-    partial = partial.reshape(depth * PACKED, LANES)
+        partial.reshape(depth * PRODUCTS // 4, 4, LANES), "nodes_1", split_axis=0, concat_axis=0, tiled=True
+    )
+    partial = partial.reshape(depth * PRODUCTS, LANES)
     devices = lax.axis_size(PLANE_FEAT)
     correlation, loss = call(
         finish,

time: 207 us -> 205 us (level)
  blocking collectives: 149 us -> 146 us
    all_to_all x2, blocking collectives: 101 us -> 98.8 us  [over_nodes(): lax.all_to_all(blocks, NODES_FEAT, split_axis=0, concat_axis=0, axis_inde...]
where the time goes in v6:
time: 205 us; the launch traced here: 204 us
  blocking collectives  146 us (71%)
  Pallas kernels  28.7 us (14%)
  starting transfers between devices  13.8 us (7%)
  waiting for transfers between devices  11.1 us (5%)
    all_to_all x2, blocking collectives, over_nodes(): lax.all_to_all(blocks, NODES_FEAT, split_axis=0, concat_axis=0, axis_inde...  98.8 us
    pallas_call x8, Pallas kernels, call(): pl.pallas_call(body, out_shape=outs, in_specs=[SMEM] * len(scalars) + [VM...  28.7 us
    all_to_all x1, blocking collectives, sum_over_nodes(): lax.all_to_all(blocks, PLANE, split_axis=0, concat_axis=0, tiled=True)  12.6 us
    all_to_all x1, blocking collectives, per_device(): losses = lax.all_to_all(loss, PLANE_FEAT, 0, 0, tiled=True)  12.5 us
    all_to_all x1, blocking collectives, per_device(): lax.all_to_all(partial.reshape(planes * PRODUCTS // 4, 4, LANES), PLANE,...  11.3 us
    all_to_all x1, blocking collectives, sum_over_nodes(): lax.all_to_all(copies, 'nodes_1', split_axis=0, concat_axis=0, tiled=True)  11.1 us
    ppermute x5, starting transfers between devices, partner(): return lax.ppermute(value, 'feat', swap)  10.4 us
    all_to_all x1, waiting for transfers between devices, per_device(): lax.all_to_all(partial.reshape(depth * PRODUCTS // 4, 4, LANES), 'nodes_1...  8.1 us
  transfers between devices with their start and end apart: 6, of which 3 were waited for; matrix products, arithmetic and copies ran while one was open for 1% of the time, Pallas kernels for 2%

profile of v6, /device:TPU:1, one launch (start us, length us, event | category | flops | bytes accessed | tf_op | source)
XLA Modules:
  0.0 204.1 jit_solution(2398492724831383097)
XLA Ops:
  0.7 3.3 %collective-permute-start.1 = (bf16[512,256]{1,0:T(8,128)(2,1)}, bf16[512,256]{1,0:T(8,128)(2,1)S(1)}, u32[]{:S(2)}, u32[]{:S(2)}) collective-permute-start(bf16[512,256]{1,0:T(8,128)(2,1)} %w2_own.1), channel_id=1, source_target_pairs={{0,1},{1,0},{2,3},{3,2},{4,5},{5,4},{6,7},{7,6},{8,9},{9,8},{10,11... | collective-permute-start | bytes 786440 | tf_op jit(solution)/shard_map/ppermute | solution.py:411
  3.9 0.1 collective-permute-start
  4.1 0.4 collective-permute-start.2
  4.5 0.8 copy.12
  5.3 0.1 reshape.53.outbound
  5.4 0.9 copy-done.1
  6.3 3.9 %send_features.1 = (bf16[4096,128]{1,0:T(8,128)(2,1)S(1)}, f32[512,128]{1,0:T(8,128)S(1)}) custom-call(s32[1]{0:T(128)} %bitcast.core, s32[8192]{0:T(1024)S(1)} %reshape.53.outbound, bf16[512,128]{1,0:T(8,128)(2,1)S(1)} %copy-done.1), custom_call_target="tpu_custom_call" | custom-call | tf_op jit(solution)/shard_map/send_features/pallas_call | solution.py:30
  10.2 0.0 collective-permute-done.w1_other
  10.2 0.0 collective-permute-done.1.w2_other
  10.2 37.7 %all_to_all.35 = bf16[128,32,128]{2,1,0:T(8,128)(2,1)S(1)} all-to-all(bf16[128,32,128]{2,1,0:T(8,128)(2,1)S(1)} %bitcast.18), channel_id=1, replica_groups={{0,2,4,6,8,10,12,14,16,18,20,22,24,26,28,30,32,34,36,38,40,42,44,46,48,..., dimensions={0} | all-to-all | bytes 2097152 | tf_op jit(solution)/shard_map/all_to_all | solution.py:417
  47.9 2.8 %collective-permute-start.3 = (bf16[128,32,128]{2,1,0:T(8,128)(2,1)S(1)}, bf16[128,32,128]{2,1,0:T(8,128)(2,1)S(1)}, u32[]{:S(2)}, u32[]{:S(2)}) collective-permute-start(bf16[128,32,128]{2,1,0:T(8,128)(2,1)S(1)} %all_to_all.35), channel_id=1, source_target_pairs={{0,1},{1,0},{2,3},{3,2},{4,5},{5,4},{6,7},{7,6},{8,9},{9,8},{10,11... | collective-permute-start | bytes 3145736 | tf_op jit(solution)/shard_map/ppermute | solution.py:411
  51.4 0.1 fusion.5
  51.5 1.5 collective-permute-done.3
  53.0 10.3 %first_mix.1 = (f32[512,128]{1,0:T(8,128)S(1)}, s32[4352,128]{1,0:T(8,128)S(1)}) custom-call(s32[1]{0:T(128)} %bitcast.core, s32[1]{0:T(128)S(6)} %copy.13.live_count, s32[4096]{0:T(1024)S(1)} %compare_select_fusion.1.sources, s32[8192]{0:T(1024)S(1)} %reshape.53.outbound, f32[512,128]{1,0:T(8,128)S(1)} %get-tuple-element.18.features, ...), custom_call_target="tpu_custom_call" | custom-call | tf_op jit(solution)/shard_map/first_mix/pallas_call | solution.py:30
  63.3 0.0 copy-start
  63.3 0.0 copy-start.2
  63.3 0.0 copy-start.3
  63.3 61.1 %all_to_all.36 = s32[2176,2,128]{2,1,0:T(2,128)S(1)} all-to-all(s32[2176,2,128]{2,1,0:T(2,128)S(1)} %bitcast.15), channel_id=1, replica_groups={{0,2,4,6,8,10,12,14,16,18,20,22,24,26,28,30,32,34,36,38,40,42,44,46,48,..., dimensions={0} | all-to-all | bytes 4456448 | tf_op jit(solution)/shard_map/all_to_all | solution.py:417
  124.4 11.6 %second_mix.1 = (f32[512,512]{1,0:T(8,128)S(1)}, f32[16,8,128]{2,1,0:T(8,128)S(1)}, f32[8,128]{1,0:T(8,128)S(1)}) custom-call(s32[1]{0:T(128)} %bitcast.core, s32[1]{0:T(128)S(6)} %copy.13.live_count, s32[4096]{0:T(1024)S(1)} %bitcast.22, s32[4352,128]{1,0:T(8,128)S(1)} %bitcast.13, f32[512,128]{1,0:T(8,128)S(1)} %get-tuple-element.22.mixed, ...), custom_call_target="tpu_custom_call" | custom-call | tf_op jit(solution)/shard_map/second_mix/pallas_call | solution.py:30
  136.1 12.6 %all_to_all.37.arrived = f32[16,8,128]{2,1,0:T(8,128)S(1)} all-to-all(f32[16,8,128]{2,1,0:T(8,128)S(1)} %get-tuple-element.26), channel_id=1, replica_groups=mesh['nodes_0'=4,'nodes_1'=8,'nodes_2'=4,'feat'=2] {'nodes_0','nodes_2'}, dimensions={0} | all-to-all | bytes 131072 | tf_op jit(solution)/shard_map/all_to_all | solution.py:427
  148.7 11.1 %all_to_all.38.sums = f32[8,8,128]{2,1,0:T(8,128)S(1)} all-to-all(f32[8,8,128]{2,1,0:T(8,128)S(1)} %add_sums.1), channel_id=1, replica_groups=mesh['nodes_0'=4,'nodes_1'=8,'nodes_2'=4,'feat'=2] {'nodes_1'}, dimensions={0} | all-to-all | bytes 65536 | tf_op jit(solution)/shard_map/all_to_all | solution.py:431
  159.8 0.2 normalize.1.own
  160.1 3.9 %collective-permute-start.4 = (bf16[512,512]{1,0:T(8,128)(2,1)S(1)}, bf16[512,512]{1,0:T(8,128)(2,1)S(1)}, u32[]{:S(2)}, u32[]{:S(2)}) collective-permute-start(bf16[512,512]{1,0:T(8,128)(2,1)S(1)} %normalize.1.own), channel_id=1, source_target_pairs={{0,1},{1,0},{2,3},{3,2},{4,5},{5,4},{6,7},{7,6},{8,9},{9,8},{10,11... | collective-permute-start | bytes 1572872 | tf_op jit(solution)/shard_map/ppermute | solution.py:411
  164.0 1.5 collective-permute-done.4.other
  165.5 1.2 correlate.1
  166.7 11.3 %all_to_all.39 = s32[144,4,128]{2,1,0:T(4,128)S(1)} all-to-all(s32[144,4,128]{2,1,0:T(4,128)S(1)} %bitcast.20), channel_id=1, replica_groups=mesh['nodes_0'=4,'nodes_1'=8,'nodes_2'=4,'feat'=2] {'nodes_0','nodes_2'}, dimensions={0} | all-to-all | bytes 589824 | tf_op jit(solution)/shard_map/all_to_all | solution.py:526
  178.0 0.8 add_products.1
  178.8 3.4 %all-to-all-start.5 = ((s32[72,4,128]{2,1,0:T(4,128)}), s32[72,4,128]{2,1,0:T(4,128)S(1)}, u32[]{:S(2)}, u32[]{:S(2)}) async-start(s32[72,4,128]{2,1,0:T(4,128)} %bitcast.11), calls=%async_computation.5 | async-start | bytes 294912 | tf_op jit(solution)/shard_map/all_to_all | solution.py:536
  182.2 8.1 %all-to-all-done.5 = s32[72,4,128]{2,1,0:T(4,128)S(1)} async-done(((s32[72,4,128]{2,1,0:T(4,128)}), s32[72,4,128]{2,1,0:T(4,128)S(1)}, u32[]{:S(2)}, u32[]{:S(2)}) %all-to-all-start.5) | async-done | bytes 147488 | tf_op jit(solution)/shard_map/all_to_all | solution.py:536
  190.3 0.7 finish.1
  191.0 12.5 %all_to_all.40 = f32[32,1,128]{2,1,0:T(1,128)S(1)} all-to-all(f32[32,1,128]{2,1,0:T(1,128)S(1)} %get-tuple-element.32), channel_id=1, replica_groups=mesh['nodes_0'=4,'nodes_1'=8,'nodes_2'=4,'feat'=2] {'nodes_0','nodes_2',..., dimensions={0} | all-to-all | bytes 32768 | tf_op jit(solution)/shard_map/all_to_all | solution.py:550
  203.4 0.6 slice_reduce_fusion
  (14 shorter events, 0.1 us)
Async XLA Ops:
  0.6 50.7 %copy-start.5 = (s32[2,4096]{1,0:T(2,128)S(1)}, s32[2,4096]{1,0:T(2,128)}, u32[]{:S(2)}) copy-start(s32[2,4096]{1,0:T(2,128)} %param.14) | copy-start | bytes 98308
  0.6 50.7 %copy-start.4 = (s32[2,4096]{1,0:T(2,128)S(1)}, s32[2,4096]{1,0:T(2,128)}, u32[]{:S(2)}) copy-start(s32[2,4096]{1,0:T(2,128)} %param.13) | copy-start | bytes 98308
  0.7 50.7 %copy-start.6 = (s32[2,4096]{1,0:T(2,128)S(1)}, s32[2,4096]{1,0:T(2,128)}, u32[]{:S(2)}) copy-start(s32[2,4096]{1,0:T(2,128)} %param.12) | copy-start | bytes 98308
  0.7 9.5 %collective-permute-start.1 = (bf16[512,256]{1,0:T(8,128)(2,1)}, bf16[512,256]{1,0:T(8,128)(2,1)S(1)}, u32[]{:S(2)}, u32[]{:S(2)}) collective-permute-start(bf16[512,256]{1,0:T(8,128)(2,1)} %w2_own.1), channel_id=1, source_target_pairs={{0,1},{1,0},{2,3},{3,2},{4,5},{5,4},{6,7},{7,6},{8,9},{9,8},{10,11... | collective-permute-start | bytes 786440 | tf_op jit(solution)/shard_map/ppermute | solution.py:411
  3.9 6.2 %collective-permute-start = (bf16[128,256]{1,0:T(8,128)(2,1)}, bf16[128,256]{1,0:T(8,128)(2,1)S(1)}, u32[]{:S(2)}, u32[]{:S(2)}) collective-permute-start(bf16[128,256]{1,0:T(8,128)(2,1)} %w1_own.1), channel_id=1, source_target_pairs={{0,1},{1,0},{2,3},{3,2},{4,5},{5,4},{6,7},{7,6},{8,9},{9,8},{10,11... | collective-permute-start | bytes 196616 | tf_op jit(solution)/shard_map/ppermute | solution.py:411
  4.1 6.1 %collective-permute-start.2 = (f32[1,256]{1,0:T(1,128)}, f32[1,256]{1,0:T(1,128)S(1)}, u32[]{:S(2)}, u32[]{:S(2)}) collective-permute-start(f32[1,256]{1,0:T(1,128)} %bitcast.23), channel_id=1, source_target_pairs={{0,1},{1,0},{2,3},{3,2},{4,5},{5,4},{6,7},{7,6},{8,9},{9,8},{10,11... | collective-permute-start | bytes 3080 | tf_op jit(solution)/shard_map/ppermute | solution.py:411
  5.4 0.9 copy-start.1
  47.9 5.0 %collective-permute-start.3 = (bf16[128,32,128]{2,1,0:T(8,128)(2,1)S(1)}, bf16[128,32,128]{2,1,0:T(8,128)(2,1)S(1)}, u32[]{:S(2)}, u32[]{:S(2)}) collective-permute-start(bf16[128,32,128]{2,1,0:T(8,128)(2,1)S(1)} %all_to_all.35), channel_id=1, source_target_pairs={{0,1},{1,0},{2,3},{3,2},{4,5},{5,4},{6,7},{7,6},{8,9},{9,8},{10,11... | collective-permute-start | bytes 3145736 | tf_op jit(solution)/shard_map/ppermute | solution.py:411
  63.3 61.2 %copy-start = (bf16[512,256]{1,0:T(8,128)(2,1)S(1)}, bf16[512,256]{1,0:T(8,128)(2,1)}, u32[]{:S(2)}) copy-start(bf16[512,256]{1,0:T(8,128)(2,1)} %w2_own.1) | copy-start | bytes 786436
  63.3 61.2 %copy-start.2 = (bf16[128,256]{1,0:T(8,128)(2,1)S(1)}, bf16[128,256]{1,0:T(8,128)(2,1)}, u32[]{:S(2)}) copy-start(bf16[128,256]{1,0:T(8,128)(2,1)} %w1_own.1) | copy-start | bytes 196612
  63.3 61.1 %copy-start.3 = (f32[256]{0:T(256)S(1)}, f32[256]{0:T(256)}, u32[]{:S(2)}) copy-start(f32[256]{0:T(256)} %param.16) | copy-start | bytes 3076
  160.1 5.4 %collective-permute-start.4 = (bf16[512,512]{1,0:T(8,128)(2,1)S(1)}, bf16[512,512]{1,0:T(8,128)(2,1)S(1)}, u32[]{:S(2)}, u32[]{:S(2)}) collective-permute-start(bf16[512,512]{1,0:T(8,128)(2,1)S(1)} %normalize.1.own), channel_id=1, source_target_pairs={{0,1},{1,0},{2,3},{3,2},{4,5},{5,4},{6,7},{7,6},{8,9},{9,8},{10,11... | collective-permute-start | bytes 1572872 | tf_op jit(solution)/shard_map/ppermute | solution.py:411
  178.8 11.5 %all-to-all-start.5 = ((s32[72,4,128]{2,1,0:T(4,128)}), s32[72,4,128]{2,1,0:T(4,128)S(1)}, u32[]{:S(2)}, u32[]{:S(2)}) async-start(s32[72,4,128]{2,1,0:T(4,128)} %bitcast.11), calls=%async_computation.5 | async-start | bytes 294912 | tf_op jit(solution)/shard_map/all_to_all | solution.py:536

commit v7 on v6

--- a/solution.py
+++ b/solution.py
@@ -53,24 +53,21 @@
     return table.astype(jnp.bfloat16), jnp.sum(table, 1, keepdims=True)
 
 
-def place_of(core, peer, peers):
-    return jnp.where(core[0] == 0, peer, peers - 1 - peer)
-
-
-def send_features(core, outbound, features, out, table, rows):
-    table[...] = features[...].astype(jnp.float32)
+FOUR = 4
+
+
+def send_features(core, outbound, table, out, rows):
     half = out.shape[0] // LANES
     first = core[0] * half
 
     def step(block, _):
-        place = place_of(core, block, out.shape[0] // (4 * half))
-        base = pl.multiple_of(place * 4 * half, 4 * half)
-        for peer in range(4):
-            to = base + jnp.where(core[0] == 0, peer, 3 - peer) * half
+        place = jnp.where(core[0] == 0, block, out.shape[0] // (FOUR * half) - 1 - block)
+        base = pl.multiple_of(place * FOUR * half, FOUR * half)
+        for peer in range(FOUR):
             for slot in range(half):
                 near = outbound.at[pl.ds(peer * 2 * half + slot, outbound.shape[0] - 8 * half)]
                 source = near[block * (8 * half) + first]
-                rows[pl.ds(to + slot, 1), :] = table[pl.ds(source, 1), :]
+                rows[pl.ds(base + peer * half + slot, 1), :] = table[pl.ds(source, 1), :]
         return 0
 
     lax.fori_loop(0, out.shape[0] // (4 * half), step, 0)
@@ -82,7 +79,6 @@
 
 
 def first_mix(
-    core,
     live_count,
     sources,
     outbound,
@@ -143,7 +139,7 @@
             coded[slot : slot + 1, :] = codes[pl.ds(near[block * 256], 1), :]
 
     def pack(peer, first, coded):
-        to = place_of(core, peer, words.shape[0] // PACKED) * PACKED
+        to = peer * PACKED
         octet = [coded[first + 8 * k : first + 8 * k + 8, :] for k in range(8)]
         for k in range(4):
             low = (octet[k] >> 1) & 0xFFFF
@@ -225,8 +221,7 @@
 
     def unpack(peer):
         base = peer * PACKED
-        to = place_of(core, peer, words.shape[0] // PACKED) * 64
-        to = pl.multiple_of(local + to, 64)
+        to = pl.multiple_of(local + peer * 64, 64)
         pairs = [words[pl.ds(base + 8 * k, 8), :] for k in range(4)]
         rest = words[pl.ds(base + 26, 8), :]
         rest = jnp.where(row < 6, pltpu.roll(rest, 6, 0), rest)
@@ -241,12 +236,12 @@
         return rest
 
     def unpack_several(block, counts):
-        for one in range(8):
-            counts = counts + unpack(block * 8 + one)
+        for one in range(16):
+            counts = counts + unpack(block * 16 + one)
         return counts
 
     counts = lax.fori_loop(
-        0, words.shape[0] // (8 * PACKED), unpack_several, jnp.zeros((8, LANES), jnp.int32)
+        0, words.shape[0] // (16 * PACKED), unpack_several, jnp.zeros((8, LANES), jnp.int32)
     )
     counts = jnp.where((lane == COARSE - 1) & (row == 0), counts, 0).astype(jnp.float32)
     counts = jnp.sum(jnp.sum(counts, 1, keepdims=True), 0, keepdims=True)
@@ -411,17 +406,9 @@
         return lax.ppermute(value, "feat", swap)
 
     first_cores = [2 * peer for peer in range(peers)]
-    second_cores = [2 * peer + 1 for peer in reversed(range(peers))]
-
-    def over_nodes(blocks):
-        return lax.all_to_all(
-            blocks,
-            NODES_FEAT,
-            split_axis=0,
-            concat_axis=0,
-            axis_index_groups=[first_cores, second_cores],
-            tiled=True,
-        )
+    second_cores = [
+        2 * (four + peer) + 1 for four in reversed(range(0, peers, FOUR)) for peer in range(FOUR)
+    ]
 
     def sum_over_nodes(blocks):
         blocks = lax.all_to_all(blocks, PLANE, split_axis=0, concat_axis=0, tiled=True)
@@ -440,23 +427,32 @@
     targets = jnp.where(kept == 1, targets, -1).reshape(tiles, edges // tiles)
 
     rows_half = peers * halo // 2
-    sent, wide = call(
+    wide = features.astype(f32)
+    sent = call(
         send_features,
-        (shape((rows_half, f_in), bf16), shape((local, f_in), f32)),
+        shape((rows_half, f_in), bf16),
         [pltpu.VMEM((rows_half, f_in), f32)],
-        features,
+        wide,
         scalars=(core, outbound),
         name="send_features",
     )
     sent, w1_other, w2_other, bias_other = lax.optimization_barrier(
         (sent, w1_other, w2_other, bias_other)
     )
-    got = over_nodes(sent.reshape(peers, halo // 2, f_in))
+    got = lax.all_to_all(
+        sent.reshape(peers, halo // 2, f_in),
+        NODES_FEAT,
+        split_axis=0,
+        concat_axis=0,
+        axis_index_groups=[first_cores, second_cores],
+        tiled=True,
+    )
     got_other = partner(got)
     remote = sources - local
     slot_half = (remote % halo) // (halo // 2)
     from_other = (slot_half != core_index).astype(i32)
-    sender = jnp.where(slot_half == 1, peers - 1 - remote // halo, remote // halo)
+    sender = remote // halo
+    sender = jnp.where(slot_half == 1, peers - FOUR - sender + 2 * (sender % FOUR), sender)
     remote = sender * (halo // 2) + remote % (halo // 2) + from_other * rows_half
     first_sources = jnp.where(sources < local, sources, remote + local)
     mixed, words = call(
@@ -473,10 +469,12 @@
         got.reshape(rows_half, f_in),
         got_other.reshape(rows_half, f_in),
         targets,
-        scalars=(core, row_counts, first_sources, outbound),
+        scalars=(row_counts, first_sources, outbound),
         name="first_mix",
     )
-    arrived = over_nodes(words.reshape(peers * PACKED // 2, 2, f_in))
+    arrived = lax.all_to_all(
+        words.reshape(peers * PACKED // 2, 2, f_in), NODES, split_axis=0, concat_axis=0, tiled=True
+    )
     embedded, sums, node_total = call(
         second_mix,
         (

time: 205 us -> 204 us (level)
  blocking collectives: 146 us -> 149 us
  starting transfers between devices: 13.8 us -> 11.2 us
    all_to_all x2, blocking collectives: 98.8 us -> 103 us  [the longest x1 62 us: per_device(): lax.all_to_all(words.reshape(peers * PACKED // 2, 2, f_in), NODES, split_...]
    ppermute x5, starting transfers between devices: 10.4 us -> 7.8 us  [partner(): return lax.ppermute(value, 'feat', swap)]
where the time goes in v7:
time: 204 us; the launch traced here: 203 us
  blocking collectives  149 us (73%)
  Pallas kernels  27.7 us (14%)
  waiting for transfers between devices  11.3 us (6%)
  starting transfers between devices  11.2 us (5%)
    all_to_all x1, blocking collectives, per_device(): lax.all_to_all(words.reshape(peers * PACKED // 2, 2, f_in), NODES, split_...  62 us
    all_to_all x1, blocking collectives, per_device(): lax.all_to_all(sent.reshape(peers, halo // 2, f_in), NODES_FEAT, split_ax...  40.9 us
    pallas_call x8, Pallas kernels, call(): pl.pallas_call(body, out_shape=outs, in_specs=[SMEM] * len(scalars) + [VM...  27.7 us
    all_to_all x1, blocking collectives, per_device(): losses = lax.all_to_all(loss, PLANE_FEAT, 0, 0, tiled=True)  12.5 us
    all_to_all x1, blocking collectives, sum_over_nodes(): lax.all_to_all(blocks, PLANE, split_axis=0, concat_axis=0, tiled=True)  11.8 us
    all_to_all x1, blocking collectives, per_device(): lax.all_to_all(partial.reshape(planes * PRODUCTS // 4, 4, LANES), PLANE,...  11.3 us
    all_to_all x1, blocking collectives, sum_over_nodes(): lax.all_to_all(copies, 'nodes_1', split_axis=0, concat_axis=0, tiled=True)  10.7 us
    all_to_all x1, waiting for transfers between devices, per_device(): lax.all_to_all(partial.reshape(depth * PRODUCTS // 4, 4, LANES), 'nodes_1...  8.1 us
  transfers between devices with their start and end apart: 6, of which 3 were waited for; matrix products, arithmetic and copies ran while one was open for 1% of the time, Pallas kernels for 2%

profile of v7, /device:TPU:1, one launch (start us, length us, event | category | flops | bytes accessed | tf_op | source)
XLA Modules:
  0.0 203.4 jit_solution(9031459518926079204)
XLA Ops:
  0.7 3.3 %collective-permute-start.1 = (bf16[512,256]{1,0:T(8,128)(2,1)}, bf16[512,256]{1,0:T(8,128)(2,1)S(1)}, u32[]{:S(2)}, u32[]{:S(2)}) collective-permute-start(bf16[512,256]{1,0:T(8,128)(2,1)} %w2_own.1), channel_id=1, source_target_pairs={{0,1},{1,0},{2,3},{3,2},{4,5},{5,4},{6,7},{7,6},{8,9},{9,8},{10,11... | collective-permute-start | bytes 786440 | tf_op jit(solution)/shard_map/ppermute | solution.py:406
  3.9 0.1 collective-permute-start
  4.1 0.4 collective-permute-start.2
  4.5 0.8 copy.12
  5.3 0.1 reshape.53.outbound
  5.4 0.9 convert_element_type.4.table.features
  6.3 3.6 %send_features.1 = bf16[4096,128]{1,0:T(8,128)(2,1)S(1)} custom-call(s32[1]{0:T(128)} %bitcast.core, s32[8192]{0:T(1024)S(1)} %reshape.53.outbound, f32[512,128]{1,0:T(8,128)S(1)} %convert_element_type.4.table.features), custom_call_target="tpu_custom_call" | custom-call | tf_op jit(solution)/shard_map/send_features/pallas_call | solution.py:30
  10.0 0.0 collective-permute-done.w1_other
  10.0 40.9 %all_to_all.35 = bf16[128,32,128]{2,1,0:T(8,128)(2,1)S(1)} all-to-all(bf16[128,32,128]{2,1,0:T(8,128)(2,1)S(1)} %bitcast.14), channel_id=1, replica_groups={{0,2,4,6,8,10,12,14,16,18,20,22,24,26,28,30,32,34,36,38,40,42,44,46,48,..., dimensions={0} | all-to-all | bytes 2097152 | tf_op jit(solution)/shard_map/all_to_all | solution.py:442
  50.8 0.2 collective-permute-start.3
  51.7 0.1 fusion.9
  51.8 0.1 compare_select_fusion.1.sources
  51.9 1.6 collective-permute-done.3
  53.5 10.1 %first_mix.1 = (f32[512,128]{1,0:T(8,128)S(1)}, s32[4352,128]{1,0:T(8,128)S(1)}) custom-call(s32[1]{0:T(128)S(6)} %copy.13.live_count, s32[4096]{0:T(1024)S(1)} %compare_select_fusion.1.sources, s32[8192]{0:T(1024)S(1)} %reshape.53.outbound, f32[512,128]{1,0:T(8,128)S(1)} %convert_element_type.4.table.features, bf16[4096,128]{1,0:T(8,128)(2,1)S(1)} %bitcast.15, ...), custom_call_target="tpu_custom_call" | custom-call | tf_op jit(solution)/shard_map/first_mix/pallas_call | solution.py:30
  63.6 0.0 copy-start
  63.7 0.0 copy-start.1
  63.7 0.0 copy-start.2
  63.7 62.0 %all_to_all.36 = s32[2176,2,128]{2,1,0:T(2,128)S(1)} all-to-all(s32[2176,2,128]{2,1,0:T(2,128)S(1)} %bitcast.16), channel_id=1, replica_groups=mesh['nodes_0'=4,'nodes_1'=8,'nodes_2'=4,'feat'=2] {'nodes_0','nodes_1',..., dimensions={0} | all-to-all | bytes 4456448 | tf_op jit(solution)/shard_map/all_to_all | solution.py:475
  125.7 11.0 %second_mix.1 = (f32[512,512]{1,0:T(8,128)S(1)}, f32[16,8,128]{2,1,0:T(8,128)S(1)}, f32[8,128]{1,0:T(8,128)S(1)}) custom-call(s32[1]{0:T(128)} %bitcast.core, s32[1]{0:T(128)S(6)} %copy.13.live_count, s32[4096]{0:T(1024)S(1)} %bitcast.22, s32[4352,128]{1,0:T(8,128)S(1)} %bitcast.13, f32[512,128]{1,0:T(8,128)S(1)} %get-tuple-element.18.mixed, ...), custom_call_target="tpu_custom_call" | custom-call | tf_op jit(solution)/shard_map/second_mix/pallas_call | solution.py:30
  136.7 11.8 %all_to_all.37.arrived = f32[16,8,128]{2,1,0:T(8,128)S(1)} all-to-all(f32[16,8,128]{2,1,0:T(8,128)S(1)} %get-tuple-element.22), channel_id=1, replica_groups=mesh['nodes_0'=4,'nodes_1'=8,'nodes_2'=4,'feat'=2] {'nodes_0','nodes_2'}, dimensions={0} | all-to-all | bytes 131072 | tf_op jit(solution)/shard_map/all_to_all | solution.py:414
  148.5 10.7 %all_to_all.38.sums = f32[8,8,128]{2,1,0:T(8,128)S(1)} all-to-all(f32[8,8,128]{2,1,0:T(8,128)S(1)} %add_sums.1), channel_id=1, replica_groups=mesh['nodes_0'=4,'nodes_1'=8,'nodes_2'=4,'feat'=2] {'nodes_1'}, dimensions={0} | all-to-all | bytes 65536 | tf_op jit(solution)/shard_map/all_to_all | solution.py:418
  159.3 0.2 normalize.1.own
  159.5 3.8 %collective-permute-start.4 = (bf16[512,512]{1,0:T(8,128)(2,1)S(1)}, bf16[512,512]{1,0:T(8,128)(2,1)S(1)}, u32[]{:S(2)}, u32[]{:S(2)}) collective-permute-start(bf16[512,512]{1,0:T(8,128)(2,1)S(1)} %normalize.1.own), channel_id=1, source_target_pairs={{0,1},{1,0},{2,3},{3,2},{4,5},{5,4},{6,7},{7,6},{8,9},{9,8},{10,11... | collective-permute-start | bytes 1572872 | tf_op jit(solution)/shard_map/ppermute | solution.py:406
  163.3 1.5 collective-permute-done.4.other
  164.8 1.2 correlate.1
  166.0 11.3 %all_to_all.39 = s32[144,4,128]{2,1,0:T(4,128)S(1)} all-to-all(s32[144,4,128]{2,1,0:T(4,128)S(1)} %bitcast.20), channel_id=1, replica_groups=mesh['nodes_0'=4,'nodes_1'=8,'nodes_2'=4,'feat'=2] {'nodes_0','nodes_2'}, dimensions={0} | all-to-all | bytes 589824 | tf_op jit(solution)/shard_map/all_to_all | solution.py:524
  177.3 0.8 add_products.1
  178.1 3.4 %all-to-all-start.5 = ((s32[72,4,128]{2,1,0:T(4,128)}), s32[72,4,128]{2,1,0:T(4,128)S(1)}, u32[]{:S(2)}, u32[]{:S(2)}) async-start(s32[72,4,128]{2,1,0:T(4,128)} %bitcast.11), calls=%async_computation.5 | async-start | bytes 294912 | tf_op jit(solution)/shard_map/all_to_all | solution.py:534
  181.5 8.1 %all-to-all-done.5 = s32[72,4,128]{2,1,0:T(4,128)S(1)} async-done(((s32[72,4,128]{2,1,0:T(4,128)}), s32[72,4,128]{2,1,0:T(4,128)S(1)}, u32[]{:S(2)}, u32[]{:S(2)}) %all-to-all-start.5) | async-done | bytes 147488 | tf_op jit(solution)/shard_map/all_to_all | solution.py:534
  189.6 0.7 finish.1
  190.3 12.5 %all_to_all.40 = f32[32,1,128]{2,1,0:T(1,128)S(1)} all-to-all(f32[32,1,128]{2,1,0:T(1,128)S(1)} %get-tuple-element.28), channel_id=1, replica_groups=mesh['nodes_0'=4,'nodes_1'=8,'nodes_2'=4,'feat'=2] {'nodes_0','nodes_2',..., dimensions={0} | all-to-all | bytes 32768 | tf_op jit(solution)/shard_map/all_to_all | solution.py:548
  202.7 0.6 slice_reduce_fusion
  (13 shorter events, 0.1 us)
Async XLA Ops:
  0.6 51.1 %copy-start.4 = (s32[2,4096]{1,0:T(2,128)S(1)}, s32[2,4096]{1,0:T(2,128)}, u32[]{:S(2)}) copy-start(s32[2,4096]{1,0:T(2,128)} %param.14) | copy-start | bytes 98308
  0.6 51.1 %copy-start.3 = (s32[2,4096]{1,0:T(2,128)S(1)}, s32[2,4096]{1,0:T(2,128)}, u32[]{:S(2)}) copy-start(s32[2,4096]{1,0:T(2,128)} %param.13) | copy-start | bytes 98308
  0.7 51.1 %copy-start.5 = (s32[2,4096]{1,0:T(2,128)S(1)}, s32[2,4096]{1,0:T(2,128)}, u32[]{:S(2)}) copy-start(s32[2,4096]{1,0:T(2,128)} %param.12) | copy-start | bytes 98308
  0.7 9.3 %collective-permute-start.1 = (bf16[512,256]{1,0:T(8,128)(2,1)}, bf16[512,256]{1,0:T(8,128)(2,1)S(1)}, u32[]{:S(2)}, u32[]{:S(2)}) collective-permute-start(bf16[512,256]{1,0:T(8,128)(2,1)} %w2_own.1), channel_id=1, source_target_pairs={{0,1},{1,0},{2,3},{3,2},{4,5},{5,4},{6,7},{7,6},{8,9},{9,8},{10,11... | collective-permute-start | bytes 786440 | tf_op jit(solution)/shard_map/ppermute | solution.py:406
  3.9 6.0 %collective-permute-start = (bf16[128,256]{1,0:T(8,128)(2,1)}, bf16[128,256]{1,0:T(8,128)(2,1)S(1)}, u32[]{:S(2)}, u32[]{:S(2)}) collective-permute-start(bf16[128,256]{1,0:T(8,128)(2,1)} %w1_own.1), channel_id=1, source_target_pairs={{0,1},{1,0},{2,3},{3,2},{4,5},{5,4},{6,7},{7,6},{8,9},{9,8},{10,11... | collective-permute-start | bytes 196616 | tf_op jit(solution)/shard_map/ppermute | solution.py:406
  4.1 5.9 %collective-permute-start.2 = (f32[1,256]{1,0:T(1,128)}, f32[1,256]{1,0:T(1,128)S(1)}, u32[]{:S(2)}, u32[]{:S(2)}) collective-permute-start(f32[1,256]{1,0:T(1,128)} %bitcast.23), channel_id=1, source_target_pairs={{0,1},{1,0},{2,3},{3,2},{4,5},{5,4},{6,7},{7,6},{8,9},{9,8},{10,11... | collective-permute-start | bytes 3080 | tf_op jit(solution)/shard_map/ppermute | solution.py:406
  50.8 2.7 %collective-permute-start.3 = (bf16[128,32,128]{2,1,0:T(8,128)(2,1)S(1)}, bf16[128,32,128]{2,1,0:T(8,128)(2,1)S(1)}, u32[]{:S(2)}, u32[]{:S(2)}) collective-permute-start(bf16[128,32,128]{2,1,0:T(8,128)(2,1)S(1)} %all_to_all.35), channel_id=1, source_target_pairs={{0,1},{1,0},{2,3},{3,2},{4,5},{5,4},{6,7},{7,6},{8,9},{9,8},{10,11... | collective-permute-start | bytes 3145736 | tf_op jit(solution)/shard_map/ppermute | solution.py:406
  63.6 62.0 %copy-start = (bf16[512,256]{1,0:T(8,128)(2,1)S(1)}, bf16[512,256]{1,0:T(8,128)(2,1)}, u32[]{:S(2)}) copy-start(bf16[512,256]{1,0:T(8,128)(2,1)} %w2_own.1) | copy-start | bytes 786436
  63.7 62.0 %copy-start.1 = (bf16[128,256]{1,0:T(8,128)(2,1)S(1)}, bf16[128,256]{1,0:T(8,128)(2,1)}, u32[]{:S(2)}) copy-start(bf16[128,256]{1,0:T(8,128)(2,1)} %w1_own.1) | copy-start | bytes 196612
  63.7 62.0 %copy-start.2 = (f32[256]{0:T(256)S(1)}, f32[256]{0:T(256)}, u32[]{:S(2)}) copy-start(f32[256]{0:T(256)} %param.16) | copy-start | bytes 3076
  159.5 5.3 %collective-permute-start.4 = (bf16[512,512]{1,0:T(8,128)(2,1)S(1)}, bf16[512,512]{1,0:T(8,128)(2,1)S(1)}, u32[]{:S(2)}, u32[]{:S(2)}) collective-permute-start(bf16[512,512]{1,0:T(8,128)(2,1)S(1)} %normalize.1.own), channel_id=1, source_target_pairs={{0,1},{1,0},{2,3},{3,2},{4,5},{5,4},{6,7},{7,6},{8,9},{9,8},{10,11... | collective-permute-start | bytes 1572872 | tf_op jit(solution)/shard_map/ppermute | solution.py:406
  178.1 11.5 %all-to-all-start.5 = ((s32[72,4,128]{2,1,0:T(4,128)}), s32[72,4,128]{2,1,0:T(4,128)S(1)}, u32[]{:S(2)}, u32[]{:S(2)}) async-start(s32[72,4,128]{2,1,0:T(4,128)} %bitcast.11), calls=%async_computation.5 | async-start | bytes 294912 | tf_op jit(solution)/shard_map/all_to_all | solution.py:534

commit v8 on v7

--- a/solution.py
+++ b/solution.py
@@ -501,23 +501,29 @@
         scalars=(core, row_counts, sources),
         name="second_mix",
     )
+    embedded_other = partner(embedded)
     sums = sum_over_nodes(sums)
-    own = call(
-        normalize,
-        shape((local, width), bf16),
-        [],
-        sums,
-        node_total,
-        embedded,
-        scalars=(row_counts,),
-        name="normalize",
-    )
+    sums_other = partner(sums)
+
+    def normalized(sums, embedded):
+        return call(
+            normalize,
+            shape((local, width), bf16),
+            [],
+            sums,
+            node_total,
+            embedded,
+            scalars=(row_counts,),
+            name="normalize",
+        )
+
+    own, other = normalized(sums, embedded), normalized(sums_other, embedded_other)
     normed, partial = call(
         correlate,
         (shape((2, local, half), bf16), shape((planes * PRODUCTS, LANES), i32)),
         [],
         own,
-        partner(own),
+        other,
         scalars=(core,),
         name="correlate",
     )

time: 204 us -> 203 us (level)
  blocking collectives: 149 us -> 146 us
  starting transfers between devices: 11.2 us -> 14 us
    ppermute x5 -> x6, starting transfers between devices: 7.8 us -> 10.6 us  [partner(): return lax.ppermute(value, 'feat', swap)]
    pallas_call x8 -> x9, Pallas kernels: 27.7 us -> 27.9 us  [call(): pl.pallas_call(body, out_shape=outs, in_specs=[SMEM] * len(scalars) + [VM...]
  transfers between devices with their start and end apart: 6 -> 7, of which waited for: 3 -> 3; matrix products, arithmetic and copies ran while one was open for 1% -> 1% of each run, Pallas kernels for 2% -> 2%
where the time goes in v8:
time: 203 us
  blocking collectives  146 us (72%)
  Pallas kernels  27.9 us (14%)
  starting transfers between devices  14 us (7%)
  waiting for transfers between devices  10.4 us (5%)
    all_to_all x1, blocking collectives, per_device(): lax.all_to_all(words.reshape(peers * PACKED // 2, 2, f_in), NODES, split_...  62 us
    all_to_all x1, blocking collectives, per_device(): lax.all_to_all(sent.reshape(peers, halo // 2, f_in), NODES_FEAT, split_ax...  40.9 us
    pallas_call x9, Pallas kernels, call(): pl.pallas_call(body, out_shape=outs, in_specs=[SMEM] * len(scalars) + [VM...  27.9 us
    all_to_all x1, blocking collectives, per_device(): losses = lax.all_to_all(loss, PLANE_FEAT, 0, 0, tiled=True)  12.4 us
    all_to_all x1, blocking collectives, per_device(): lax.all_to_all(partial.reshape(planes * PRODUCTS // 4, 4, LANES), PLANE,...  11.3 us
    ppermute x6, starting transfers between devices, partner(): return lax.ppermute(value, 'feat', swap)  10.6 us
    all_to_all x1, blocking collectives, sum_over_nodes(): lax.all_to_all(blocks, PLANE, split_axis=0, concat_axis=0, tiled=True)  10 us
    all_to_all x1, blocking collectives, sum_over_nodes(): lax.all_to_all(copies, 'nodes_1', split_axis=0, concat_axis=0, tiled=True)  9.71 us
  transfers between devices with their start and end apart: 7, of which 3 were waited for; matrix products, arithmetic and copies ran while one was open for 1% of the time, Pallas kernels for 2%

profile of v8, /device:TPU:1, one launch (start us, length us, event | category | flops | bytes accessed | tf_op | source)
XLA Modules:
  0.0 202.7 jit_solution(15273655338129199522)
XLA Ops:
  0.7 3.3 %collective-permute-start.1 = (bf16[512,256]{1,0:T(8,128)(2,1)}, bf16[512,256]{1,0:T(8,128)(2,1)S(1)}, u32[]{:S(2)}, u32[]{:S(2)}) collective-permute-start(bf16[512,256]{1,0:T(8,128)(2,1)} %w2_own.1), channel_id=1, source_target_pairs={{0,1},{1,0},{2,3},{3,2},{4,5},{5,4},{6,7},{7,6},{8,9},{9,8},{10,11... | collective-permute-start | bytes 786440 | tf_op jit(solution)/shard_map/ppermute | solution.py:406
  3.9 0.1 collective-permute-start
  4.1 0.4 collective-permute-start.2
  4.5 0.8 copy.12
  5.3 0.1 reshape.53.outbound
  5.4 0.9 convert_element_type.4.table.features
  6.3 3.6 %send_features.1 = bf16[4096,128]{1,0:T(8,128)(2,1)S(1)} custom-call(s32[1]{0:T(128)} %bitcast.core, s32[8192]{0:T(1024)S(1)} %reshape.53.outbound, f32[512,128]{1,0:T(8,128)S(1)} %convert_element_type.4.table.features), custom_call_target="tpu_custom_call" | custom-call | tf_op jit(solution)/shard_map/send_features/pallas_call | solution.py:30
  10.0 40.9 %all_to_all.35 = bf16[128,32,128]{2,1,0:T(8,128)(2,1)S(1)} all-to-all(bf16[128,32,128]{2,1,0:T(8,128)(2,1)S(1)} %bitcast.14), channel_id=1, replica_groups={{0,2,4,6,8,10,12,14,16,18,20,22,24,26,28,30,32,34,36,38,40,42,44,46,48,..., dimensions={0} | all-to-all | bytes 2097152 | tf_op jit(solution)/shard_map/all_to_all | solution.py:442
  50.8 0.2 collective-permute-start.3
  51.7 0.1 fusion.9
  51.8 0.1 compare_select_fusion.1.sources
  51.9 1.6 collective-permute-done.3
  53.5 10.1 %first_mix.1 = (f32[512,128]{1,0:T(8,128)S(1)}, s32[4352,128]{1,0:T(8,128)S(1)}) custom-call(s32[1]{0:T(128)S(6)} %copy.13.live_count, s32[4096]{0:T(1024)S(1)} %compare_select_fusion.1.sources, s32[8192]{0:T(1024)S(1)} %reshape.53.outbound, f32[512,128]{1,0:T(8,128)S(1)} %convert_element_type.4.table.features, bf16[4096,128]{1,0:T(8,128)(2,1)S(1)} %bitcast.15, ...), custom_call_target="tpu_custom_call" | custom-call | tf_op jit(solution)/shard_map/first_mix/pallas_call | solution.py:30
  63.7 0.0 copy-start.1
  63.7 0.0 copy-start.2
  63.7 62.0 %all_to_all.36 = s32[2176,2,128]{2,1,0:T(2,128)S(1)} all-to-all(s32[2176,2,128]{2,1,0:T(2,128)S(1)} %bitcast.16), channel_id=1, replica_groups=mesh['nodes_0'=4,'nodes_1'=8,'nodes_2'=4,'feat'=2] {'nodes_0','nodes_1',..., dimensions={0} | all-to-all | bytes 4456448 | tf_op jit(solution)/shard_map/all_to_all | solution.py:475
  125.6 11.0 %second_mix.1 = (f32[512,512]{1,0:T(8,128)S(1)}, f32[16,8,128]{2,1,0:T(8,128)S(1)}, f32[8,128]{1,0:T(8,128)S(1)}) custom-call(s32[1]{0:T(128)} %bitcast.core, s32[1]{0:T(128)S(6)} %copy.13.live_count, s32[4096]{0:T(1024)S(1)} %bitcast.22, s32[4352,128]{1,0:T(8,128)S(1)} %bitcast.13, f32[512,128]{1,0:T(8,128)S(1)} %get-tuple-element.18.mixed, ...), custom_call_target="tpu_custom_call" | custom-call | tf_op jit(solution)/shard_map/second_mix/pallas_call | solution.py:30
  136.7 4.0 %collective-permute-start.5 = (f32[512,512]{1,0:T(8,128)S(1)}, f32[512,512]{1,0:T(8,128)S(1)}, u32[]{:S(2)}, u32[]{:S(2)}) collective-permute-start(f32[512,512]{1,0:T(8,128)S(1)} %get-tuple-element.24.embedded), channel_id=1, source_target_pairs={{0,1},{1,0},{2,3},{3,2},{4,5},{5,4},{6,7},{7,6},{8,9},{9,8},{10,11... | collective-permute-start | bytes 3145736 | tf_op jit(solution)/shard_map/ppermute | solution.py:406
  140.7 10.0 %all_to_all.37.arrived = f32[16,8,128]{2,1,0:T(8,128)S(1)} all-to-all(f32[16,8,128]{2,1,0:T(8,128)S(1)} %get-tuple-element.22), channel_id=1, replica_groups=mesh['nodes_0'=4,'nodes_1'=8,'nodes_2'=4,'feat'=2] {'nodes_0','nodes_2'}, dimensions={0} | all-to-all | bytes 131072 | tf_op jit(solution)/shard_map/all_to_all | solution.py:414
  150.7 9.7 %all_to_all.38.sums = f32[8,8,128]{2,1,0:T(8,128)S(1)} all-to-all(f32[8,8,128]{2,1,0:T(8,128)S(1)} %add_sums.1), channel_id=1, replica_groups=mesh['nodes_0'=4,'nodes_1'=8,'nodes_2'=4,'feat'=2] {'nodes_1'}, dimensions={0} | all-to-all | bytes 65536 | tf_op jit(solution)/shard_map/all_to_all | solution.py:418
  160.5 2.6 %collective-permute-start.4 = (f32[8,8,128]{2,1,0:T(8,128)S(1)}, f32[8,8,128]{2,1,0:T(8,128)S(1)}, u32[]{:S(2)}, u32[]{:S(2)}) collective-permute-start(f32[8,8,128]{2,1,0:T(8,128)S(1)} %all_to_all.38.sums), channel_id=1, source_target_pairs={{0,1},{1,0},{2,3},{3,2},{4,5},{5,4},{6,7},{7,6},{8,9},{9,8},{10,11... | collective-permute-start | bytes 98312 | tf_op jit(solution)/shard_map/ppermute | solution.py:406
  163.1 0.2 normalize.2.own
  163.3 0.6 collective-permute-done.4.sums
  163.9 0.2 normalize.3.other
  164.2 1.2 correlate.1
  165.4 11.3 %all_to_all.39 = s32[144,4,128]{2,1,0:T(4,128)S(1)} all-to-all(s32[144,4,128]{2,1,0:T(4,128)S(1)} %bitcast.20), channel_id=1, replica_groups=mesh['nodes_0'=4,'nodes_1'=8,'nodes_2'=4,'feat'=2] {'nodes_0','nodes_2'}, dimensions={0} | all-to-all | bytes 589824 | tf_op jit(solution)/shard_map/all_to_all | solution.py:530
  176.7 0.8 add_products.1
  177.5 3.4 %all-to-all-start.5 = ((s32[72,4,128]{2,1,0:T(4,128)}), s32[72,4,128]{2,1,0:T(4,128)S(1)}, u32[]{:S(2)}, u32[]{:S(2)}) async-start(s32[72,4,128]{2,1,0:T(4,128)} %bitcast.11), calls=%async_computation.5 | async-start | bytes 294912 | tf_op jit(solution)/shard_map/all_to_all | solution.py:540
  180.9 8.1 %all-to-all-done.5 = s32[72,4,128]{2,1,0:T(4,128)S(1)} async-done(((s32[72,4,128]{2,1,0:T(4,128)}), s32[72,4,128]{2,1,0:T(4,128)S(1)}, u32[]{:S(2)}, u32[]{:S(2)}) %all-to-all-start.5) | async-done | bytes 147488 | tf_op jit(solution)/shard_map/all_to_all | solution.py:540
  189.0 0.7 finish.1
  189.7 12.4 %all_to_all.40 = f32[32,1,128]{2,1,0:T(1,128)S(1)} all-to-all(f32[32,1,128]{2,1,0:T(1,128)S(1)} %get-tuple-element.28), channel_id=1, replica_groups=mesh['nodes_0'=4,'nodes_1'=8,'nodes_2'=4,'feat'=2] {'nodes_0','nodes_2',..., dimensions={0} | all-to-all | bytes 32768 | tf_op jit(solution)/shard_map/all_to_all | solution.py:554
  202.1 0.6 slice_reduce_fusion
  (16 shorter events, 0.1 us)
Async XLA Ops:
  0.6 51.1 %copy-start.4 = (s32[2,4096]{1,0:T(2,128)S(1)}, s32[2,4096]{1,0:T(2,128)}, u32[]{:S(2)}) copy-start(s32[2,4096]{1,0:T(2,128)} %param.14) | copy-start | bytes 98308
  0.6 51.1 %copy-start.3 = (s32[2,4096]{1,0:T(2,128)S(1)}, s32[2,4096]{1,0:T(2,128)}, u32[]{:S(2)}) copy-start(s32[2,4096]{1,0:T(2,128)} %param.13) | copy-start | bytes 98308
  0.7 51.1 %copy-start.5 = (s32[2,4096]{1,0:T(2,128)S(1)}, s32[2,4096]{1,0:T(2,128)}, u32[]{:S(2)}) copy-start(s32[2,4096]{1,0:T(2,128)} %param.12) | copy-start | bytes 98308
  0.7 9.3 %collective-permute-start.1 = (bf16[512,256]{1,0:T(8,128)(2,1)}, bf16[512,256]{1,0:T(8,128)(2,1)S(1)}, u32[]{:S(2)}, u32[]{:S(2)}) collective-permute-start(bf16[512,256]{1,0:T(8,128)(2,1)} %w2_own.1), channel_id=1, source_target_pairs={{0,1},{1,0},{2,3},{3,2},{4,5},{5,4},{6,7},{7,6},{8,9},{9,8},{10,11... | collective-permute-start | bytes 786440 | tf_op jit(solution)/shard_map/ppermute | solution.py:406
  3.9 6.0 %collective-permute-start = (bf16[128,256]{1,0:T(8,128)(2,1)}, bf16[128,256]{1,0:T(8,128)(2,1)S(1)}, u32[]{:S(2)}, u32[]{:S(2)}) collective-permute-start(bf16[128,256]{1,0:T(8,128)(2,1)} %w1_own.1), channel_id=1, source_target_pairs={{0,1},{1,0},{2,3},{3,2},{4,5},{5,4},{6,7},{7,6},{8,9},{9,8},{10,11... | collective-permute-start | bytes 196616 | tf_op jit(solution)/shard_map/ppermute | solution.py:406
  4.1 5.9 %collective-permute-start.2 = (f32[1,256]{1,0:T(1,128)}, f32[1,256]{1,0:T(1,128)S(1)}, u32[]{:S(2)}, u32[]{:S(2)}) collective-permute-start(f32[1,256]{1,0:T(1,128)} %bitcast.23), channel_id=1, source_target_pairs={{0,1},{1,0},{2,3},{3,2},{4,5},{5,4},{6,7},{7,6},{8,9},{9,8},{10,11... | collective-permute-start | bytes 3080 | tf_op jit(solution)/shard_map/ppermute | solution.py:406
  50.8 2.7 %collective-permute-start.3 = (bf16[128,32,128]{2,1,0:T(8,128)(2,1)S(1)}, bf16[128,32,128]{2,1,0:T(8,128)(2,1)S(1)}, u32[]{:S(2)}, u32[]{:S(2)}) collective-permute-start(bf16[128,32,128]{2,1,0:T(8,128)(2,1)S(1)} %all_to_all.35), channel_id=1, source_target_pairs={{0,1},{1,0},{2,3},{3,2},{4,5},{5,4},{6,7},{7,6},{8,9},{9,8},{10,11... | collective-permute-start | bytes 3145736 | tf_op jit(solution)/shard_map/ppermute | solution.py:406
  63.6 62.0 %copy-start = (bf16[512,256]{1,0:T(8,128)(2,1)S(1)}, bf16[512,256]{1,0:T(8,128)(2,1)}, u32[]{:S(2)}) copy-start(bf16[512,256]{1,0:T(8,128)(2,1)} %w2_own.1) | copy-start | bytes 786436
  63.7 62.0 %copy-start.1 = (bf16[128,256]{1,0:T(8,128)(2,1)S(1)}, bf16[128,256]{1,0:T(8,128)(2,1)}, u32[]{:S(2)}) copy-start(bf16[128,256]{1,0:T(8,128)(2,1)} %w1_own.1) | copy-start | bytes 196612
  63.7 62.0 %copy-start.2 = (f32[256]{0:T(256)S(1)}, f32[256]{0:T(256)}, u32[]{:S(2)}) copy-start(f32[256]{0:T(256)} %param.16) | copy-start | bytes 3076
  136.7 27.3 %collective-permute-start.5 = (f32[512,512]{1,0:T(8,128)S(1)}, f32[512,512]{1,0:T(8,128)S(1)}, u32[]{:S(2)}, u32[]{:S(2)}) collective-permute-start(f32[512,512]{1,0:T(8,128)S(1)} %get-tuple-element.24.embedded), channel_id=1, source_target_pairs={{0,1},{1,0},{2,3},{3,2},{4,5},{5,4},{6,7},{7,6},{8,9},{9,8},{10,11... | collective-permute-start | bytes 3145736 | tf_op jit(solution)/shard_map/ppermute | solution.py:406
  160.5 3.5 %collective-permute-start.4 = (f32[8,8,128]{2,1,0:T(8,128)S(1)}, f32[8,8,128]{2,1,0:T(8,128)S(1)}, u32[]{:S(2)}, u32[]{:S(2)}) collective-permute-start(f32[8,8,128]{2,1,0:T(8,128)S(1)} %all_to_all.38.sums), channel_id=1, source_target_pairs={{0,1},{1,0},{2,3},{3,2},{4,5},{5,4},{6,7},{7,6},{8,9},{9,8},{10,11... | collective-permute-start | bytes 98312 | tf_op jit(solution)/shard_map/ppermute | solution.py:406
  177.5 11.5 %all-to-all-start.5 = ((s32[72,4,128]{2,1,0:T(4,128)}), s32[72,4,128]{2,1,0:T(4,128)S(1)}, u32[]{:S(2)}, u32[]{:S(2)}) async-start(s32[72,4,128]{2,1,0:T(4,128)} %bitcast.11), calls=%async_computation.5 | async-start | bytes 294912 | tf_op jit(solution)/shard_map/all_to_all | solution.py:540
